TPU v7x, 1024 devices: a whole 8x8x8 slice. The times are simulated.
1024 devices in a mesh: dp: 32 (over z_hi, x, core), tensor: 32 (over z_lo, y).
Axes of the slice: x: 8, y: 8, z: 8 (z_hi: 2, z_lo: 4; z = z_hi * 4 + z_lo), core: 2. Of those that a mesh axis runs over, the one named last changes fastest.
Arguments:
- grad_out: bfloat16 [8192, 4096], P(('dp', 'tensor')), may hold values from -2.5 to 2.5
- gate_pre: bfloat16 [8192, 14848], P('dp', 'tensor'), may hold values from -8 to 8
- up_pre: bfloat16 [8192, 14848], P('dp', 'tensor'), may hold values from -6 to 6
- down_weight: bfloat16 [4096, 14848], P(None, 'tensor'), may hold values from -1.5 to 1.5
Outputs:
- grad_weight: float32 [4096, 14848], P('dp', 'tensor')
- grad_gate: bfloat16 [8192, 14848], P('dp', 'tensor')
- grad_up: bfloat16 [8192, 14848], P('dp', 'tensor')
All inputs are finite; a program needn't handle non-finite values.
Results may differ from a plain program's by a relative error of at most 0.015.
Values may be sent and summed in bfloat16 or wider, within the bound.
No kernel may reach another device: no remote copies, remote signals or barrier semaphores. Data moves between devices by JAX's collectives and lax.ppermute only.
A program may use at most 32 MiB of HBM per device.

v0:
```python
import jax
import jax.numpy as jnp
from jax import lax
from jax.experimental import pallas as pl
from jax.experimental.pallas import tpu as pltpu
from jax.sharding import Mesh, PartitionSpec as P


AXES = ("zh", "x", "c", "zl", "y")
STEPS = (64.0, 32.0, 16.0, 8.0, 4.0, 2.0)


def exponents(most):
    k = jnp.zeros_like(most)
    for bit in STEPS:
        fits = most * (2.0**bit) <= 32768.0
        most = jnp.where(fits, most * (2.0**bit), most)
        k = jnp.where(fits, k + bit, k)
    return k


def power(k, sign):
    scale = jnp.ones_like(k)
    for bit in STEPS:
        has = k >= bit
        scale = jnp.where(has, scale * (2.0 ** (sign * bit)), scale)
        k = jnp.where(has, k - bit, k)
    return scale


def coded(rows):
    n = rows.shape[0]
    wide = rows.astype(jnp.float32)
    most = jnp.max(jnp.abs(wide).reshape(n * 8, 4, 128), axis=(0, 2))
    k = jnp.repeat(exponents(most), 128)[None, None, :]
    return (wide * power(k, 1)).astype(jnp.float16), jnp.broadcast_to(k, (1, 8, 512)).astype(jnp.float16)


def hidden_kernel(gate_ref, up_ref, out_ref, done, sem):
    gate = gate_ref[...].astype(jnp.float32)
    sig = jax.nn.sigmoid(gate)
    done[...] = ((gate * sig) * up_ref[...].astype(jnp.float32)).astype(jnp.bfloat16)
    copies = [pltpu.make_async_copy(done, out_ref.at[i], sem.at[i]) for i in range(8)]
    for copy in copies:
        copy.start()
    for copy in copies:
        copy.wait()


def hidden_copies(gate, up):
    h, t = gate.shape
    return pl.pallas_call(
        hidden_kernel,
        out_shape=jax.ShapeDtypeStruct((8, h, t), jnp.bfloat16),
        in_specs=[pl.BlockSpec(memory_space=pltpu.VMEM)] * 2,
        out_specs=pl.BlockSpec(memory_space=pl.ANY),
        scratch_shapes=[pltpu.VMEM((h, t), jnp.bfloat16), pltpu.SemaphoreType.DMA((8,))],
        cost_estimate=pl.CostEstimate(flops=2_000_000, bytes_accessed=10 * h * t * 2, transcendentals=h * t),
        name="hidden_copies",
    )(gate, up)


def split_kernel(g_ref, out_ref, held, sem):
    zh, c = lax.axis_index("zh"), lax.axis_index("c")
    for x in range(8):
        for i, z in enumerate((1 - zh, zh)):
            for j, core in enumerate((1 - c, c)):
                at = pl.multiple_of(2048 * z + 256 * x + 128 * core, 128)
                piece = g_ref[:, pl.ds(at, 128)]
                for zl in range(4):
                    held[4 * x + zl, :, 256 * i + 128 * j : 256 * i + 128 * (j + 1)] = piece
    copy = pltpu.make_async_copy(held, out_ref, sem)
    copy.start()
    copy.wait()


def split_rows(g):
    return pl.pallas_call(
        split_kernel,
        out_shape=jax.ShapeDtypeStruct((32, 8, 512), jnp.bfloat16),
        in_specs=[pl.BlockSpec(memory_space=pltpu.VMEM)],
        out_specs=pl.BlockSpec(memory_space=pl.ANY),
        scratch_shapes=[pltpu.VMEM((32, 8, 512), jnp.bfloat16), pltpu.SemaphoreType.DMA],
        name="split_rows",
    )(g)


def turned(x, axis, by):
    size = lax.axis_size(axis)
    return lax.ppermute(x, axis, [(i, (i + by) % size) for i in range(size)])


def sections(grad_out, gate_pre, up_pre, down_weight):
    gate_t, up_t = gate_pre.T, up_pre.T
    h, t = gate_t.shape
    zl = lax.axis_index("zl")

    pieces = split_rows(grad_out)
    mine = lax.all_to_all(pieces, ("x", "zl"), 0, 0)
    turns = [grad_out]
    for s in (1, 2, 3):
        turns.append(turned(grad_out, "zl", s))
    copies = hidden_copies(gate_t, up_t)
    hiddens = lax.all_to_all(copies, "x", 0, 0)

    near = jnp.stack(turns).reshape(4, 8, 8, 512).transpose(2, 0, 1, 3)
    near = jnp.take(near, (zl - jnp.arange(4)) % 4, axis=1)
    a, ka = coded(near.reshape(32, 8, 512))
    b, kb = coded(mine)
    message = jnp.concatenate([a, b, ka, kb], 0)
    got = lax.all_gather(message, "y", axis=1, tiled=True)

    def half(got, i):
        rows = got[:, :, 256 * i : 256 * (i + 1)]
        feats = (rows[32:64].astype(jnp.float32) * power(rows[65].astype(jnp.float32), -1)).astype(jnp.bfloat16).reshape(8, t, 256)
        part = lax.dot_general(hiddens, feats, (((0, 2), (0, 1)), ((), ())), preferred_element_type=jnp.float32)
        other = turned(part[:, :128].astype(jnp.bfloat16), "c", 1)
        return part[:, 128:] + other.astype(jnp.float32)

    first = half(got, 0).astype(jnp.bfloat16)
    away = turned(first, "zh", 1)
    got, first = lax.optimization_barrier((got, first))
    here = half(got, 1)

    whole = (got[:32].astype(jnp.float32) * power(got[64].astype(jnp.float32), -1)).astype(jnp.bfloat16).reshape(8, t, 512)
    weight = down_weight.T.reshape(h, 8, 512)
    grad_hidden = lax.dot_general(weight, whole, (((1, 2), (0, 2)), ((), ())), preferred_element_type=jnp.float32)
    gate = gate_t.astype(jnp.float32)
    upper = up_t.astype(jnp.float32)
    sig = jax.nn.sigmoid(gate)
    act = gate * sig
    grad_up = (grad_hidden * act).astype(jnp.bfloat16)
    grad_gate = (grad_hidden * upper * sig * (1.0 + gate * (1.0 - sig))).astype(jnp.bfloat16)
    return (here + away.astype(jnp.float32)).T, grad_gate.T, grad_up.T


def solution(mesh):
    dims = (2, 8, 2, 4, 8)
    fine = Mesh(mesh.devices.reshape(dims), AXES)
    dp, tensor = ("zh", "x", "c"), ("zl", "y")
    in_specs = (P(dp + tensor, None), P(dp, tensor), P(dp, tensor), P(None, tensor))
    out_specs = (P(dp, tensor), P(dp, tensor), P(dp, tensor))
    return jax.shard_map(sections, mesh=fine, in_specs=in_specs, out_specs=out_specs, check_vma=False)
```

profile of v0, /device:TPU:1, one launch (start us, length us, event | category | flops | bytes accessed | tf_op | source)
XLA Modules:
  0.0 117.0 jit_solution(10563981478213973126)
XLA Ops:
  0.6 0.0 copy-start.2
  0.6 11.3 %collective-permute-start.2 = (bf16[8,4096]{1,0:T(8,128)(2,1)}, bf16[8,4096]{1,0:T(8,128)(2,1)S(1)}, u32[]{:S(2)}, u32[]{:S(2)}) collective-permute-start(bf16[8,4096]{1,0:T(8,128)(2,1)} %g_ref.1), channel_id=1, source_target_pairs={{0,24},{8,0},{16,8},{24,16},{1,25},{9,1},{17,9},{25,17},{2,26},{10... | collective-permute-start | bytes 196616 | tf_op jit(solution)/shard_map/ppermute | solution.py:90
  11.9 1.9 %collective-permute-start.1 = (bf16[8,4096]{1,0:T(8,128)(2,1)}, bf16[8,4096]{1,0:T(8,128)(2,1)S(1)}, u32[]{:S(2)}, u32[]{:S(2)}) collective-permute-start(bf16[8,4096]{1,0:T(8,128)(2,1)} %g_ref.1), channel_id=1, source_target_pairs={{0,16},{8,24},{16,0},{24,8},{1,17},{9,25},{17,1},{25,9},{2,18},{10... | collective-permute-start | bytes 196616 | tf_op jit(solution)/shard_map/ppermute | solution.py:90
  13.9 2.2 %collective-permute-start = (bf16[8,4096]{1,0:T(8,128)(2,1)}, bf16[8,4096]{1,0:T(8,128)(2,1)S(1)}, u32[]{:S(2)}, u32[]{:S(2)}) collective-permute-start(bf16[8,4096]{1,0:T(8,128)(2,1)} %g_ref.1), channel_id=1, source_target_pairs={{0,8},{8,16},{16,24},{24,0},{1,9},{9,17},{17,25},{25,1},{2,10},{10... | collective-permute-start | bytes 196616 | tf_op jit(solution)/shard_map/ppermute | solution.py:90
  16.1 1.6 %split_rows.1 = bf16[32,8,512]{2,1,0:T(8,128)(2,1)} custom-call(bf16[8,4096]{1,0:T(8,128)(2,1)} %g_ref.1), custom_call_target="tpu_custom_call" | custom-call | tf_op jit(solution)/shard_map/split_rows/pallas_call | solution.py:78
  17.7 9.6 %all-to-all-start.1 = ((bf16[32,8,512]{2,1,0:T(8,128)(2,1)}), bf16[32,8,512]{2,1,0:T(8,128)(2,1)S(1)}, u32[]{:S(2)}, u32[]{:S(2)}) async-start(bf16[32,8,512]{2,1,0:T(8,128)(2,1)} %split_rows.1), calls=%async_computation.1 | async-start | bytes 524288 | tf_op jit(solution)/shard_map/all_to_all | solution.py:99
  27.3 0.1 broadcast_in_dim.41
  27.4 2.5 %hidden_copies.1 = bf16[8,464,256]{2,1,0:T(8,128)(2,1)} custom-call(bf16[464,256]{1,0:T(8,128)(2,1)} %bitcast.110, bf16[464,256]{1,0:T(8,128)(2,1)} %bitcast.111), custom_call_target="tpu_custom_call" | custom-call | flops 2000000 | bytes 2375680 | tf_op jit(solution)/shard_map/hidden_copies/pallas_call | solution.py:52
  29.9 0.0 collective-permute-done.2
  29.9 0.0 collective-permute-done.1
  29.9 0.0 collective-permute-done
  30.0 0.0 copy-done.2
  30.0 0.6 gather_fusion
  30.6 0.1 abs_reduce_fusion
  30.7 0.1 bitcast_reduce_fusion.1
  30.8 0.1 bitcast_convert_fusion.1
  30.9 0.1 multiply_select_fusion.20
  31.0 0.2 multiply_convert_fusion.3
  31.2 7.2 %all-to-all-done.1 = bf16[32,8,512]{2,1,0:T(8,128)(2,1)S(1)} async-done(((bf16[32,8,512]{2,1,0:T(8,128)(2,1)}), bf16[32,8,512]{2,1,0:T(8,128)(2,1)S(1)}, u32[]{:S(2)}, u32[]{:S(2)}) %all-to-all-start.1) | async-done | bytes 262176 | tf_op jit(solution)/shard_map/all_to_all | solution.py:99
  38.4 3.6 %all-to-all-start = ((bf16[8,464,256]{2,1,0:T(8,128)(2,1)}), bf16[8,464,256]{2,1,0:T(8,128)(2,1)S(1)}, u32[]{:S(2)}, u32[]{:S(2)}) async-start(bf16[8,464,256]{2,1,0:T(8,128)(2,1)} %hidden_copies.1), calls=%async_computation | async-start | bytes 3801088 | tf_op jit(solution)/shard_map/all_to_all | solution.py:104
  42.0 0.1 bitcast_reduce_fusion
  42.2 0.1 bitcast_convert_fusion
  42.2 0.1 multiply_select_fusion.15
  42.3 0.1 fusion.7
  42.4 0.2 pad_maximum_fusion
  42.6 44.8 %all-gather.1 = f16[66,64,512]{2,1,0:T(8,128)(2,1)S(1)} all-gather(f16[66,8,512]{2,1,0:T(8,128)(2,1)S(1)} %pad_maximum_fusion), channel_id=1, replica_groups=mesh['zh'=2,'x'=8,'c'=2,'zl'=4,'y'=8] {'y'}, dimensions={1}, use_global_device_ids=true | all-gather | bytes 4866048 | tf_op jit(solution)/shard_map/all_gather | solution.py:111
  87.4 0.0 copy-start
  87.4 0.1 fusion.23
  87.5 1.9 %copy-done = f16[66,64,512]{2,1,0:T(8,128)(2,1)} copy-done((f16[66,64,512]{2,1,0:T(8,128)(2,1)}, f16[66,64,512]{2,1,0:T(8,128)(2,1)S(1)}, u32[]{:S(2)}) %copy-start) | copy-done | bytes 4325400
  89.4 0.3 multiply_convert_fusion.2
  89.7 0.0 all-to-all-done
  89.7 0.0 copy-start.1
  89.7 0.7 convolution_bitcast_fusion.1
  90.4 6.5 %collective-permute-start.3 = (bf16[464,128]{1,0:T(8,128)(2,1)S(1)}, bf16[464,128]{1,0:T(8,128)(2,1)S(1)}, u32[]{:S(2)}, u32[]{:S(2)}) collective-permute-start(bf16[464,128]{1,0:T(8,128)(2,1)S(1)} %slice.73), channel_id=1, source_target_pairs={{0,32},{32,0},{1,33},{33,1},{2,34},{34,2},{3,35},{35,3},{4,36},{36... | collective-permute-start | bytes 356360 | tf_op jit(solution)/shard_map/ppermute | solution.py:90
  96.9 0.9 collective-permute-done.3
  97.9 11.6 %collective-permute-start.5 = (bf16[464,128]{1,0:T(8,128)(2,1)S(1)}, bf16[464,128]{1,0:T(8,128)(2,1)S(1)}, u32[]{:S(2)}, u32[]{:S(2)}) collective-permute-start(bf16[464,128]{1,0:T(8,128)(2,1)S(1)} %fusion.18), channel_id=1, source_target_pairs={{0,512},{512,0},{1,513},{513,1},{2,514},{514,2},{3,515},{515,3},{4... | collective-permute-start | bytes 356360 | tf_op jit(solution)/shard_map/ppermute | solution.py:90
  109.5 0.0 copy-done.1
  109.5 0.1 fusion.24
  109.5 0.1 fusion.20
  109.7 0.3 multiply_convert_fusion.1
  110.0 0.7 convolution_bitcast_fusion
  110.7 0.0 copy-start.3
  110.7 0.0 copy-start.4
  110.7 0.0 copy-start.5
  110.7 2.8 %collective-permute-start.4 = (bf16[464,128]{1,0:T(8,128)(2,1)S(1)}, bf16[464,128]{1,0:T(8,128)(2,1)S(1)}, u32[]{:S(2)}, u32[]{:S(2)}) collective-permute-start(bf16[464,128]{1,0:T(8,128)(2,1)S(1)} %slice.72), channel_id=1, source_target_pairs={{0,32},{32,0},{1,33},{33,1},{2,34},{34,2},{3,35},{35,3},{4,36},{36... | collective-permute-start | bytes 356360 | tf_op jit(solution)/shard_map/ppermute | solution.py:90
  113.5 0.6 multiply_convert_fusion
  114.1 0.0 copy-done.3
  114.1 0.0 copy-done.4
  114.1 0.0 copy-done.5
  114.2 2.1 %fusion.15 = (bf16[256,464]{0,1:T(8,128)(2,1)}, bf16[256,464]{0,1:T(8,128)(2,1)}) fusion(bf16[256,464]{0,1:T(8,128)(2,1)S(1)} %copy-done.3, bf16[256,464]{0,1:T(8,128)(2,1)S(1)} %copy-done.4, bf16[8,256,512]{2,1,0:T(8,128)(2,1)S(1)} %bitcast.106, bf16[58,8,8,512]{3,2,1,0:T(8,128)(2,1)S(1)} %bitcast.115), kind=kOutput, calls=%fused_computation.27 | convolution fusion | flops 974860288 | bytes 6848512 | tf_op jit(solution)/shard_map/dot_general | solution.py:127
  116.3 0.0 collective-permute-done.5
  116.3 0.0 collective-permute-done.4
  116.3 0.7 fusion.17
  (14 shorter events, 0.3 us)
Async XLA Ops:
  0.6 29.3 %copy-start.2 = (bf16[8,4096]{1,0:T(8,128)(2,1)S(1)}, bf16[8,4096]{1,0:T(8,128)(2,1)}, u32[]{:S(2)}) copy-start(bf16[8,4096]{1,0:T(8,128)(2,1)} %g_ref.1) | copy-start | bytes 196612
  0.6 29.3 %collective-permute-start.2 = (bf16[8,4096]{1,0:T(8,128)(2,1)}, bf16[8,4096]{1,0:T(8,128)(2,1)S(1)}, u32[]{:S(2)}, u32[]{:S(2)}) collective-permute-start(bf16[8,4096]{1,0:T(8,128)(2,1)} %g_ref.1), channel_id=1, source_target_pairs={{0,24},{8,0},{16,8},{24,16},{1,25},{9,1},{17,9},{25,17},{2,26},{10... | collective-permute-start | bytes 196616 | tf_op jit(solution)/shard_map/ppermute | solution.py:90
  11.9 18.0 %collective-permute-start.1 = (bf16[8,4096]{1,0:T(8,128)(2,1)}, bf16[8,4096]{1,0:T(8,128)(2,1)S(1)}, u32[]{:S(2)}, u32[]{:S(2)}) collective-permute-start(bf16[8,4096]{1,0:T(8,128)(2,1)} %g_ref.1), channel_id=1, source_target_pairs={{0,16},{8,24},{16,0},{24,8},{1,17},{9,25},{17,1},{25,9},{2,18},{10... | collective-permute-start | bytes 196616 | tf_op jit(solution)/shard_map/ppermute | solution.py:90
  13.9 16.1 %collective-permute-start = (bf16[8,4096]{1,0:T(8,128)(2,1)}, bf16[8,4096]{1,0:T(8,128)(2,1)S(1)}, u32[]{:S(2)}, u32[]{:S(2)}) collective-permute-start(bf16[8,4096]{1,0:T(8,128)(2,1)} %g_ref.1), channel_id=1, source_target_pairs={{0,8},{8,16},{16,24},{24,0},{1,9},{9,17},{17,25},{25,1},{2,10},{10... | collective-permute-start | bytes 196616 | tf_op jit(solution)/shard_map/ppermute | solution.py:90
  17.7 20.7 %all-to-all-start.1 = ((bf16[32,8,512]{2,1,0:T(8,128)(2,1)}), bf16[32,8,512]{2,1,0:T(8,128)(2,1)S(1)}, u32[]{:S(2)}, u32[]{:S(2)}) async-start(bf16[32,8,512]{2,1,0:T(8,128)(2,1)} %split_rows.1), calls=%async_computation.1 | async-start | bytes 524288 | tf_op jit(solution)/shard_map/all_to_all | solution.py:99
  38.4 51.3 %all-to-all-start = ((bf16[8,464,256]{2,1,0:T(8,128)(2,1)}), bf16[8,464,256]{2,1,0:T(8,128)(2,1)S(1)}, u32[]{:S(2)}, u32[]{:S(2)}) async-start(bf16[8,464,256]{2,1,0:T(8,128)(2,1)} %hidden_copies.1), calls=%async_computation | async-start | bytes 3801088 | tf_op jit(solution)/shard_map/all_to_all | solution.py:104
  87.4 2.0 %copy-start = (f16[66,64,512]{2,1,0:T(8,128)(2,1)}, f16[66,64,512]{2,1,0:T(8,128)(2,1)S(1)}, u32[]{:S(2)}) copy-start(f16[66,64,512]{2,1,0:T(8,128)(2,1)S(1)} %all-gather.1) | copy-start | bytes 12976132
  89.7 19.8 %copy-start.1 = (f16[66,64,512]{2,1,0:T(8,128)(2,1)S(1)}, f16[66,64,512]{2,1,0:T(8,128)(2,1)}, u32[]{:S(2)}) copy-start(f16[66,64,512]{2,1,0:T(8,128)(2,1)} %copy-done) | copy-start | bytes 12976132
  90.4 7.4 %collective-permute-start.3 = (bf16[464,128]{1,0:T(8,128)(2,1)S(1)}, bf16[464,128]{1,0:T(8,128)(2,1)S(1)}, u32[]{:S(2)}, u32[]{:S(2)}) collective-permute-start(bf16[464,128]{1,0:T(8,128)(2,1)S(1)} %slice.73), channel_id=1, source_target_pairs={{0,32},{32,0},{1,33},{33,1},{2,34},{34,2},{3,35},{35,3},{4,36},{36... | collective-permute-start | bytes 356360 | tf_op jit(solution)/shard_map/ppermute | solution.py:90
  97.9 18.4 %collective-permute-start.5 = (bf16[464,128]{1,0:T(8,128)(2,1)S(1)}, bf16[464,128]{1,0:T(8,128)(2,1)S(1)}, u32[]{:S(2)}, u32[]{:S(2)}) collective-permute-start(bf16[464,128]{1,0:T(8,128)(2,1)S(1)} %fusion.18), channel_id=1, source_target_pairs={{0,512},{512,0},{1,513},{513,1},{2,514},{514,2},{3,515},{515,3},{4... | collective-permute-start | bytes 356360 | tf_op jit(solution)/shard_map/ppermute | solution.py:90
  110.7 3.5 %copy-start.3 = (bf16[256,464]{0,1:T(8,128)(2,1)S(1)}, bf16[256,464]{0,1:T(8,128)(2,1)}, u32[]{:S(2)}) copy-start(bf16[256,464]{0,1:T(8,128)(2,1)} %param.5) | copy-start | bytes 712708
  110.7 3.5 %copy-start.4 = (bf16[256,464]{0,1:T(8,128)(2,1)S(1)}, bf16[256,464]{0,1:T(8,128)(2,1)}, u32[]{:S(2)}) copy-start(bf16[256,464]{0,1:T(8,128)(2,1)} %param.6) | copy-start | bytes 712708
  110.7 3.5 %copy-start.5 = (bf16[4096,464]{0,1:T(8,128)(2,1)S(1)}, bf16[4096,464]{0,1:T(8,128)(2,1)}, u32[]{:S(2)}) copy-start(bf16[4096,464]{0,1:T(8,128)(2,1)} %param.7) | copy-start | bytes 11403268
  110.7 5.6 %collective-permute-start.4 = (bf16[464,128]{1,0:T(8,128)(2,1)S(1)}, bf16[464,128]{1,0:T(8,128)(2,1)S(1)}, u32[]{:S(2)}, u32[]{:S(2)}) collective-permute-start(bf16[464,128]{1,0:T(8,128)(2,1)S(1)} %slice.72), channel_id=1, source_target_pairs={{0,32},{32,0},{1,33},{33,1},{2,34},{34,2},{3,35},{35,3},{4,36},{36... | collective-permute-start | bytes 356360 | tf_op jit(solution)/shard_map/ppermute | solution.py:90
where the time goes:
time: 117 us
  starting transfers between devices  49.5 us (42%)
  blocking collectives  44.8 us (38%)
  waiting for transfers between devices  8.17 us (7%)
  Pallas kernels  4.09 us (3%)
  matrix products  3.41 us (3%)
  other arithmetic  3.39 us (3%)
  local copies, waits for them, and re-layouts  2.67 us (2%)
    all_gather x1, blocking collectives, sections(): got = lax.all_gather(message, 'y', axis=1, tiled=True)  44.8 us
    ppermute x6, starting transfers between devices, turned(): return lax.ppermute(x, axis, [(i, (i + by) % size) for i in range(size)])  36.3 us
    all_to_all x1, starting transfers between devices, sections(): mine = lax.all_to_all(pieces, ('x', 'zl'), 0, 0)  9.58 us
    all_to_all x1, waiting for transfers between devices, sections(): mine = lax.all_to_all(pieces, ('x', 'zl'), 0, 0)  7.2 us
    all_to_all x1, starting transfers between devices, sections(): hiddens = lax.all_to_all(copies, 'x', 0, 0)  3.6 us
    pallas_call x1, Pallas kernels, hidden_copies(): pl.pallas_call(hidden_kernel, out_shape=jax.ShapeDtypeStruct((8, h, t), j...  2.5 us
  transfers between devices with their start and end apart: 8, of which 2 were waited for; matrix products, arithmetic and copies ran while one was open for 5% of the time, Pallas kernels for 3%

commit v1 on v0

v1 whole, which is shorter than its diff:
```python
import jax
import jax.numpy as jnp
from jax import lax
from jax.experimental import pallas as pl
from jax.experimental.pallas import tpu as pltpu
from jax.sharding import Mesh, PartitionSpec as P


AXES = ("zh", "x", "c", "zl", "y")
STEPS = (64.0, 32.0, 16.0, 8.0, 4.0, 2.0)


def exponents(most):
    k = jnp.zeros_like(most)
    for bit in STEPS:
        fits = most * (2.0**bit) <= 32768.0
        most = jnp.where(fits, most * (2.0**bit), most)
        k = jnp.where(fits, k + bit, k)
    return k


def power(k, sign):
    scale = jnp.ones_like(k)
    for bit in STEPS:
        has = k >= bit
        scale = jnp.where(has, scale * (2.0 ** (sign * bit)), scale)
        k = jnp.where(has, k - bit, k)
    return scale


def scales_of(most):
    k = exponents(jnp.max(jnp.max(most, axis=1, keepdims=True), axis=0, keepdims=True))
    return power(k, 1), k


def own_kernel(a_ref, b_ref, c_ref, d_ref, out_ref, k_ref):
    zl = lax.axis_index("zl")
    turns = (a_ref, b_ref, c_ref, d_ref)
    for b in range(4):
        most = None
        for ref in turns:
            for q in range(8):
                value = jnp.abs(ref[:, 512 * q + 128 * b : 512 * q + 128 * (b + 1)].astype(jnp.float32))
                most = value if most is None else jnp.maximum(most, value)
        scale, k = scales_of(most)
        k_ref[:, 128 * b : 128 * (b + 1)] = jnp.broadcast_to(k, (8, 128)).astype(jnp.bfloat16)
        for s, ref in enumerate(turns):
            place = lax.rem(zl + 4 - s, 4)
            for q in range(8):
                value = ref[:, 512 * q + 128 * b : 512 * q + 128 * (b + 1)].astype(jnp.float32) * scale
                out_ref[4 * q + place, :, 128 * b : 128 * (b + 1)] = value.astype(jnp.bfloat16)


def rows_kernel(rows_ref, out_ref, k_ref):
    for b in range(4):
        cols = slice(128 * b, 128 * (b + 1))
        most = jnp.max(jnp.abs(rows_ref[:, :, cols].astype(jnp.float32)), axis=0)
        scale, k = scales_of(most)
        k_ref[:, cols] = jnp.broadcast_to(k, (8, 128)).astype(jnp.bfloat16)
        out_ref[:, :, cols] = (rows_ref[:, :, cols].astype(jnp.float32) * scale[None]).astype(jnp.bfloat16)


def scaled(kernel, *rows):
    return pl.pallas_call(
        kernel,
        out_shape=(jax.ShapeDtypeStruct((32, 8, 512), jnp.bfloat16), jax.ShapeDtypeStruct((8, 512), jnp.bfloat16)),
        in_specs=[pl.BlockSpec(memory_space=pltpu.VMEM)] * len(rows),
        out_specs=(pl.BlockSpec(memory_space=pltpu.VMEM),) * 2,
        cost_estimate=pl.CostEstimate(flops=1_000_000, bytes_accessed=600_000, transcendentals=0),
        compiler_params=pltpu.CompilerParams(vmem_limit_bytes=4 << 20),
    )(*rows)


def hidden_kernel(gate_ref, up_ref, out_ref, done, sem):
    h = gate_ref.shape[0]
    copies = []
    for n in range(4):
        part = h // 4 // 16 * 16
        at = pl.ds(n * part, part if n < 3 else h - 3 * part)
        gate = gate_ref[at, :].astype(jnp.float32)
        sig = jax.nn.sigmoid(gate)
        done[at, :] = ((gate * sig) * up_ref[at, :].astype(jnp.float32)).astype(jnp.bfloat16)
        for i in range(8):
            copies.append(pltpu.make_async_copy(done.at[at, :], out_ref.at[i, at, :], sem.at[n, i]))
            copies[-1].start()
    for copy in copies:
        copy.wait()


def hidden_copies(gate, up):
    h, t = gate.shape
    return pl.pallas_call(
        hidden_kernel,
        out_shape=jax.ShapeDtypeStruct((8, h, t), jnp.bfloat16),
        in_specs=[pl.BlockSpec(memory_space=pltpu.VMEM)] * 2,
        out_specs=pl.BlockSpec(memory_space=pl.ANY),
        scratch_shapes=[pltpu.VMEM((h, t), jnp.bfloat16), pltpu.SemaphoreType.DMA((4, 8))],
        cost_estimate=pl.CostEstimate(flops=2_000_000, bytes_accessed=10 * h * t * 2, transcendentals=h * t),
        compiler_params=pltpu.CompilerParams(vmem_limit_bytes=2 << 20),
        name="hidden_copies",
    )(gate, up)


def split_kernel(g_ref, out_ref, held, sem):
    zh, c = lax.axis_index("zh"), lax.axis_index("c")
    for x in range(8):
        for i, core in enumerate((1 - c, c)):
            for j, z in enumerate((1 - zh, zh)):
                at = pl.multiple_of(2048 * z + 256 * x + 128 * core, 128)
                piece = g_ref[:, pl.ds(at, 128)]
                for zl in range(4):
                    held[4 * x + zl, :, 256 * i + 128 * j : 256 * i + 128 * (j + 1)] = piece
    copy = pltpu.make_async_copy(held, out_ref, sem)
    copy.start()
    copy.wait()


def split_rows(g):
    return pl.pallas_call(
        split_kernel,
        out_shape=jax.ShapeDtypeStruct((32, 8, 512), jnp.bfloat16),
        in_specs=[pl.BlockSpec(memory_space=pltpu.VMEM)],
        out_specs=pl.BlockSpec(memory_space=pl.ANY),
        scratch_shapes=[pltpu.VMEM((32, 8, 512), jnp.bfloat16), pltpu.SemaphoreType.DMA],
        compiler_params=pltpu.CompilerParams(vmem_limit_bytes=2 << 20),
        name="split_rows",
    )(g)


def turned(x, axis, by):
    size = lax.axis_size(axis)
    return lax.ppermute(x, axis, [(i, (i + by) % size) for i in range(size)])


def sections(grad_out, gate_pre, up_pre, down_weight):
    gate_t, up_t = gate_pre.T, up_pre.T
    h, t = gate_t.shape

    pieces = split_rows(grad_out)
    mine = lax.all_to_all(pieces, ("x", "zl"), 0, 0)
    turns = [grad_out]
    for s in (1, 2, 3):
        turns.append(turned(grad_out, "zl", s))
    copies = hidden_copies(gate_t, up_t)
    hiddens = lax.all_to_all(copies, "x", 0, 0)

    own, own_k = scaled(own_kernel, *turns)
    feats, feats_k = scaled(rows_kernel, mine)
    message = jnp.concatenate([own, feats, own_k[None], feats_k[None]], 0).astype(jnp.float16)
    got = lax.all_gather(message, "y", axis=1, tiled=True)

    scale = power(got[65].astype(jnp.float32), -1)
    feats = (got[32:64].astype(jnp.float32) * scale).astype(jnp.bfloat16).reshape(8, t, 512)
    part = lax.dot_general(hiddens, feats, (((0, 2), (0, 1)), ((), ())), preferred_element_type=jnp.float32)
    swap = lax.all_gather(part[:, :256].astype(jnp.bfloat16), "c", axis=0)
    part = part[:, 256:] + lax.dynamic_index_in_dim(swap, 1 - lax.axis_index("c"), 0, keepdims=False).astype(jnp.float32)
    away = turned(part[:, :128].astype(jnp.bfloat16), "zh", 1)
    here = part[:, 128:]

    scale = power(got[64].astype(jnp.float32), -1)
    whole = (got[:32].astype(jnp.float32) * scale).astype(jnp.bfloat16).reshape(8, t, 512)
    weight = down_weight.T.reshape(h, 8, 512)
    grad_hidden = lax.dot_general(weight, whole, (((1, 2), (0, 2)), ((), ())), preferred_element_type=jnp.float32)
    gate = gate_t.astype(jnp.float32)
    upper = up_t.astype(jnp.float32)
    sig = jax.nn.sigmoid(gate)
    act = gate * sig
    grad_up = (grad_hidden * act).astype(jnp.bfloat16)
    grad_gate = (grad_hidden * upper * sig * (1.0 + gate * (1.0 - sig))).astype(jnp.bfloat16)
    return (here + away.astype(jnp.float32)).T, grad_gate.T, grad_up.T


def solution(mesh):
    dims = (2, 8, 2, 4, 8)
    fine = Mesh(mesh.devices.reshape(dims), AXES)
    dp, tensor = ("zh", "x", "c"), ("zl", "y")
    in_specs = (P(dp + tensor, None), P(dp, tensor), P(dp, tensor), P(None, tensor))
    out_specs = (P(dp, tensor), P(dp, tensor), P(dp, tensor))
    return jax.shard_map(sections, mesh=fine, in_specs=in_specs, out_specs=out_specs, check_vma=False)
```

time: 117 us -> 121 us (1.034)
  the two profiles are of different devices: /device:TPU:1 before, /device:TPU:130 now
where the time goes in v1:
time: 121 us; the launch traced here: 120 us
  blocking collectives  47.5 us (39%)
  starting transfers between devices  42.1 us (35%)
  waiting for transfers between devices  15.3 us (13%)
  matrix products  5.55 us (5%)
  other arithmetic  3.75 us (3%)
  local copies, waits for them, and re-layouts  2.79 us (2%)
  Pallas kernels  2.71 us (2%)
    all_gather x1, blocking collectives, sections(): got = lax.all_gather(message, 'y', axis=1, tiled=True)  45.2 us
    ppermute x4, starting transfers between devices, turned(): return lax.ppermute(x, axis, [(i, (i + by) % size) for i in range(size)])  22.7 us
    all_to_all x1, starting transfers between devices, sections(): mine = lax.all_to_all(pieces, ('x', 'zl'), 0, 0)  14.9 us
    ppermute x4, waiting for transfers between devices, turned(): return lax.ppermute(x, axis, [(i, (i + by) % size) for i in range(size)])  8.3 us
    all_to_all x1, waiting for transfers between devices, sections(): mine = lax.all_to_all(pieces, ('x', 'zl'), 0, 0)  6.95 us
    all_to_all x1, starting transfers between devices, sections(): hiddens = lax.all_to_all(copies, 'x', 0, 0)  4.55 us
    dot_general x1, matrix products, sections(): lax.dot_general(hiddens, feats, (((0, 2), (0, 1)), ((), ())), preferred_e...  3.45 us
    unnamed x14, local copies, waits for them, and re-layouts  2.74 us
  transfers between devices with their start and end apart: 6, of which 4 were waited for; matrix products, arithmetic and copies ran while one was open for 4% of the time, Pallas kernels for 2%

profile of v1, /device:TPU:130, one launch (start us, length us, event | category | flops | bytes accessed | tf_op | source)
XLA Modules:
  0.0 120.5 jit_solution(7887204369416534409)
XLA Ops:
  0.6 0.0 copy-start
  0.6 0.8 copy-done
  1.5 0.7 split_rows.1
  2.2 14.9 %all-to-all-start.1 = ((bf16[32,8,512]{2,1,0:T(8,128)(2,1)}), bf16[32,8,512]{2,1,0:T(8,128)(2,1)S(1)}, u32[]{:S(2)}, u32[]{:S(2)}) async-start(bf16[32,8,512]{2,1,0:T(8,128)(2,1)} %split_rows.1), calls=%async_computation.1 | async-start | bytes 524288 | tf_op jit(solution)/shard_map/all_to_all | solution.py:140
  17.1 0.0 copy-start.2
  17.1 0.9 copy-done.2
  18.1 0.0 copy-start.4
  18.1 0.9 copy-done.4
  19.0 1.6 %hidden_copies.1 = bf16[8,464,256]{2,1,0:T(8,128)(2,1)} custom-call(bf16[464,256]{1,0:T(8,128)(2,1)S(1)} %bitcast.32, bf16[464,256]{1,0:T(8,128)(2,1)S(1)} %bitcast.33), custom_call_target="tpu_custom_call" | custom-call | flops 2000000 | bytes 2375680 | tf_op jit(solution)/shard_map/hidden_copies/pallas_call | solution.py:92
  20.6 0.0 copy-start.1
  20.6 6.9 %all-to-all-done.1.rows_ref = bf16[32,8,512]{2,1,0:T(8,128)(2,1)S(1)} async-done(((bf16[32,8,512]{2,1,0:T(8,128)(2,1)}), bf16[32,8,512]{2,1,0:T(8,128)(2,1)S(1)}, u32[]{:S(2)}, u32[]{:S(2)}) %all-to-all-start.1) | async-done | bytes 262176 | tf_op jit(solution)/shard_map/all_to_all | solution.py:140
  27.6 4.6 %all-to-all-start = ((bf16[8,464,256]{2,1,0:T(8,128)(2,1)}), bf16[8,464,256]{2,1,0:T(8,128)(2,1)}, u32[]{:S(2)}, u32[]{:S(2)}) async-start(bf16[8,464,256]{2,1,0:T(8,128)(2,1)} %hidden_copies.1), calls=%async_computation | async-start | bytes 3801088 | tf_op jit(solution)/shard_map/all_to_all | solution.py:145
  32.1 0.0 copy-done.1
  32.1 3.3 %collective-permute-start = (bf16[8,4096]{1,0:T(8,128)(2,1)S(1)}, bf16[8,4096]{1,0:T(8,128)(2,1)S(1)}, u32[]{:S(2)}, u32[]{:S(2)}) collective-permute-start(bf16[8,4096]{1,0:T(8,128)(2,1)S(1)} %copy-done.1), channel_id=1, source_target_pairs={{0,8},{8,16},{16,24},{24,0},{1,9},{9,17},{17,25},{25,1},{2,10},{10... | collective-permute-start | bytes 196616 | tf_op jit(solution)/shard_map/ppermute | solution.py:132
  35.4 5.6 %collective-permute-start.1 = (bf16[8,4096]{1,0:T(8,128)(2,1)S(1)}, bf16[8,4096]{1,0:T(8,128)(2,1)S(1)}, u32[]{:S(2)}, u32[]{:S(2)}) collective-permute-start(bf16[8,4096]{1,0:T(8,128)(2,1)S(1)} %copy-done.1), channel_id=1, source_target_pairs={{0,16},{8,24},{16,0},{24,8},{1,17},{9,25},{17,1},{25,9},{2,18},{10... | collective-permute-start | bytes 196616 | tf_op jit(solution)/shard_map/ppermute | solution.py:132
  41.0 1.9 %collective-permute-start.2 = (bf16[8,4096]{1,0:T(8,128)(2,1)S(1)}, bf16[8,4096]{1,0:T(8,128)(2,1)S(1)}, u32[]{:S(2)}, u32[]{:S(2)}) collective-permute-start(bf16[8,4096]{1,0:T(8,128)(2,1)S(1)} %copy-done.1), channel_id=1, source_target_pairs={{0,24},{8,0},{16,8},{24,16},{1,25},{9,1},{17,9},{25,17},{2,26},{10... | collective-permute-start | bytes 196616 | tf_op jit(solution)/shard_map/ppermute | solution.py:132
  42.9 0.0 collective-permute-done.b_ref
  42.9 0.4 collective-permute-done.1.c_ref
  43.3 3.8 %collective-permute-done.2.d_ref = bf16[8,4096]{1,0:T(8,128)(2,1)S(1)} collective-permute-done((bf16[8,4096]{1,0:T(8,128)(2,1)S(1)}, bf16[8,4096]{1,0:T(8,128)(2,1)S(1)}, u32[]{:S(2)}, u32[]{:S(2)}) %collective-permute-start.2) | collective-permute-done | bytes 65568 | tf_op jit(solution)/shard_map/ppermute | solution.py:132
  47.2 0.2 shard_map.67
  47.4 0.2 shard_map.68
  47.6 0.2 maximum_convert_fusion
  47.7 45.2 %all-gather.2 = f16[66,64,512]{2,1,0:T(8,128)(2,1)S(1)} all-gather(f16[66,8,512]{2,1,0:T(8,128)(2,1)S(1)} %maximum_convert_fusion), channel_id=1, replica_groups=mesh['zh'=2,'x'=8,'c'=2,'zl'=4,'y'=8] {'y'}, dimensions={1}, use_global_device_ids=true | all-gather | bytes 4866048 | tf_op jit(solution)/shard_map/all_gather | solution.py:150
  93.0 0.2 fusion.18
  93.2 2.6 %multiply_convert_fusion = (bf16[32,64,512]{2,1,0:T(8,128)(2,1)S(1)}, bf16[32,64,512]{2,1,0:T(8,128)(2,1)}) fusion(f16[66,64,512]{2,1,0:T(8,128)(2,1)S(1)} %all-gather.2, f32[64,512]{1,0:T(8,128)S(1)} %get-tuple-element.13, f32[64,512]{1,0:T(8,128)S(1)} %get-tuple-element.14), kind=kLoop, calls=%fused_computation | loop fusion | flops 6291456 | bytes 8650752 | tf_op jit(solution)/shard_map/convert_element_type | solution.py:161
  95.8 0.0 all-to-all-done
  95.8 0.0 copy-start.6
  95.8 3.5 %convolution_bitcast_fusion = f32[464,512]{1,0:T(8,128)S(1)} fusion(bf16[8,464,256]{2,1,0:T(8,128)(2,1)} %all-to-all-done, bf16[8,256,512]{2,1,0:T(8,128)(2,1)} %bitcast.37), kind=kOutput, calls=%fused_computation.5 | convolution fusion | flops 973078528 | bytes 4947968 | tf_op jit(solution)/shard_map/dot_general | solution.py:154
  99.2 0.0 copy-start.3
  99.3 0.0 copy-start.5
  99.3 2.3 %all-gather = bf16[928,256]{1,0:T(8,128)(2,1)S(1)} all-gather(bf16[464,256]{1,0:T(8,128)(2,1)S(1)} %slice.52), channel_id=2, replica_groups=mesh['zh'=2,'x'=8,'c'=2,'zl'=4,'y'=8] {'c'}, dimensions={0}, use_global_device_ids=true | all-gather | bytes 712704 | tf_op jit(solution)/shard_map/all_gather | solution.py:155
  101.6 0.1 slice_add_fusion
  101.7 11.9 %collective-permute-start.3 = (bf16[464,128]{1,0:T(8,128)(2,1)S(1)}, bf16[464,128]{1,0:T(8,128)(2,1)S(1)}, u32[]{:S(2)}, u32[]{:S(2)}) collective-permute-start(bf16[464,128]{1,0:T(8,128)(2,1)S(1)} %slice.53), channel_id=1, source_target_pairs={{0,512},{512,0},{1,513},{513,1},{2,514},{514,2},{3,515},{515,3},{4... | collective-permute-start | bytes 356360 | tf_op jit(solution)/shard_map/ppermute | solution.py:132
  113.6 0.0 copy-done.6
  113.6 0.0 copy-done.3
  113.6 0.0 copy-done.5
  113.6 2.1 %fusion.13 = (bf16[256,464]{0,1:T(8,128)(2,1)}, bf16[256,464]{0,1:T(8,128)(2,1)}) fusion(bf16[256,464]{0,1:T(8,128)(2,1)S(1)} %copy-done.3, bf16[256,464]{0,1:T(8,128)(2,1)S(1)} %copy-done.5, bf16[8,256,512]{2,1,0:T(8,128)(2,1)S(1)} %bitcast.36, bf16[58,8,8,512]{3,2,1,0:T(8,128)(2,1)S(1)} %bitcast.39), kind=kOutput, calls=%fused_computation.18 | convolution fusion | flops 974860288 | bytes 6848512 | tf_op jit(solution)/shard_map/dot_general | solution.py:163
  115.7 4.1 %collective-permute-done.3 = bf16[464,128]{1,0:T(8,128)(2,1)S(1)} collective-permute-done((bf16[464,128]{1,0:T(8,128)(2,1)S(1)}, bf16[464,128]{1,0:T(8,128)(2,1)S(1)}, u32[]{:S(2)}, u32[]{:S(2)}) %collective-permute-start.3) | collective-permute-done | bytes 118816 | tf_op jit(solution)/shard_map/ppermute | solution.py:132
  119.8 0.7 fusion.14
  (2 shorter events, 0.1 us)
Async XLA Ops:
  0.6 0.8 copy-start
  2.2 25.3 %all-to-all-start.1 = ((bf16[32,8,512]{2,1,0:T(8,128)(2,1)}), bf16[32,8,512]{2,1,0:T(8,128)(2,1)S(1)}, u32[]{:S(2)}, u32[]{:S(2)}) async-start(bf16[32,8,512]{2,1,0:T(8,128)(2,1)} %split_rows.1), calls=%async_computation.1 | async-start | bytes 524288 | tf_op jit(solution)/shard_map/all_to_all | solution.py:140
  17.1 0.9 copy-start.2
  18.1 0.9 copy-start.4
  20.6 11.5 %copy-start.1 = (bf16[8,4096]{1,0:T(8,128)(2,1)S(1)}, bf16[8,4096]{1,0:T(8,128)(2,1)}, u32[]{:S(2)}) copy-start(bf16[8,4096]{1,0:T(8,128)(2,1)} %g_ref.1) | copy-start | bytes 196612
  27.6 68.2 %all-to-all-start = ((bf16[8,464,256]{2,1,0:T(8,128)(2,1)}), bf16[8,464,256]{2,1,0:T(8,128)(2,1)}, u32[]{:S(2)}, u32[]{:S(2)}) async-start(bf16[8,464,256]{2,1,0:T(8,128)(2,1)} %hidden_copies.1), calls=%async_computation | async-start | bytes 3801088 | tf_op jit(solution)/shard_map/all_to_all | solution.py:145
  32.1 10.8 %collective-permute-start = (bf16[8,4096]{1,0:T(8,128)(2,1)S(1)}, bf16[8,4096]{1,0:T(8,128)(2,1)S(1)}, u32[]{:S(2)}, u32[]{:S(2)}) collective-permute-start(bf16[8,4096]{1,0:T(8,128)(2,1)S(1)} %copy-done.1), channel_id=1, source_target_pairs={{0,8},{8,16},{16,24},{24,0},{1,9},{9,17},{17,25},{25,1},{2,10},{10... | collective-permute-start | bytes 196616 | tf_op jit(solution)/shard_map/ppermute | solution.py:132
  35.4 8.0 %collective-permute-start.1 = (bf16[8,4096]{1,0:T(8,128)(2,1)S(1)}, bf16[8,4096]{1,0:T(8,128)(2,1)S(1)}, u32[]{:S(2)}, u32[]{:S(2)}) collective-permute-start(bf16[8,4096]{1,0:T(8,128)(2,1)S(1)} %copy-done.1), channel_id=1, source_target_pairs={{0,16},{8,24},{16,0},{24,8},{1,17},{9,25},{17,1},{25,9},{2,18},{10... | collective-permute-start | bytes 196616 | tf_op jit(solution)/shard_map/ppermute | solution.py:132
  41.0 6.2 %collective-permute-start.2 = (bf16[8,4096]{1,0:T(8,128)(2,1)S(1)}, bf16[8,4096]{1,0:T(8,128)(2,1)S(1)}, u32[]{:S(2)}, u32[]{:S(2)}) collective-permute-start(bf16[8,4096]{1,0:T(8,128)(2,1)S(1)} %copy-done.1), channel_id=1, source_target_pairs={{0,24},{8,0},{16,8},{24,16},{1,25},{9,1},{17,9},{25,17},{2,26},{10... | collective-permute-start | bytes 196616 | tf_op jit(solution)/shard_map/ppermute | solution.py:132
  95.8 17.8 %copy-start.6 = (bf16[4096,464]{0,1:T(8,128)(2,1)S(1)}, bf16[4096,464]{0,1:T(8,128)(2,1)}, u32[]{:S(2)}) copy-start(bf16[4096,464]{0,1:T(8,128)(2,1)} %param.7) | copy-start | bytes 11403268
  99.2 14.3 %copy-start.3 = (bf16[256,464]{0,1:T(8,128)(2,1)S(1)}, bf16[256,464]{0,1:T(8,128)(2,1)}, u32[]{:S(2)}) copy-start(bf16[256,464]{0,1:T(8,128)(2,1)} %param.5) | copy-start | bytes 712708
  99.3 14.3 %copy-start.5 = (bf16[256,464]{0,1:T(8,128)(2,1)S(1)}, bf16[256,464]{0,1:T(8,128)(2,1)}, u32[]{:S(2)}) copy-start(bf16[256,464]{0,1:T(8,128)(2,1)} %param.6) | copy-start | bytes 712708
  101.7 18.1 %collective-permute-start.3 = (bf16[464,128]{1,0:T(8,128)(2,1)S(1)}, bf16[464,128]{1,0:T(8,128)(2,1)S(1)}, u32[]{:S(2)}, u32[]{:S(2)}) collective-permute-start(bf16[464,128]{1,0:T(8,128)(2,1)S(1)} %slice.53), channel_id=1, source_target_pairs={{0,512},{512,0},{1,513},{513,1},{2,514},{514,2},{3,515},{515,3},{4... | collective-permute-start | bytes 356360 | tf_op jit(solution)/shard_map/ppermute | solution.py:132

commit v2 on v1

--- a/solution.py
+++ b/solution.py
@@ -71,17 +71,24 @@
     )(*rows)
 
 
-def hidden_kernel(gate_ref, up_ref, out_ref, done, sem):
+def hidden_kernel(gate_ref, up_ref, out_ref, gate_in, up_in, done, in_sem, out_sem):
     h = gate_ref.shape[0]
+    part = h // 4 // 16 * 16
+    bands = [pl.ds(n * part, part if n < 3 else h - 3 * part) for n in range(4)]
+    loads = []
+    for n, band in enumerate(bands):
+        for i, (ref, into) in enumerate(((gate_ref, gate_in), (up_ref, up_in))):
+            loads.append(pltpu.make_async_copy(ref.at[band, :], into.at[band, :], in_sem.at[n, i]))
+            loads[-1].start()
     copies = []
-    for n in range(4):
-        part = h // 4 // 16 * 16
-        at = pl.ds(n * part, part if n < 3 else h - 3 * part)
-        gate = gate_ref[at, :].astype(jnp.float32)
+    for n, band in enumerate(bands):
+        loads[2 * n].wait()
+        loads[2 * n + 1].wait()
+        gate = gate_in[band, :].astype(jnp.float32)
         sig = jax.nn.sigmoid(gate)
-        done[at, :] = ((gate * sig) * up_ref[at, :].astype(jnp.float32)).astype(jnp.bfloat16)
+        done[band, :] = ((gate * sig) * up_in[band, :].astype(jnp.float32)).astype(jnp.bfloat16)
         for i in range(8):
-            copies.append(pltpu.make_async_copy(done.at[at, :], out_ref.at[i, at, :], sem.at[n, i]))
+            copies.append(pltpu.make_async_copy(done.at[band, :], out_ref.at[i, band, :], out_sem.at[n, i]))
             copies[-1].start()
     for copy in copies:
         copy.wait()
@@ -92,11 +99,11 @@
     return pl.pallas_call(
         hidden_kernel,
         out_shape=jax.ShapeDtypeStruct((8, h, t), jnp.bfloat16),
-        in_specs=[pl.BlockSpec(memory_space=pltpu.VMEM)] * 2,
+        in_specs=[pl.BlockSpec(memory_space=pltpu.HBM)] * 2,
         out_specs=pl.BlockSpec(memory_space=pl.ANY),
-        scratch_shapes=[pltpu.VMEM((h, t), jnp.bfloat16), pltpu.SemaphoreType.DMA((4, 8))],
+        scratch_shapes=[pltpu.VMEM((h, t), jnp.bfloat16)] * 3 + [pltpu.SemaphoreType.DMA((4, 2)), pltpu.SemaphoreType.DMA((4, 8))],
         cost_estimate=pl.CostEstimate(flops=2_000_000, bytes_accessed=10 * h * t * 2, transcendentals=h * t),
-        compiler_params=pltpu.CompilerParams(vmem_limit_bytes=2 << 20),
+        compiler_params=pltpu.CompilerParams(vmem_limit_bytes=60 * 1024 * 1024),
         name="hidden_copies",
     )(gate, up)
 
@@ -127,6 +134,34 @@
     )(g)
 
 
+def weights_kernel(hidden_ref, feats_ref, theirs_ref, ours_ref, held, sem):
+    t = hidden_ref.shape[2]
+    loads = [pltpu.make_async_copy(hidden_ref.at[i], held.at[:, t * i : t * (i + 1)], sem.at[i]) for i in range(8)]
+    for load in loads:
+        load.start()
+    for i in range(0, 8, 2):
+        loads[i].wait()
+        loads[i + 1].wait()
+        cols = slice(t * i, t * (i + 2))
+        for n, ref in enumerate((theirs_ref, ours_ref)):
+            part = jnp.dot(held[:, cols], feats_ref[cols, 256 * n : 256 * (n + 1)], preferred_element_type=jnp.float32)
+            ref[...] = part if i == 0 else ref[...] + part
+
+
+def weight_parts(hiddens, feats):
+    _, h, t = hiddens.shape
+    return pl.pallas_call(
+        weights_kernel,
+        out_shape=(jax.ShapeDtypeStruct((h, 256), jnp.float32),) * 2,
+        in_specs=[pl.BlockSpec(memory_space=pltpu.HBM), pl.BlockSpec(memory_space=pltpu.VMEM)],
+        out_specs=(pl.BlockSpec(memory_space=pltpu.VMEM),) * 2,
+        scratch_shapes=[pltpu.VMEM((h, 8 * t), jnp.bfloat16), pltpu.SemaphoreType.DMA((8,))],
+        cost_estimate=pl.CostEstimate(flops=2 * 8 * t * h * 512, bytes_accessed=4_000_000, transcendentals=0),
+        compiler_params=pltpu.CompilerParams(vmem_limit_bytes=12 << 20),
+        name="weight_parts",
+    )(hiddens, feats)
+
+
 def turned(x, axis, by):
     size = lax.axis_size(axis)
     return lax.ppermute(x, axis, [(i, (i + by) % size) for i in range(size)])
@@ -150,10 +185,10 @@
     got = lax.all_gather(message, "y", axis=1, tiled=True)
 
     scale = power(got[65].astype(jnp.float32), -1)
-    feats = (got[32:64].astype(jnp.float32) * scale).astype(jnp.bfloat16).reshape(8, t, 512)
-    part = lax.dot_general(hiddens, feats, (((0, 2), (0, 1)), ((), ())), preferred_element_type=jnp.float32)
-    swap = lax.all_gather(part[:, :256].astype(jnp.bfloat16), "c", axis=0)
-    part = part[:, 256:] + lax.dynamic_index_in_dim(swap, 1 - lax.axis_index("c"), 0, keepdims=False).astype(jnp.float32)
+    feats = (got[32:64].astype(jnp.float32) * scale).astype(jnp.bfloat16).reshape(8 * t, 512)
+    theirs, ours = weight_parts(hiddens, feats)
+    swap = lax.all_gather(theirs.astype(jnp.bfloat16), "c", axis=0)
+    part = ours + lax.dynamic_index_in_dim(swap, 1 - lax.axis_index("c"), 0, keepdims=False).astype(jnp.float32)
     away = turned(part[:, :128].astype(jnp.bfloat16), "zh", 1)
     here = part[:, 128:]
 

time: 121 us -> 120 us (level)
  matrix products: 5.55 us -> 2.03 us
  Pallas kernels: 2.71 us -> 6.21 us
  local copies, waits for them, and re-layouts: 2.79 us -> 0.87 us
    dot_general x1 -> x0, matrix products: 3.45 us -> none  [sections(): lax.dot_general(hiddens, feats, (((0, 2), (0, 1)), ((), ())), preferred_e...]
    pallas_call x0 -> x1, Pallas kernels: none -> 2.59 us  [weight_parts(): pl.pallas_call(weights_kernel, out_shape=(jax.ShapeDtypeStruct((h, 256),...]
    unnamed x14 -> x12, local copies, waits for them, and re-layouts: 2.74 us -> 0.85 us
where the time goes in v2:
time: 120 us; the launch traced here: 119 us
  blocking collectives  47.4 us (40%)
  starting transfers between devices  42.1 us (35%)
  waiting for transfers between devices  16.3 us (14%)
  Pallas kernels  6.21 us (5%)
  other arithmetic  3.75 us (3%)
  matrix products  2.03 us (2%)
    all_gather x1, blocking collectives, sections(): got = lax.all_gather(message, 'y', axis=1, tiled=True)  45.2 us
    ppermute x4, starting transfers between devices, turned(): return lax.ppermute(x, axis, [(i, (i + by) % size) for i in range(size)])  22.7 us
    all_to_all x1, starting transfers between devices, sections(): mine = lax.all_to_all(pieces, ('x', 'zl'), 0, 0)  14.9 us
    ppermute x4, waiting for transfers between devices, turned(): return lax.ppermute(x, axis, [(i, (i + by) % size) for i in range(size)])  8.35 us
    all_to_all x1, waiting for transfers between devices, sections(): mine = lax.all_to_all(pieces, ('x', 'zl'), 0, 0)  7.93 us
    all_to_all x1, starting transfers between devices, sections(): hiddens = lax.all_to_all(copies, 'x', 0, 0)  4.55 us
    pallas_call x1, Pallas kernels, weight_parts(): pl.pallas_call(weights_kernel, out_shape=(jax.ShapeDtypeStruct((h, 256),...  2.59 us
    convert_element_type x1, other arithmetic, sections(): (got[:32].astype(jnp.float32) * scale).astype(jnp.bfloat16)  2.56 us
  transfers between devices with their start and end apart: 6, of which 4 were waited for; matrix products, arithmetic and copies ran while one was open for 4% of the time, Pallas kernels for 2%

profile of v2, /device:TPU:130, one launch (start us, length us, event | category | flops | bytes accessed | tf_op | source)
XLA Modules:
  0.0 119.4 jit_solution(11830781249969856909)
XLA Ops:
  0.6 0.0 copy-start
  0.6 0.8 copy-done
  1.5 0.0 copy-start.1
  1.5 0.7 split_rows.1
  2.2 14.9 %all-to-all-start.1 = ((bf16[32,8,512]{2,1,0:T(8,128)(2,1)}), bf16[32,8,512]{2,1,0:T(8,128)(2,1)S(1)}, u32[]{:S(2)}, u32[]{:S(2)}) async-start(bf16[32,8,512]{2,1,0:T(8,128)(2,1)} %split_rows.1), calls=%async_computation.1 | async-start | bytes 524288 | tf_op jit(solution)/shard_map/all_to_all | solution.py:175
  17.1 2.5 %hidden_copies.1 = bf16[8,464,256]{2,1,0:T(8,128)(2,1)} custom-call(bf16[464,256]{1,0:T(8,128)(2,1)} %bitcast.33, bf16[464,256]{1,0:T(8,128)(2,1)} %bitcast.34), custom_call_target="tpu_custom_call" | custom-call | flops 2000000 | bytes 2375680 | tf_op jit(solution)/shard_map/hidden_copies/pallas_call | solution.py:99
  19.6 7.9 %all-to-all-done.1.rows_ref = bf16[32,8,512]{2,1,0:T(8,128)(2,1)S(1)} async-done(((bf16[32,8,512]{2,1,0:T(8,128)(2,1)}), bf16[32,8,512]{2,1,0:T(8,128)(2,1)S(1)}, u32[]{:S(2)}, u32[]{:S(2)}) %all-to-all-start.1) | async-done | bytes 262176 | tf_op jit(solution)/shard_map/all_to_all | solution.py:175
  27.6 4.6 %all-to-all-start = ((bf16[8,464,256]{2,1,0:T(8,128)(2,1)}), bf16[8,464,256]{2,1,0:T(8,128)(2,1)}, u32[]{:S(2)}, u32[]{:S(2)}) async-start(bf16[8,464,256]{2,1,0:T(8,128)(2,1)} %hidden_copies.1), calls=%async_computation | async-start | bytes 3801088 | tf_op jit(solution)/shard_map/all_to_all | solution.py:180
  32.1 0.0 copy-done.1
  32.1 3.3 %collective-permute-start = (bf16[8,4096]{1,0:T(8,128)(2,1)S(1)}, bf16[8,4096]{1,0:T(8,128)(2,1)S(1)}, u32[]{:S(2)}, u32[]{:S(2)}) collective-permute-start(bf16[8,4096]{1,0:T(8,128)(2,1)S(1)} %copy-done.1), channel_id=1, source_target_pairs={{0,8},{8,16},{16,24},{24,0},{1,9},{9,17},{17,25},{25,1},{2,10},{10... | collective-permute-start | bytes 196616 | tf_op jit(solution)/shard_map/ppermute | solution.py:167
  35.4 5.6 %collective-permute-start.1 = (bf16[8,4096]{1,0:T(8,128)(2,1)S(1)}, bf16[8,4096]{1,0:T(8,128)(2,1)S(1)}, u32[]{:S(2)}, u32[]{:S(2)}) collective-permute-start(bf16[8,4096]{1,0:T(8,128)(2,1)S(1)} %copy-done.1), channel_id=1, source_target_pairs={{0,16},{8,24},{16,0},{24,8},{1,17},{9,25},{17,1},{25,9},{2,18},{10... | collective-permute-start | bytes 196616 | tf_op jit(solution)/shard_map/ppermute | solution.py:167
  41.0 1.9 %collective-permute-start.2 = (bf16[8,4096]{1,0:T(8,128)(2,1)S(1)}, bf16[8,4096]{1,0:T(8,128)(2,1)S(1)}, u32[]{:S(2)}, u32[]{:S(2)}) collective-permute-start(bf16[8,4096]{1,0:T(8,128)(2,1)S(1)} %copy-done.1), channel_id=1, source_target_pairs={{0,24},{8,0},{16,8},{24,16},{1,25},{9,1},{17,9},{25,17},{2,26},{10... | collective-permute-start | bytes 196616 | tf_op jit(solution)/shard_map/ppermute | solution.py:167
  42.9 0.0 collective-permute-done.b_ref
  42.9 0.4 collective-permute-done.1.c_ref
  43.3 3.8 %collective-permute-done.2.d_ref = bf16[8,4096]{1,0:T(8,128)(2,1)S(1)} collective-permute-done((bf16[8,4096]{1,0:T(8,128)(2,1)S(1)}, bf16[8,4096]{1,0:T(8,128)(2,1)S(1)}, u32[]{:S(2)}, u32[]{:S(2)}) %collective-permute-start.2) | collective-permute-done | bytes 65568 | tf_op jit(solution)/shard_map/ppermute | solution.py:167
  47.2 0.2 shard_map.67
  47.4 0.2 shard_map.68
  47.6 0.2 maximum_convert_fusion
  47.7 45.2 %all-gather.2 = f16[66,64,512]{2,1,0:T(8,128)(2,1)S(1)} all-gather(f16[66,8,512]{2,1,0:T(8,128)(2,1)S(1)} %maximum_convert_fusion), channel_id=1, replica_groups=mesh['zh'=2,'x'=8,'c'=2,'zl'=4,'y'=8] {'y'}, dimensions={1}, use_global_device_ids=true | all-gather | bytes 4866048 | tf_op jit(solution)/shard_map/all_gather | solution.py:185
  93.0 0.2 fusion.18
  93.2 2.6 %multiply_convert_fusion = (bf16[32,64,512]{2,1,0:T(8,128)(2,1)}, bf16[32,64,512]{2,1,0:T(8,128)(2,1)S(1)}) fusion(f16[66,64,512]{2,1,0:T(8,128)(2,1)S(1)} %all-gather.2, f32[64,512]{1,0:T(8,128)S(1)} %get-tuple-element.17, f32[64,512]{1,0:T(8,128)S(1)} %get-tuple-element.18), kind=kLoop, calls=%fused_computation | loop fusion | flops 6291456 | bytes 8650752 | tf_op jit(solution)/shard_map/convert_element_type | solution.py:196
  95.8 0.0 copy-start.3
  95.8 0.0 copy-start.4
  95.8 0.0 all-to-all-done.hidden_ref
  95.8 0.0 copy-start.2
  95.8 0.0 copy-start.5
  95.8 2.6 %weight_parts.1 = (f32[464,256]{1,0:T(8,128)S(1)}, f32[464,256]{1,0:T(8,128)S(1)}) custom-call(bf16[8,464,256]{2,1,0:T(8,128)(2,1)} %all-to-all-done.hidden_ref, bf16[2048,512]{1,0:T(8,128)(2,1)S(1)} %bitcast.28), custom_call_target="tpu_custom_call" | custom-call | flops 973078528 | bytes 4000000 | tf_op jit(solution)/shard_map/weight_parts/pallas_call | solution.py:153
  98.4 2.1 %all-gather = bf16[928,256]{1,0:T(8,128)(2,1)S(1)} all-gather(bf16[464,256]{1,0:T(8,128)(2,1)S(1)} %convert_element_type.57), channel_id=2, replica_groups=mesh['zh'=2,'x'=8,'c'=2,'zl'=4,'y'=8] {'c'}, dimensions={0}, use_global_device_ids=true | all-gather | bytes 712704 | tf_op jit(solution)/shard_map/all_gather | solution.py:190
  100.6 0.1 convert_add_fusion
  100.7 11.9 %collective-permute-start.3 = (bf16[464,128]{1,0:T(8,128)(2,1)S(1)}, bf16[464,128]{1,0:T(8,128)(2,1)S(1)}, u32[]{:S(2)}, u32[]{:S(2)}) collective-permute-start(bf16[464,128]{1,0:T(8,128)(2,1)S(1)} %slice.39), channel_id=1, source_target_pairs={{0,512},{512,0},{1,513},{513,1},{2,514},{514,2},{3,515},{515,3},{4... | collective-permute-start | bytes 356360 | tf_op jit(solution)/shard_map/ppermute | solution.py:167
  112.5 0.0 copy-done.3
  112.5 0.0 copy-done.4
  112.5 0.0 copy-done.2
  112.6 0.0 copy-done.5
  112.6 2.0 %fusion.13 = (bf16[256,464]{0,1:T(8,128)(2,1)}, bf16[256,464]{0,1:T(8,128)(2,1)}) fusion(bf16[256,464]{0,1:T(8,128)(2,1)S(1)} %copy-done.3, bf16[256,464]{0,1:T(8,128)(2,1)S(1)} %copy-done.4, bf16[8,256,512]{2,1,0:T(8,128)(2,1)S(1)} %bitcast.31, bf16[58,8,8,512]{3,2,1,0:T(8,128)(2,1)S(1)} %bitcast.35), kind=kOutput, calls=%fused_computation.17 | convolution fusion | flops 974860288 | bytes 6848512 | tf_op jit(solution)/shard_map/dot_general | solution.py:198
  114.6 4.1 %collective-permute-done.3 = bf16[464,128]{1,0:T(8,128)(2,1)S(1)} collective-permute-done((bf16[464,128]{1,0:T(8,128)(2,1)S(1)}, bf16[464,128]{1,0:T(8,128)(2,1)S(1)}, u32[]{:S(2)}, u32[]{:S(2)}) %collective-permute-start.3) | collective-permute-done | bytes 118816 | tf_op jit(solution)/shard_map/ppermute | solution.py:167
  118.7 0.7 fusion.14
  (2 shorter events, 0.0 us)
Async XLA Ops:
  0.6 0.8 copy-start
  1.5 30.6 %copy-start.1 = (bf16[8,4096]{1,0:T(8,128)(2,1)S(1)}, bf16[8,4096]{1,0:T(8,128)(2,1)}, u32[]{:S(2)}) copy-start(bf16[8,4096]{1,0:T(8,128)(2,1)} %g_ref.1) | copy-start | bytes 196612
  2.2 25.3 %all-to-all-start.1 = ((bf16[32,8,512]{2,1,0:T(8,128)(2,1)}), bf16[32,8,512]{2,1,0:T(8,128)(2,1)S(1)}, u32[]{:S(2)}, u32[]{:S(2)}) async-start(bf16[32,8,512]{2,1,0:T(8,128)(2,1)} %split_rows.1), calls=%async_computation.1 | async-start | bytes 524288 | tf_op jit(solution)/shard_map/all_to_all | solution.py:175
  27.6 68.2 %all-to-all-start = ((bf16[8,464,256]{2,1,0:T(8,128)(2,1)}), bf16[8,464,256]{2,1,0:T(8,128)(2,1)}, u32[]{:S(2)}, u32[]{:S(2)}) async-start(bf16[8,464,256]{2,1,0:T(8,128)(2,1)} %hidden_copies.1), calls=%async_computation | async-start | bytes 3801088 | tf_op jit(solution)/shard_map/all_to_all | solution.py:180
  32.1 10.8 %collective-permute-start = (bf16[8,4096]{1,0:T(8,128)(2,1)S(1)}, bf16[8,4096]{1,0:T(8,128)(2,1)S(1)}, u32[]{:S(2)}, u32[]{:S(2)}) collective-permute-start(bf16[8,4096]{1,0:T(8,128)(2,1)S(1)} %copy-done.1), channel_id=1, source_target_pairs={{0,8},{8,16},{16,24},{24,0},{1,9},{9,17},{17,25},{25,1},{2,10},{10... | collective-permute-start | bytes 196616 | tf_op jit(solution)/shard_map/ppermute | solution.py:167
  35.4 8.0 %collective-permute-start.1 = (bf16[8,4096]{1,0:T(8,128)(2,1)S(1)}, bf16[8,4096]{1,0:T(8,128)(2,1)S(1)}, u32[]{:S(2)}, u32[]{:S(2)}) collective-permute-start(bf16[8,4096]{1,0:T(8,128)(2,1)S(1)} %copy-done.1), channel_id=1, source_target_pairs={{0,16},{8,24},{16,0},{24,8},{1,17},{9,25},{17,1},{25,9},{2,18},{10... | collective-permute-start | bytes 196616 | tf_op jit(solution)/shard_map/ppermute | solution.py:167
  41.0 6.2 %collective-permute-start.2 = (bf16[8,4096]{1,0:T(8,128)(2,1)S(1)}, bf16[8,4096]{1,0:T(8,128)(2,1)S(1)}, u32[]{:S(2)}, u32[]{:S(2)}) collective-permute-start(bf16[8,4096]{1,0:T(8,128)(2,1)S(1)} %copy-done.1), channel_id=1, source_target_pairs={{0,24},{8,0},{16,8},{24,16},{1,25},{9,1},{17,9},{25,17},{2,26},{10... | collective-permute-start | bytes 196616 | tf_op jit(solution)/shard_map/ppermute | solution.py:167
  95.8 16.8 %copy-start.3 = (bf16[256,464]{0,1:T(8,128)(2,1)S(1)}, bf16[256,464]{0,1:T(8,128)(2,1)}, u32[]{:S(2)}) copy-start(bf16[256,464]{0,1:T(8,128)(2,1)} %param.5) | copy-start | bytes 712708
  95.8 16.8 %copy-start.4 = (bf16[256,464]{0,1:T(8,128)(2,1)S(1)}, bf16[256,464]{0,1:T(8,128)(2,1)}, u32[]{:S(2)}) copy-start(bf16[256,464]{0,1:T(8,128)(2,1)} %param.6) | copy-start | bytes 712708
  95.8 16.8 %copy-start.2 = (bf16[32,64,512]{2,1,0:T(8,128)(2,1)S(1)}, bf16[32,64,512]{2,1,0:T(8,128)(2,1)}, u32[]{:S(2)}) copy-start(bf16[32,64,512]{2,1,0:T(8,128)(2,1)} %get-tuple-element.15) | copy-start | bytes 6291460
  95.8 16.8 %copy-start.5 = (bf16[4096,464]{0,1:T(8,128)(2,1)S(1)}, bf16[4096,464]{0,1:T(8,128)(2,1)}, u32[]{:S(2)}) copy-start(bf16[4096,464]{0,1:T(8,128)(2,1)} %param.7) | copy-start | bytes 11403268
  100.7 18.1 %collective-permute-start.3 = (bf16[464,128]{1,0:T(8,128)(2,1)S(1)}, bf16[464,128]{1,0:T(8,128)(2,1)S(1)}, u32[]{:S(2)}, u32[]{:S(2)}) collective-permute-start(bf16[464,128]{1,0:T(8,128)(2,1)S(1)} %slice.39), channel_id=1, source_target_pairs={{0,512},{512,0},{1,513},{513,1},{2,514},{514,2},{3,515},{515,3},{4... | collective-permute-start | bytes 356360 | tf_op jit(solution)/shard_map/ppermute | solution.py:167

commit v3 on v2

--- a/solution.py
+++ b/solution.py
@@ -45,7 +45,7 @@
         scale, k = scales_of(most)
         k_ref[:, 128 * b : 128 * (b + 1)] = jnp.broadcast_to(k, (8, 128)).astype(jnp.bfloat16)
         for s, ref in enumerate(turns):
-            place = lax.rem(zl + 4 - s, 4)
+            place = lax.bitwise_xor(zl, s)
             for q in range(8):
                 value = ref[:, 512 * q + 128 * b : 512 * q + 128 * (b + 1)].astype(jnp.float32) * scale
                 out_ref[4 * q + place, :, 128 * b : 128 * (b + 1)] = value.astype(jnp.bfloat16)
@@ -163,13 +163,54 @@
 
 
 def turned(x, axis, by):
-    size = lax.axis_size(axis)
-    return lax.ppermute(x, axis, [(i, (i + by) % size) for i in range(size)])
+    return lax.ppermute(x, axis, [(i, i ^ by) for i in range(lax.axis_size(axis))])
+
+
+def inputs_kernel(whole_ref, weight_ref, gate_ref, up_ref, grad_gate_ref, grad_up_ref, weight, gate_in, up_in, total, sem):
+    n = weight.shape[0]
+    loads = [pltpu.make_async_copy(weight_ref.at[:, 512 * q : 512 * (q + 1)], weight.at[q], sem.at[q]) for q in range(n)]
+    loads.append(pltpu.make_async_copy(gate_ref, gate_in, sem.at[n]))
+    loads.append(pltpu.make_async_copy(up_ref, up_in, sem.at[n + 1]))
+    for load in loads:
+        load.start()
+    for q in range(n):
+        loads[q].wait()
+        part = lax.dot_general(weight[q], whole_ref[q], (((1,), (1,)), ((), ())), preferred_element_type=jnp.float32)
+        total[...] = part if q == 0 else total[...] + part
+    loads[n].wait()
+    loads[n + 1].wait()
+    grad_hidden = total[...]
+    gate = gate_in[...].astype(jnp.float32)
+    upper = up_in[...].astype(jnp.float32)
+    sig = jax.nn.sigmoid(gate)
+    grad_up_ref[...] = (grad_hidden * (gate * sig)).astype(jnp.bfloat16)
+    grad_gate_ref[...] = (grad_hidden * upper * sig * (1.0 + gate * (1.0 - sig))).astype(jnp.bfloat16)
+
+
+def input_grads(whole, weight, gate, up):
+    h, t = gate.shape
+    n = whole.shape[0]
+    return pl.pallas_call(
+        inputs_kernel,
+        out_shape=(jax.ShapeDtypeStruct((h, t), jnp.bfloat16),) * 2,
+        in_specs=[pl.BlockSpec(memory_space=pltpu.VMEM)] + [pl.BlockSpec(memory_space=pltpu.HBM)] * 3,
+        out_specs=(pl.BlockSpec(memory_space=pltpu.VMEM),) * 2,
+        scratch_shapes=[
+            pltpu.VMEM((n, h, 512), jnp.bfloat16),
+            pltpu.VMEM((h, t), jnp.bfloat16),
+            pltpu.VMEM((h, t), jnp.bfloat16),
+            pltpu.VMEM((h, t), jnp.float32),
+            pltpu.SemaphoreType.DMA((n + 2,)),
+        ],
+        cost_estimate=pl.CostEstimate(flops=2 * h * t * 512 * n, bytes_accessed=6_000_000, transcendentals=h * t),
+        compiler_params=pltpu.CompilerParams(vmem_limit_bytes=50 << 20),
+        name="input_grads",
+    )(whole, weight, gate, up)
 
 
 def sections(grad_out, gate_pre, up_pre, down_weight):
     gate_t, up_t = gate_pre.T, up_pre.T
-    h, t = gate_t.shape
+    _, t = gate_t.shape
 
     pieces = split_rows(grad_out)
     mine = lax.all_to_all(pieces, ("x", "zl"), 0, 0)
@@ -194,14 +235,7 @@
 
     scale = power(got[64].astype(jnp.float32), -1)
     whole = (got[:32].astype(jnp.float32) * scale).astype(jnp.bfloat16).reshape(8, t, 512)
-    weight = down_weight.T.reshape(h, 8, 512)
-    grad_hidden = lax.dot_general(weight, whole, (((1, 2), (0, 2)), ((), ())), preferred_element_type=jnp.float32)
-    gate = gate_t.astype(jnp.float32)
-    upper = up_t.astype(jnp.float32)
-    sig = jax.nn.sigmoid(gate)
-    act = gate * sig
-    grad_up = (grad_hidden * act).astype(jnp.bfloat16)
-    grad_gate = (grad_hidden * upper * sig * (1.0 + gate * (1.0 - sig))).astype(jnp.bfloat16)
+    grad_gate, grad_up = input_grads(whole, down_weight.T, gate_t, up_t)
     return (here + away.astype(jnp.float32)).T, grad_gate.T, grad_up.T
 
 

time: 120 us -> 125 us (1.042)
  the two profiles are of different devices: /device:TPU:130 before, /device:TPU:1 now
where the time goes in v3:
time: 125 us; the launch traced here: 124 us
  blocking collectives  52.2 us (42%)
  starting transfers between devices  41 us (33%)
  waiting for transfers between devices  13 us (10%)
  Pallas kernels  10.9 us (9%)
  other arithmetic  3.75 us (3%)
  local copies, waits for them, and re-layouts  2.46 us (2%)
    all_gather x1, blocking collectives, sections(): got = lax.all_gather(message, 'y', axis=1, tiled=True)  46.6 us
    ppermute x4, starting transfers between devices, turned(): lax.ppermute(x, axis, [(i, i ^ by) for i in range(lax.axis_size(axis))])  20.8 us
    all_to_all x1, starting transfers between devices, sections(): mine = lax.all_to_all(pieces, ('x', 'zl'), 0, 0)  15.9 us
    all_to_all x1, waiting for transfers between devices, sections(): mine = lax.all_to_all(pieces, ('x', 'zl'), 0, 0)  8.5 us
    all_gather x1, blocking collectives, sections(): swap = lax.all_gather(theirs.astype(jnp.bfloat16), 'c', axis=0)  5.69 us
    pallas_call x1, Pallas kernels, input_grads(): pl.pallas_call(inputs_kernel, out_shape=(jax.ShapeDtypeStruct((h, t), jnp...  4.78 us
    ppermute x4, waiting for transfers between devices, turned(): lax.ppermute(x, axis, [(i, i ^ by) for i in range(lax.axis_size(axis))])  4.53 us
    all_to_all x1, starting transfers between devices, sections(): hiddens = lax.all_to_all(copies, 'x', 0, 0)  4.34 us
  transfers between devices with their start and end apart: 6, of which 3 were waited for; matrix products, arithmetic and copies ran while one was open for 2% of the time, Pallas kernels for 6%

profile of v3, /device:TPU:1, one launch (start us, length us, event | category | flops | bytes accessed | tf_op | source)
XLA Modules:
  0.0 124.2 jit_solution(14192931079442244746)
XLA Ops:
  0.6 0.0 copy-start.3
  0.6 0.8 copy-done.3
  1.5 0.0 copy-start.4
  1.5 0.8 split_rows.1
  2.2 15.9 %all-to-all-start.1 = ((bf16[32,8,512]{2,1,0:T(8,128)(2,1)}), bf16[32,8,512]{2,1,0:T(8,128)(2,1)S(1)}, u32[]{:S(2)}, u32[]{:S(2)}) async-start(bf16[32,8,512]{2,1,0:T(8,128)(2,1)} %split_rows.1), calls=%async_computation.1 | async-start | bytes 524288 | tf_op jit(solution)/shard_map/all_to_all | solution.py:216
  18.1 2.5 %hidden_copies.1 = bf16[8,464,256]{2,1,0:T(8,128)(2,1)} custom-call(bf16[464,256]{1,0:T(8,128)(2,1)} %bitcast.21, bf16[464,256]{1,0:T(8,128)(2,1)} %bitcast.23), custom_call_target="tpu_custom_call" | custom-call | flops 2000000 | bytes 2375680 | tf_op jit(solution)/shard_map/hidden_copies/pallas_call | solution.py:99
  20.6 8.5 %all-to-all-done.1.rows_ref = bf16[32,8,512]{2,1,0:T(8,128)(2,1)S(1)} async-done(((bf16[32,8,512]{2,1,0:T(8,128)(2,1)}), bf16[32,8,512]{2,1,0:T(8,128)(2,1)S(1)}, u32[]{:S(2)}, u32[]{:S(2)}) %all-to-all-start.1) | async-done | bytes 262176 | tf_op jit(solution)/shard_map/all_to_all | solution.py:216
  29.1 4.3 %all-to-all-start = ((bf16[8,464,256]{2,1,0:T(8,128)(2,1)}), bf16[8,464,256]{2,1,0:T(8,128)(2,1)}, u32[]{:S(2)}, u32[]{:S(2)}) async-start(bf16[8,464,256]{2,1,0:T(8,128)(2,1)} %hidden_copies.1), calls=%async_computation | async-start | bytes 3801088 | tf_op jit(solution)/shard_map/all_to_all | solution.py:221
  33.4 0.0 copy-done.4
  33.5 1.9 %collective-permute-start = (bf16[8,4096]{1,0:T(8,128)(2,1)S(1)}, bf16[8,4096]{1,0:T(8,128)(2,1)S(1)}, u32[]{:S(2)}, u32[]{:S(2)}) collective-permute-start(bf16[8,4096]{1,0:T(8,128)(2,1)S(1)} %copy-done.4), channel_id=1, source_target_pairs={{0,8},{8,0},{16,24},{24,16},{1,9},{9,1},{17,25},{25,17},{2,10},{10... | collective-permute-start | bytes 196616 | tf_op jit(solution)/shard_map/ppermute | solution.py:166
  35.4 3.7 %collective-permute-start.1 = (bf16[8,4096]{1,0:T(8,128)(2,1)S(1)}, bf16[8,4096]{1,0:T(8,128)(2,1)S(1)}, u32[]{:S(2)}, u32[]{:S(2)}) collective-permute-start(bf16[8,4096]{1,0:T(8,128)(2,1)S(1)} %copy-done.4), channel_id=1, source_target_pairs={{0,16},{8,24},{16,0},{24,8},{1,17},{9,25},{17,1},{25,9},{2,18},{10... | collective-permute-start | bytes 196616 | tf_op jit(solution)/shard_map/ppermute | solution.py:166
  39.1 3.6 %collective-permute-start.2 = (bf16[8,4096]{1,0:T(8,128)(2,1)S(1)}, bf16[8,4096]{1,0:T(8,128)(2,1)S(1)}, u32[]{:S(2)}, u32[]{:S(2)}) collective-permute-start(bf16[8,4096]{1,0:T(8,128)(2,1)S(1)} %copy-done.4), channel_id=1, source_target_pairs={{0,24},{8,16},{16,8},{24,0},{1,25},{9,17},{17,9},{25,1},{2,26},{10... | collective-permute-start | bytes 196616 | tf_op jit(solution)/shard_map/ppermute | solution.py:166
  42.8 0.0 collective-permute-done.b_ref
  42.8 0.0 collective-permute-done.1.c_ref
  42.8 3.6 %collective-permute-done.2.d_ref = bf16[8,4096]{1,0:T(8,128)(2,1)S(1)} collective-permute-done((bf16[8,4096]{1,0:T(8,128)(2,1)S(1)}, bf16[8,4096]{1,0:T(8,128)(2,1)S(1)}, u32[]{:S(2)}, u32[]{:S(2)}) %collective-permute-start.2) | collective-permute-done | bytes 65568 | tf_op jit(solution)/shard_map/ppermute | solution.py:166
  46.3 0.2 shard_map.67
  46.5 0.2 shard_map.68
  46.7 0.2 maximum_convert_fusion
  46.9 46.6 %all-gather.2 = f16[66,64,512]{2,1,0:T(8,128)(2,1)S(1)} all-gather(f16[66,8,512]{2,1,0:T(8,128)(2,1)S(1)} %maximum_convert_fusion), channel_id=1, replica_groups=mesh['zh'=2,'x'=8,'c'=2,'zl'=4,'y'=8] {'y'}, dimensions={1}, use_global_device_ids=true | all-gather | bytes 4866048 | tf_op jit(solution)/shard_map/all_gather | solution.py:226
  93.5 0.2 fusion.4
  93.7 0.0 copy-start.1
  93.7 0.0 copy-start.2
  93.7 2.6 %multiply_convert_fusion = (bf16[32,64,512]{2,1,0:T(8,128)(2,1)S(1)}, bf16[32,64,512]{2,1,0:T(8,128)(2,1)}) fusion(f16[66,64,512]{2,1,0:T(8,128)(2,1)S(1)} %all-gather.2, f32[64,512]{1,0:T(8,128)S(1)} %get-tuple-element.21, f32[64,512]{1,0:T(8,128)S(1)} %get-tuple-element.22), kind=kLoop, calls=%fused_computation | loop fusion | flops 6291456 | bytes 8650752 | tf_op jit(solution)/shard_map/convert_element_type | solution.py:237
  96.3 0.0 all-to-all-done.hidden_ref
  96.3 0.0 copy-start
  96.3 1.6 %copy-done = bf16[32,64,512]{2,1,0:T(8,128)(2,1)S(1)} copy-done((bf16[32,64,512]{2,1,0:T(8,128)(2,1)S(1)}, bf16[32,64,512]{2,1,0:T(8,128)(2,1)}, u32[]{:S(2)}) %copy-start) | copy-done | bytes 2097176
  97.9 2.5 %weight_parts.1 = (f32[464,256]{1,0:T(8,128)S(1)}, f32[464,256]{1,0:T(8,128)S(1)}) custom-call(bf16[8,464,256]{2,1,0:T(8,128)(2,1)} %all-to-all-done.hidden_ref, bf16[2048,512]{1,0:T(8,128)(2,1)S(1)} %bitcast.20), custom_call_target="tpu_custom_call" | custom-call | flops 973078528 | bytes 4000000 | tf_op jit(solution)/shard_map/weight_parts/pallas_call | solution.py:153
  100.4 5.7 %all-gather = bf16[928,256]{1,0:T(8,128)(2,1)S(1)} all-gather(bf16[464,256]{1,0:T(8,128)(2,1)S(1)} %convert_element_type.40), channel_id=2, replica_groups=mesh['zh'=2,'x'=8,'c'=2,'zl'=4,'y'=8] {'c'}, dimensions={0}, use_global_device_ids=true | all-gather | bytes 712704 | tf_op jit(solution)/shard_map/all_gather | solution.py:231
  106.1 0.1 convert_add_fusion
  106.1 11.6 %collective-permute-start.3 = (bf16[464,128]{1,0:T(8,128)(2,1)S(1)}, bf16[464,128]{1,0:T(8,128)(2,1)S(1)}, u32[]{:S(2)}, u32[]{:S(2)}) collective-permute-start(bf16[464,128]{1,0:T(8,128)(2,1)S(1)} %slice.39), channel_id=1, source_target_pairs={{0,512},{512,0},{1,513},{513,1},{2,514},{514,2},{3,515},{515,3},{4... | collective-permute-start | bytes 356360 | tf_op jit(solution)/shard_map/ppermute | solution.py:166
  117.7 0.0 copy-done.1
  117.7 0.0 copy-done.2
  117.8 4.8 %input_grads.1 = (bf16[464,256]{1,0:T(8,128)(2,1)}, bf16[464,256]{1,0:T(8,128)(2,1)}) custom-call(bf16[8,256,512]{2,1,0:T(8,128)(2,1)S(1)} %bitcast.19, bf16[464,4096]{1,0:T(8,128)(2,1)} %bitcast.27, bf16[464,256]{1,0:T(8,128)(2,1)S(1)} %bitcast.22, bf16[464,256]{1,0:T(8,128)(2,1)S(1)} %bitcast.24), custom_call_target="tpu_custom_call" | custom-call | flops 973078528 | bytes 6000000 | tf_op jit(solution)/shard_map/input_grads/pallas_call | solution.py:193
  122.5 1.0 collective-permute-done.3
  123.5 0.7 fusion
  (2 shorter events, 0.0 us)
Async XLA Ops:
  0.6 0.8 copy-start.3
  1.5 32.0 %copy-start.4 = (bf16[8,4096]{1,0:T(8,128)(2,1)S(1)}, bf16[8,4096]{1,0:T(8,128)(2,1)}, u32[]{:S(2)}) copy-start(bf16[8,4096]{1,0:T(8,128)(2,1)} %g_ref.1) | copy-start | bytes 196612
  2.2 26.9 %all-to-all-start.1 = ((bf16[32,8,512]{2,1,0:T(8,128)(2,1)}), bf16[32,8,512]{2,1,0:T(8,128)(2,1)S(1)}, u32[]{:S(2)}, u32[]{:S(2)}) async-start(bf16[32,8,512]{2,1,0:T(8,128)(2,1)} %split_rows.1), calls=%async_computation.1 | async-start | bytes 524288 | tf_op jit(solution)/shard_map/all_to_all | solution.py:216
  29.1 67.2 %all-to-all-start = ((bf16[8,464,256]{2,1,0:T(8,128)(2,1)}), bf16[8,464,256]{2,1,0:T(8,128)(2,1)}, u32[]{:S(2)}, u32[]{:S(2)}) async-start(bf16[8,464,256]{2,1,0:T(8,128)(2,1)} %hidden_copies.1), calls=%async_computation | async-start | bytes 3801088 | tf_op jit(solution)/shard_map/all_to_all | solution.py:221
  33.5 9.3 %collective-permute-start = (bf16[8,4096]{1,0:T(8,128)(2,1)S(1)}, bf16[8,4096]{1,0:T(8,128)(2,1)S(1)}, u32[]{:S(2)}, u32[]{:S(2)}) collective-permute-start(bf16[8,4096]{1,0:T(8,128)(2,1)S(1)} %copy-done.4), channel_id=1, source_target_pairs={{0,8},{8,0},{16,24},{24,16},{1,9},{9,1},{17,25},{25,17},{2,10},{10... | collective-permute-start | bytes 196616 | tf_op jit(solution)/shard_map/ppermute | solution.py:166
  35.4 7.4 %collective-permute-start.1 = (bf16[8,4096]{1,0:T(8,128)(2,1)S(1)}, bf16[8,4096]{1,0:T(8,128)(2,1)S(1)}, u32[]{:S(2)}, u32[]{:S(2)}) collective-permute-start(bf16[8,4096]{1,0:T(8,128)(2,1)S(1)} %copy-done.4), channel_id=1, source_target_pairs={{0,16},{8,24},{16,0},{24,8},{1,17},{9,25},{17,1},{25,9},{2,18},{10... | collective-permute-start | bytes 196616 | tf_op jit(solution)/shard_map/ppermute | solution.py:166
  39.1 7.2 %collective-permute-start.2 = (bf16[8,4096]{1,0:T(8,128)(2,1)S(1)}, bf16[8,4096]{1,0:T(8,128)(2,1)S(1)}, u32[]{:S(2)}, u32[]{:S(2)}) collective-permute-start(bf16[8,4096]{1,0:T(8,128)(2,1)S(1)} %copy-done.4), channel_id=1, source_target_pairs={{0,24},{8,16},{16,8},{24,0},{1,25},{9,17},{17,9},{25,1},{2,26},{10... | collective-permute-start | bytes 196616 | tf_op jit(solution)/shard_map/ppermute | solution.py:166
  93.7 24.0 %copy-start.1 = (bf16[256,464]{0,1:T(8,128)(2,1)S(1)}, bf16[256,464]{0,1:T(8,128)(2,1)}, u32[]{:S(2)}) copy-start(bf16[256,464]{0,1:T(8,128)(2,1)} %param.5) | copy-start | bytes 712708
  93.7 24.0 %copy-start.2 = (bf16[256,464]{0,1:T(8,128)(2,1)S(1)}, bf16[256,464]{0,1:T(8,128)(2,1)}, u32[]{:S(2)}) copy-start(bf16[256,464]{0,1:T(8,128)(2,1)} %param.6) | copy-start | bytes 712708
  96.3 1.6 %copy-start = (bf16[32,64,512]{2,1,0:T(8,128)(2,1)S(1)}, bf16[32,64,512]{2,1,0:T(8,128)(2,1)}, u32[]{:S(2)}) copy-start(bf16[32,64,512]{2,1,0:T(8,128)(2,1)} %get-tuple-element.20) | copy-start | bytes 6291460
  106.1 17.4 %collective-permute-start.3 = (bf16[464,128]{1,0:T(8,128)(2,1)S(1)}, bf16[464,128]{1,0:T(8,128)(2,1)S(1)}, u32[]{:S(2)}, u32[]{:S(2)}) collective-permute-start(bf16[464,128]{1,0:T(8,128)(2,1)S(1)} %slice.39), channel_id=1, source_target_pairs={{0,512},{512,0},{1,513},{513,1},{2,514},{514,2},{3,515},{515,3},{4... | collective-permute-start | bytes 356360 | tf_op jit(solution)/shard_map/ppermute | solution.py:166

commit v4 on v2

--- a/solution.py
+++ b/solution.py
@@ -45,7 +45,7 @@
         scale, k = scales_of(most)
         k_ref[:, 128 * b : 128 * (b + 1)] = jnp.broadcast_to(k, (8, 128)).astype(jnp.bfloat16)
         for s, ref in enumerate(turns):
-            place = lax.rem(zl + 4 - s, 4)
+            place = lax.bitwise_xor(zl, s)
             for q in range(8):
                 value = ref[:, 512 * q + 128 * b : 512 * q + 128 * (b + 1)].astype(jnp.float32) * scale
                 out_ref[4 * q + place, :, 128 * b : 128 * (b + 1)] = value.astype(jnp.bfloat16)
@@ -163,8 +163,7 @@
 
 
 def turned(x, axis, by):
-    size = lax.axis_size(axis)
-    return lax.ppermute(x, axis, [(i, (i + by) % size) for i in range(size)])
+    return lax.ppermute(x, axis, [(i, i ^ by) for i in range(lax.axis_size(axis))])
 
 
 def sections(grad_out, gate_pre, up_pre, down_weight):

time: 120 us -> 123 us (1.025)
  the two profiles are of different devices: /device:TPU:130 before, /device:TPU:1 now
where the time goes in v4:
time: 123 us
  blocking collectives  52.2 us (42%)
  starting transfers between devices  41 us (33%)
  waiting for transfers between devices  15.7 us (13%)
  Pallas kernels  6.21 us (5%)
  other arithmetic  3.75 us (3%)
  matrix products  2.04 us (2%)
    all_gather x1, blocking collectives, sections(): got = lax.all_gather(message, 'y', axis=1, tiled=True)  46.6 us
    ppermute x4, starting transfers between devices, turned(): lax.ppermute(x, axis, [(i, i ^ by) for i in range(lax.axis_size(axis))])  20.9 us
    all_to_all x1, starting transfers between devices, sections(): mine = lax.all_to_all(pieces, ('x', 'zl'), 0, 0)  15.9 us
    all_to_all x1, waiting for transfers between devices, sections(): mine = lax.all_to_all(pieces, ('x', 'zl'), 0, 0)  8.49 us
    ppermute x4, waiting for transfers between devices, turned(): lax.ppermute(x, axis, [(i, i ^ by) for i in range(lax.axis_size(axis))])  7.25 us
    all_gather x1, blocking collectives, sections(): swap = lax.all_gather(theirs.astype(jnp.bfloat16), 'c', axis=0)  5.69 us
    all_to_all x1, starting transfers between devices, sections(): hiddens = lax.all_to_all(copies, 'x', 0, 0)  4.32 us
    pallas_call x1, Pallas kernels, weight_parts(): pl.pallas_call(weights_kernel, out_shape=(jax.ShapeDtypeStruct((h, 256),...  2.59 us
  transfers between devices with their start and end apart: 6, of which 3 were waited for; matrix products, arithmetic and copies ran while one was open for 4% of the time, Pallas kernels for 2%

profile of v4, /device:TPU:1, one launch (start us, length us, event | category | flops | bytes accessed | tf_op | source)
XLA Modules:
  0.0 122.7 jit_solution(4027809701574793571)
XLA Ops:
  0.6 0.0 copy-start
  0.6 0.8 copy-done
  1.5 0.0 copy-start.1
  1.5 0.7 split_rows.1
  2.2 15.9 %all-to-all-start.1 = ((bf16[32,8,512]{2,1,0:T(8,128)(2,1)}), bf16[32,8,512]{2,1,0:T(8,128)(2,1)S(1)}, u32[]{:S(2)}, u32[]{:S(2)}) async-start(bf16[32,8,512]{2,1,0:T(8,128)(2,1)} %split_rows.1), calls=%async_computation.1 | async-start | bytes 524288 | tf_op jit(solution)/shard_map/all_to_all | solution.py:174
  18.1 2.5 %hidden_copies.1 = bf16[8,464,256]{2,1,0:T(8,128)(2,1)} custom-call(bf16[464,256]{1,0:T(8,128)(2,1)} %bitcast.33, bf16[464,256]{1,0:T(8,128)(2,1)} %bitcast.34), custom_call_target="tpu_custom_call" | custom-call | flops 2000000 | bytes 2375680 | tf_op jit(solution)/shard_map/hidden_copies/pallas_call | solution.py:99
  20.6 8.5 %all-to-all-done.1.rows_ref = bf16[32,8,512]{2,1,0:T(8,128)(2,1)S(1)} async-done(((bf16[32,8,512]{2,1,0:T(8,128)(2,1)}), bf16[32,8,512]{2,1,0:T(8,128)(2,1)S(1)}, u32[]{:S(2)}, u32[]{:S(2)}) %all-to-all-start.1) | async-done | bytes 262176 | tf_op jit(solution)/shard_map/all_to_all | solution.py:174
  29.1 4.3 %all-to-all-start = ((bf16[8,464,256]{2,1,0:T(8,128)(2,1)}), bf16[8,464,256]{2,1,0:T(8,128)(2,1)}, u32[]{:S(2)}, u32[]{:S(2)}) async-start(bf16[8,464,256]{2,1,0:T(8,128)(2,1)} %hidden_copies.1), calls=%async_computation | async-start | bytes 3801088 | tf_op jit(solution)/shard_map/all_to_all | solution.py:179
  33.4 0.0 copy-done.1
  33.4 1.9 %collective-permute-start = (bf16[8,4096]{1,0:T(8,128)(2,1)S(1)}, bf16[8,4096]{1,0:T(8,128)(2,1)S(1)}, u32[]{:S(2)}, u32[]{:S(2)}) collective-permute-start(bf16[8,4096]{1,0:T(8,128)(2,1)S(1)} %copy-done.1), channel_id=1, source_target_pairs={{0,8},{8,0},{16,24},{24,16},{1,9},{9,1},{17,25},{25,17},{2,10},{10... | collective-permute-start | bytes 196616 | tf_op jit(solution)/shard_map/ppermute | solution.py:166
  35.3 3.7 %collective-permute-start.1 = (bf16[8,4096]{1,0:T(8,128)(2,1)S(1)}, bf16[8,4096]{1,0:T(8,128)(2,1)S(1)}, u32[]{:S(2)}, u32[]{:S(2)}) collective-permute-start(bf16[8,4096]{1,0:T(8,128)(2,1)S(1)} %copy-done.1), channel_id=1, source_target_pairs={{0,16},{8,24},{16,0},{24,8},{1,17},{9,25},{17,1},{25,9},{2,18},{10... | collective-permute-start | bytes 196616 | tf_op jit(solution)/shard_map/ppermute | solution.py:166
  39.1 3.6 %collective-permute-start.2 = (bf16[8,4096]{1,0:T(8,128)(2,1)S(1)}, bf16[8,4096]{1,0:T(8,128)(2,1)S(1)}, u32[]{:S(2)}, u32[]{:S(2)}) collective-permute-start(bf16[8,4096]{1,0:T(8,128)(2,1)S(1)} %copy-done.1), channel_id=1, source_target_pairs={{0,24},{8,16},{16,8},{24,0},{1,25},{9,17},{17,9},{25,1},{2,26},{10... | collective-permute-start | bytes 196616 | tf_op jit(solution)/shard_map/ppermute | solution.py:166
  42.7 0.0 collective-permute-done.b_ref
  42.7 0.0 collective-permute-done.1.c_ref
  42.7 3.6 %collective-permute-done.2.d_ref = bf16[8,4096]{1,0:T(8,128)(2,1)S(1)} collective-permute-done((bf16[8,4096]{1,0:T(8,128)(2,1)S(1)}, bf16[8,4096]{1,0:T(8,128)(2,1)S(1)}, u32[]{:S(2)}, u32[]{:S(2)}) %collective-permute-start.2) | collective-permute-done | bytes 65568 | tf_op jit(solution)/shard_map/ppermute | solution.py:166
  46.3 0.2 shard_map.67
  46.5 0.2 shard_map.68
  46.7 0.2 maximum_convert_fusion
  46.9 46.6 %all-gather.2 = f16[66,64,512]{2,1,0:T(8,128)(2,1)S(1)} all-gather(f16[66,8,512]{2,1,0:T(8,128)(2,1)S(1)} %maximum_convert_fusion), channel_id=1, replica_groups=mesh['zh'=2,'x'=8,'c'=2,'zl'=4,'y'=8] {'y'}, dimensions={1}, use_global_device_ids=true | all-gather | bytes 4866048 | tf_op jit(solution)/shard_map/all_gather | solution.py:184
  93.4 0.2 fusion.18
  93.7 2.6 %multiply_convert_fusion = (bf16[32,64,512]{2,1,0:T(8,128)(2,1)}, bf16[32,64,512]{2,1,0:T(8,128)(2,1)S(1)}) fusion(f16[66,64,512]{2,1,0:T(8,128)(2,1)S(1)} %all-gather.2, f32[64,512]{1,0:T(8,128)S(1)} %get-tuple-element.17, f32[64,512]{1,0:T(8,128)S(1)} %get-tuple-element.18), kind=kLoop, calls=%fused_computation | loop fusion | flops 6291456 | bytes 8650752 | tf_op jit(solution)/shard_map/convert_element_type | solution.py:195
  96.2 0.0 copy-start.3
  96.2 0.0 copy-start.4
  96.2 0.0 all-to-all-done.hidden_ref
  96.2 0.0 copy-start.2
  96.2 0.0 copy-start.5
  96.3 2.6 %weight_parts.1 = (f32[464,256]{1,0:T(8,128)S(1)}, f32[464,256]{1,0:T(8,128)S(1)}) custom-call(bf16[8,464,256]{2,1,0:T(8,128)(2,1)} %all-to-all-done.hidden_ref, bf16[2048,512]{1,0:T(8,128)(2,1)S(1)} %bitcast.28), custom_call_target="tpu_custom_call" | custom-call | flops 973078528 | bytes 4000000 | tf_op jit(solution)/shard_map/weight_parts/pallas_call | solution.py:153
  98.9 5.7 %all-gather = bf16[928,256]{1,0:T(8,128)(2,1)S(1)} all-gather(bf16[464,256]{1,0:T(8,128)(2,1)S(1)} %convert_element_type.57), channel_id=2, replica_groups=mesh['zh'=2,'x'=8,'c'=2,'zl'=4,'y'=8] {'c'}, dimensions={0}, use_global_device_ids=true | all-gather | bytes 712704 | tf_op jit(solution)/shard_map/all_gather | solution.py:189
  104.7 11.6 %collective-permute-start.3 = (bf16[464,128]{1,0:T(8,128)(2,1)S(1)}, bf16[464,128]{1,0:T(8,128)(2,1)S(1)}, u32[]{:S(2)}, u32[]{:S(2)}) collective-permute-start(bf16[464,128]{1,0:T(8,128)(2,1)S(1)} %slice.39), channel_id=1, source_target_pairs={{0,512},{512,0},{1,513},{513,1},{2,514},{514,2},{3,515},{515,3},{4... | collective-permute-start | bytes 356360 | tf_op jit(solution)/shard_map/ppermute | solution.py:166
  116.2 0.0 copy-done.3
  116.2 0.0 copy-done.4
  116.3 0.0 copy-done.2
  116.3 0.0 copy-done.5
  116.3 2.0 %fusion.13 = (bf16[256,464]{0,1:T(8,128)(2,1)}, bf16[256,464]{0,1:T(8,128)(2,1)}) fusion(bf16[256,464]{0,1:T(8,128)(2,1)S(1)} %copy-done.3, bf16[256,464]{0,1:T(8,128)(2,1)S(1)} %copy-done.4, bf16[8,256,512]{2,1,0:T(8,128)(2,1)S(1)} %bitcast.31, bf16[58,8,8,512]{3,2,1,0:T(8,128)(2,1)S(1)} %bitcast.35), kind=kOutput, calls=%fused_computation.17 | convolution fusion | flops 974860288 | bytes 6848512 | tf_op jit(solution)/shard_map/dot_general | solution.py:197
  118.3 3.7 %collective-permute-done.3 = bf16[464,128]{1,0:T(8,128)(2,1)S(1)} collective-permute-done((bf16[464,128]{1,0:T(8,128)(2,1)S(1)}, bf16[464,128]{1,0:T(8,128)(2,1)S(1)}, u32[]{:S(2)}, u32[]{:S(2)}) %collective-permute-start.3) | collective-permute-done | bytes 118816 | tf_op jit(solution)/shard_map/ppermute | solution.py:166
  122.0 0.7 fusion.14
  (3 shorter events, 0.1 us)
Async XLA Ops:
  0.6 0.8 copy-start
  1.5 31.9 %copy-start.1 = (bf16[8,4096]{1,0:T(8,128)(2,1)S(1)}, bf16[8,4096]{1,0:T(8,128)(2,1)}, u32[]{:S(2)}) copy-start(bf16[8,4096]{1,0:T(8,128)(2,1)} %g_ref.1) | copy-start | bytes 196612
  2.2 26.9 %all-to-all-start.1 = ((bf16[32,8,512]{2,1,0:T(8,128)(2,1)}), bf16[32,8,512]{2,1,0:T(8,128)(2,1)S(1)}, u32[]{:S(2)}, u32[]{:S(2)}) async-start(bf16[32,8,512]{2,1,0:T(8,128)(2,1)} %split_rows.1), calls=%async_computation.1 | async-start | bytes 524288 | tf_op jit(solution)/shard_map/all_to_all | solution.py:174
  29.1 67.2 %all-to-all-start = ((bf16[8,464,256]{2,1,0:T(8,128)(2,1)}), bf16[8,464,256]{2,1,0:T(8,128)(2,1)}, u32[]{:S(2)}, u32[]{:S(2)}) async-start(bf16[8,464,256]{2,1,0:T(8,128)(2,1)} %hidden_copies.1), calls=%async_computation | async-start | bytes 3801088 | tf_op jit(solution)/shard_map/all_to_all | solution.py:179
  33.4 9.3 %collective-permute-start = (bf16[8,4096]{1,0:T(8,128)(2,1)S(1)}, bf16[8,4096]{1,0:T(8,128)(2,1)S(1)}, u32[]{:S(2)}, u32[]{:S(2)}) collective-permute-start(bf16[8,4096]{1,0:T(8,128)(2,1)S(1)} %copy-done.1), channel_id=1, source_target_pairs={{0,8},{8,0},{16,24},{24,16},{1,9},{9,1},{17,25},{25,17},{2,10},{10... | collective-permute-start | bytes 196616 | tf_op jit(solution)/shard_map/ppermute | solution.py:166
  35.3 7.4 %collective-permute-start.1 = (bf16[8,4096]{1,0:T(8,128)(2,1)S(1)}, bf16[8,4096]{1,0:T(8,128)(2,1)S(1)}, u32[]{:S(2)}, u32[]{:S(2)}) collective-permute-start(bf16[8,4096]{1,0:T(8,128)(2,1)S(1)} %copy-done.1), channel_id=1, source_target_pairs={{0,16},{8,24},{16,0},{24,8},{1,17},{9,25},{17,1},{25,9},{2,18},{10... | collective-permute-start | bytes 196616 | tf_op jit(solution)/shard_map/ppermute | solution.py:166
  39.1 7.2 %collective-permute-start.2 = (bf16[8,4096]{1,0:T(8,128)(2,1)S(1)}, bf16[8,4096]{1,0:T(8,128)(2,1)S(1)}, u32[]{:S(2)}, u32[]{:S(2)}) collective-permute-start(bf16[8,4096]{1,0:T(8,128)(2,1)S(1)} %copy-done.1), channel_id=1, source_target_pairs={{0,24},{8,16},{16,8},{24,0},{1,25},{9,17},{17,9},{25,1},{2,26},{10... | collective-permute-start | bytes 196616 | tf_op jit(solution)/shard_map/ppermute | solution.py:166
  96.2 20.0 %copy-start.3 = (bf16[256,464]{0,1:T(8,128)(2,1)S(1)}, bf16[256,464]{0,1:T(8,128)(2,1)}, u32[]{:S(2)}) copy-start(bf16[256,464]{0,1:T(8,128)(2,1)} %param.5) | copy-start | bytes 712708
  96.2 20.0 %copy-start.4 = (bf16[256,464]{0,1:T(8,128)(2,1)S(1)}, bf16[256,464]{0,1:T(8,128)(2,1)}, u32[]{:S(2)}) copy-start(bf16[256,464]{0,1:T(8,128)(2,1)} %param.6) | copy-start | bytes 712708
  96.2 20.0 %copy-start.2 = (bf16[32,64,512]{2,1,0:T(8,128)(2,1)S(1)}, bf16[32,64,512]{2,1,0:T(8,128)(2,1)}, u32[]{:S(2)}) copy-start(bf16[32,64,512]{2,1,0:T(8,128)(2,1)} %get-tuple-element.15) | copy-start | bytes 6291460
  96.2 20.0 %copy-start.5 = (bf16[4096,464]{0,1:T(8,128)(2,1)S(1)}, bf16[4096,464]{0,1:T(8,128)(2,1)}, u32[]{:S(2)}) copy-start(bf16[4096,464]{0,1:T(8,128)(2,1)} %param.7) | copy-start | bytes 11403268
  104.7 17.3 %collective-permute-start.3 = (bf16[464,128]{1,0:T(8,128)(2,1)S(1)}, bf16[464,128]{1,0:T(8,128)(2,1)S(1)}, u32[]{:S(2)}, u32[]{:S(2)}) collective-permute-start(bf16[464,128]{1,0:T(8,128)(2,1)S(1)} %slice.39), channel_id=1, source_target_pairs={{0,512},{512,0},{1,513},{513,1},{2,514},{514,2},{3,515},{515,3},{4... | collective-permute-start | bytes 356360 | tf_op jit(solution)/shard_map/ppermute | solution.py:166

commit v5 on v3

v5 whole, which is shorter than its diff:
```python
import jax
import jax.numpy as jnp
from jax import lax
from jax.experimental import pallas as pl
from jax.experimental.pallas import tpu as pltpu
from jax.sharding import Mesh, PartitionSpec as P


AXES = ("zh", "xh", "xl", "c", "zl", "y")
NEAR = ("zh", "xl")
STEPS = (64.0, 32.0, 16.0, 8.0, 4.0, 2.0)


def exponents(most):
    k = jnp.zeros_like(most)
    for bit in STEPS:
        fits = most * (2.0**bit) <= 32768.0
        most = jnp.where(fits, most * (2.0**bit), most)
        k = jnp.where(fits, k + bit, k)
    return k


def power(k, sign):
    scale = jnp.ones_like(k)
    for bit in STEPS:
        has = k >= bit
        scale = jnp.where(has, scale * (2.0 ** (sign * bit)), scale)
        k = jnp.where(has, k - bit, k)
    return scale


def scales_of(most):
    k = exponents(jnp.max(jnp.max(most, axis=1, keepdims=True), axis=0, keepdims=True))
    return power(k, 1), k


def columns(zh, xh, xl, c, size):
    return pl.multiple_of(2048 * zh + 512 * xh + 256 * xl + 128 * c, size)


def own_kernel(a_ref, b_ref, c_ref, d_ref, out_ref, k_ref):
    zh, xl, zl = lax.axis_index("zh"), lax.axis_index("xl"), lax.axis_index("zl")
    turns = (a_ref, b_ref, c_ref, d_ref)
    most = None
    for ref in turns:
        for n in range(32):
            value = jnp.abs(ref[:, 128 * n : 128 * (n + 1)].astype(jnp.float32))
            most = value if most is None else jnp.maximum(most, value)
    scale, k = scales_of(most)
    k_ref[...] = jnp.broadcast_to(k[None], (1, 8, 512)).astype(jnp.bfloat16)
    for turn, ref in enumerate(turns):
        place = lax.bitwise_xor(zl, turn)
        for s in (1, 2, 3):
            for xh in range(4):
                at = columns(lax.bitwise_xor(zh, s // 2), xh, lax.bitwise_xor(xl, s % 2), 0, 256)
                value = (ref[:, pl.ds(at, 256)].astype(jnp.float32) * scale).astype(jnp.bfloat16)
                out_ref[4 * (2 * (s - 1) + xh // 2) + place, :, 256 * (xh % 2) : 256 * (xh % 2 + 1)] = value


def rows_kernel(rows_ref, out_ref, k_ref):
    for half in range(2):
        for b in range(4):
            into = slice(128 * b, 128 * (b + 1))
            cols = slice(512 * half + 128 * b, 512 * half + 128 * (b + 1))
            most = jnp.max(jnp.abs(rows_ref[:, :, cols].astype(jnp.float32)), axis=0)
            scale, k = scales_of(most)
            k_ref[half, :, into] = jnp.broadcast_to(k, (8, 128)).astype(jnp.bfloat16)
            value = rows_ref[:, :, cols].astype(jnp.float32) * scale[None]
            out_ref[16 * half : 16 * (half + 1), :, into] = value.astype(jnp.bfloat16)


def scaled(kernel, blocks, ks, *rows):
    return pl.pallas_call(
        kernel,
        out_shape=(jax.ShapeDtypeStruct((blocks, 8, 512), jnp.bfloat16), jax.ShapeDtypeStruct((ks, 8, 512), jnp.bfloat16)),
        in_specs=[pl.BlockSpec(memory_space=pltpu.VMEM)] * len(rows),
        out_specs=(pl.BlockSpec(memory_space=pltpu.VMEM),) * 2,
        cost_estimate=pl.CostEstimate(flops=1_000_000, bytes_accessed=600_000, transcendentals=0),
        compiler_params=pltpu.CompilerParams(vmem_limit_bytes=4 << 20),
    )(*rows)


def hidden_kernel(gate_ref, up_ref, out_ref, gate_in, up_in, done, in_sem, out_sem):
    h = gate_ref.shape[0]
    part = h // 4 // 16 * 16
    bands = [pl.ds(n * part, part if n < 3 else h - 3 * part) for n in range(4)]
    loads = []
    for n, band in enumerate(bands):
        for i, (ref, into) in enumerate(((gate_ref, gate_in), (up_ref, up_in))):
            loads.append(pltpu.make_async_copy(ref.at[band, :], into.at[band, :], in_sem.at[n, i]))
            loads[-1].start()
    copies = []
    for n, band in enumerate(bands):
        loads[2 * n].wait()
        loads[2 * n + 1].wait()
        gate = gate_in[band, :].astype(jnp.float32)
        sig = jax.nn.sigmoid(gate)
        done[band, :] = ((gate * sig) * up_in[band, :].astype(jnp.float32)).astype(jnp.bfloat16)
        for i in range(4):
            copies.append(pltpu.make_async_copy(done.at[band, :], out_ref.at[i, band, :], out_sem.at[n, i]))
            copies[-1].start()
    for copy in copies:
        copy.wait()


def hidden_copies(gate, up):
    h, t = gate.shape
    return pl.pallas_call(
        hidden_kernel,
        out_shape=jax.ShapeDtypeStruct((4, h, t), jnp.bfloat16),
        in_specs=[pl.BlockSpec(memory_space=pltpu.HBM)] * 2,
        out_specs=pl.BlockSpec(memory_space=pl.ANY),
        scratch_shapes=[pltpu.VMEM((h, t), jnp.bfloat16)] * 3 + [pltpu.SemaphoreType.DMA((4, 2)), pltpu.SemaphoreType.DMA((4, 4))],
        cost_estimate=pl.CostEstimate(flops=2_000_000, bytes_accessed=6 * h * t * 2, transcendentals=h * t),
        compiler_params=pltpu.CompilerParams(vmem_limit_bytes=60 * 1024 * 1024),
        name="hidden_copies",
    )(gate, up)


def split_kernel(g_ref, out_ref, held, sem):
    c = lax.axis_index("c")
    for n in range(4):
        for i, core in enumerate((1 - c, c)):
            for xh in range(4):
                piece = g_ref[:, pl.ds(columns(n // 2, xh, n % 2, core, 128), 128)]
                for zl in range(4):
                    held[4 * n + zl, :, 512 * i + 128 * xh : 512 * i + 128 * (xh + 1)] = piece
    copy = pltpu.make_async_copy(held, out_ref, sem)
    copy.start()
    copy.wait()


def split_rows(g):
    return pl.pallas_call(
        split_kernel,
        out_shape=jax.ShapeDtypeStruct((16, 8, 1024), jnp.bfloat16),
        in_specs=[pl.BlockSpec(memory_space=pltpu.VMEM)],
        out_specs=pl.BlockSpec(memory_space=pl.ANY),
        scratch_shapes=[pltpu.VMEM((16, 8, 1024), jnp.bfloat16), pltpu.SemaphoreType.DMA],
        compiler_params=pltpu.CompilerParams(vmem_limit_bytes=2 << 20),
        name="split_rows",
    )(g)


def weights_kernel(hidden_ref, first_ref, second_ref, theirs_ref, ours_ref, held, total, sem):
    n, _, t = hidden_ref.shape
    loads = [pltpu.make_async_copy(hidden_ref.at[i], held.at[:, t * i : t * (i + 1)], sem.at[i]) for i in range(n)]
    for load in loads:
        load.start()
    for i in range(0, n, 2):
        loads[i].wait()
        loads[i + 1].wait()
        cols = slice(t * i, t * (i + 2))
        for half, (rows, ref) in enumerate(((first_ref, total), (second_ref, ours_ref))):
            part = jnp.dot(held[:, cols], rows[cols, :], preferred_element_type=jnp.float32)
            if half == 0 and i == n - 2:
                theirs_ref[...] = (total[...] + part).astype(jnp.bfloat16)
            else:
                ref[...] = part if i == 0 else ref[...] + part


def weight_parts(hiddens, first, second):
    n, h, t = hiddens.shape
    return pl.pallas_call(
        weights_kernel,
        out_shape=(jax.ShapeDtypeStruct((h, 512), jnp.bfloat16), jax.ShapeDtypeStruct((h, 512), jnp.float32)),
        in_specs=[pl.BlockSpec(memory_space=pltpu.HBM)] + [pl.BlockSpec(memory_space=pltpu.VMEM)] * 2,
        out_specs=(pl.BlockSpec(memory_space=pltpu.VMEM),) * 2,
        scratch_shapes=[pltpu.VMEM((h, n * t), jnp.bfloat16), pltpu.VMEM((h, 512), jnp.float32), pltpu.SemaphoreType.DMA((n,))],
        cost_estimate=pl.CostEstimate(flops=2 * n * t * h * 1024, bytes_accessed=4_000_000, transcendentals=0),
        compiler_params=pltpu.CompilerParams(vmem_limit_bytes=12 << 20),
        name="weight_parts",
    )(hiddens, first, second)


def merge_kernel(ours_ref, swap_ref, out_ref):
    other = 1 - lax.axis_index("c")
    for xh in range(4):
        cols = slice(128 * xh, 128 * (xh + 1))
        out_ref[xh] = (ours_ref[:, cols] + swap_ref[other, :, cols].astype(jnp.float32)).astype(jnp.bfloat16)


def merged(ours, swap):
    h = ours.shape[0]
    return pl.pallas_call(
        merge_kernel,
        out_shape=jax.ShapeDtypeStruct((4, h, 128), jnp.bfloat16),
        in_specs=[pl.BlockSpec(memory_space=pltpu.VMEM)] * 2,
        out_specs=pl.BlockSpec(memory_space=pltpu.VMEM),
        cost_estimate=pl.CostEstimate(flops=h * 512, bytes_accessed=h * 512 * 10, transcendentals=0),
        compiler_params=pltpu.CompilerParams(vmem_limit_bytes=4 << 20),
        name="merged",
    )(ours, swap)


def inputs_kernel(front_ref, last_ref, first_ref, second_ref, weight_ref, gate_ref, up_ref, grad_gate_ref, grad_up_ref, weight, shared, gate_in, up_in, total, sem):
    zh, xl, c = lax.axis_index("zh"), lax.axis_index("xl"), lax.axis_index("c")
    t = gate_in.shape[1]
    loads = [[] for _ in range(8)]
    for s in (1, 2, 3):
        for xh in range(4):
            at = columns(lax.bitwise_xor(zh, s // 2), xh, lax.bitwise_xor(xl, s % 2), 0, 256)
            n = 2 * (s - 1) + xh // 2
            into = weight.at[n, :, 256 * (xh % 2) : 256 * (xh % 2 + 1)]
            loads[n].append(pltpu.make_async_copy(weight_ref.at[:, pl.ds(at, 256)], into, sem.at[4 * (s - 1) + xh]))
    for half, (core, rows) in enumerate(((1 - c, first_ref), (c, second_ref))):
        loads[6 + half].append(pltpu.make_async_copy(rows.at[pl.ds((2 * zh + xl) * t, t), :], shared.at[half], sem.at[12 + half]))
        for xh in range(4):
            into = weight.at[6 + half, :, 128 * xh : 128 * (xh + 1)]
            copy = pltpu.make_async_copy(weight_ref.at[:, pl.ds(columns(zh, xh, xl, core, 128), 128)], into, sem.at[14 + 4 * half + xh])
            loads[6 + half].append(copy)
    ends = [pltpu.make_async_copy(gate_ref, gate_in, sem.at[22]), pltpu.make_async_copy(up_ref, up_in, sem.at[23])]
    for copy in [copy for group in loads for copy in group] + ends:
        copy.start()
    for n in range(8):
        for copy in loads[n]:
            copy.wait()
        rows = front_ref[n] if n < 5 else last_ref[0] if n == 5 else shared[n - 6]
        part = lax.dot_general(weight[n], rows, (((1,), (1,)), ((), ())), preferred_element_type=jnp.float32)
        total[...] = part if n == 0 else total[...] + part
    for copy in ends:
        copy.wait()
    grad_hidden = total[...]
    gate = gate_in[...].astype(jnp.float32)
    upper = up_in[...].astype(jnp.float32)
    sig = jax.nn.sigmoid(gate)
    grad_up_ref[...] = (grad_hidden * (gate * sig)).astype(jnp.bfloat16)
    grad_gate_ref[...] = (grad_hidden * upper * sig * (1.0 + gate * (1.0 - sig))).astype(jnp.bfloat16)


def input_grads(front, last, first, second, weight, gate, up):
    h, t = gate.shape
    return pl.pallas_call(
        inputs_kernel,
        out_shape=(jax.ShapeDtypeStruct((h, t), jnp.bfloat16),) * 2,
        in_specs=[pl.BlockSpec(memory_space=pltpu.VMEM)] * 2 + [pl.BlockSpec(memory_space=pl.ANY)] * 2 + [pl.BlockSpec(memory_space=pltpu.HBM)] * 3,
        out_specs=(pl.BlockSpec(memory_space=pltpu.VMEM),) * 2,
        scratch_shapes=[
            pltpu.VMEM((8, h, 512), jnp.bfloat16),
            pltpu.VMEM((2, t, 512), jnp.bfloat16),
            pltpu.VMEM((h, t), jnp.bfloat16),
            pltpu.VMEM((h, t), jnp.bfloat16),
            pltpu.VMEM((h, t), jnp.float32),
            pltpu.SemaphoreType.DMA((24,)),
        ],
        cost_estimate=pl.CostEstimate(flops=2 * h * t * 4096, bytes_accessed=6_000_000, transcendentals=h * t),
        compiler_params=pltpu.CompilerParams(vmem_limit_bytes=50 << 20),
        name="input_grads",
    )(front, last, first, second, weight, gate, up)


def turned(x, axis, by):
    return lax.ppermute(x, axis, [(i, i ^ by) for i in range(lax.axis_size(axis))])


def sections(grad_out, gate_pre, up_pre, down_weight):
    gate_t, up_t = gate_pre.T, up_pre.T
    _, t = gate_t.shape

    pieces = split_rows(grad_out)
    mine = lax.all_to_all(pieces, NEAR + ("zl",), 0, 0)
    turns = [grad_out]
    for s in (1, 2, 3):
        turns.append(turned(grad_out, "zl", s))
    copies = hidden_copies(gate_t, up_t)
    hiddens = lax.all_to_all(copies, NEAR, 0, 0)

    own, own_k = scaled(own_kernel, 24, 1, *turns)
    rows, rows_k = scaled(rows_kernel, 32, 2, mine)
    message = jnp.concatenate([own, rows, own_k, rows_k], 0).astype(jnp.float16)
    got = lax.all_gather(message, "y", axis=1, tiled=True)

    scale = power(got[56:].astype(jnp.float32), -1)
    first = (got[24:40].astype(jnp.float32) * scale[1]).astype(jnp.bfloat16).reshape(4 * t, 512)
    second = (got[40:56].astype(jnp.float32) * scale[2]).astype(jnp.bfloat16).reshape(4 * t, 512)
    front = (got[:20].astype(jnp.float32) * scale[0]).astype(jnp.bfloat16).reshape(5, t, 512)
    last = (got[20:24].astype(jnp.float32) * scale[0]).astype(jnp.bfloat16).reshape(1, t, 512)

    theirs, ours = weight_parts(hiddens, first, second)
    swap = lax.all_gather(theirs, "c", axis=0)
    part = merged(ours, swap)
    terms = lax.all_to_all(part, "xh", 0, 0)
    grad_gate, grad_up = input_grads(front, last, first, second, down_weight.T, gate_t, up_t)
    return terms.astype(jnp.float32).sum(0).T, grad_gate.T, grad_up.T


def solution(mesh):
    dims = (2, 4, 2, 2, 4, 8)
    fine = Mesh(mesh.devices.reshape(dims), AXES)
    dp, tensor = ("zh", "xh", "xl", "c"), ("zl", "y")
    in_specs = (P(dp + tensor, None), P(dp, tensor), P(dp, tensor), P(None, tensor))
    out_specs = (P(dp, tensor), P(dp, tensor), P(dp, tensor))
    return jax.shard_map(sections, mesh=fine, in_specs=in_specs, out_specs=out_specs, check_vma=False)
```

time: 125 us -> 115 us (0.920)
  the two profiles are of different devices: /device:TPU:1 before, /device:TPU:2 now
where the time goes in v5:
time: 115 us
  blocking collectives  44.5 us (39%)
  starting transfers between devices  39.8 us (35%)
  Pallas kernels  11.7 us (10%)
  waiting for transfers between devices  9.24 us (8%)
  other arithmetic  5.51 us (5%)
  local copies, waits for them, and re-layouts  3.15 us (3%)
    all_gather x1, blocking collectives, sections(): got = lax.all_gather(message, 'y', axis=1, tiled=True)  42 us
    all_to_all x1, starting transfers between devices, sections(): mine = lax.all_to_all(pieces, NEAR + ('zl',), 0, 0)  18.2 us
    ppermute x3, starting transfers between devices, turned(): lax.ppermute(x, axis, [(i, i ^ by) for i in range(lax.axis_size(axis))])  10.1 us
    pallas_call x1, Pallas kernels, input_grads(): pl.pallas_call(inputs_kernel, out_shape=(jax.ShapeDtypeStruct((h, t), jnp...  6.27 us
    all_to_all x1, starting transfers between devices, sections(): terms = lax.all_to_all(part, 'xh', 0, 0)  5.99 us
    all_to_all x1, waiting for transfers between devices, sections(): terms = lax.all_to_all(part, 'xh', 0, 0)  5.58 us
    all_to_all x1, starting transfers between devices, sections(): hiddens = lax.all_to_all(copies, NEAR, 0, 0)  5.52 us
    ppermute x3, waiting for transfers between devices, turned(): lax.ppermute(x, axis, [(i, i ^ by) for i in range(lax.axis_size(axis))])  3.65 us
  transfers between devices with their start and end apart: 6, of which 3 were waited for; matrix products, arithmetic and copies ran while one was open for 4% of the time, Pallas kernels for 8%

profile of v5, /device:TPU:2, one launch (start us, length us, event | category | flops | bytes accessed | tf_op | source)
XLA Modules:
  0.0 114.7 jit_solution(11447315501070571224)
XLA Ops:
  0.6 0.0 copy-start.2
  0.6 0.8 copy-done.2
  1.5 0.7 split_rows.1
  2.2 18.2 %all-to-all-start.1 = ((bf16[16,8,1024]{2,1,0:T(8,128)(2,1)}), bf16[16,8,1024]{2,1,0:T(8,128)(2,1)S(1)}, u32[]{:S(2)}, u32[]{:S(2)}) async-start(bf16[16,8,1024]{2,1,0:T(8,128)(2,1)} %split_rows.1), calls=%async_computation.1 | async-start | bytes 524288 | tf_op jit(solution)/shard_map/all_to_all | solution.py:261
  20.4 3.4 %collective-permute-start = (bf16[8,4096]{1,0:T(8,128)(2,1)}, bf16[8,4096]{1,0:T(8,128)(2,1)S(1)}, u32[]{:S(2)}, u32[]{:S(2)}) collective-permute-start(bf16[8,4096]{1,0:T(8,128)(2,1)} %g_ref.1), channel_id=1, source_target_pairs={{0,8},{8,0},{16,24},{24,16},{1,9},{9,1},{17,25},{25,17},{2,10},{10... | collective-permute-start | bytes 196616 | tf_op jit(solution)/shard_map/ppermute | solution.py:253
  23.8 4.3 %collective-permute-start.1 = (bf16[8,4096]{1,0:T(8,128)(2,1)}, bf16[8,4096]{1,0:T(8,128)(2,1)S(1)}, u32[]{:S(2)}, u32[]{:S(2)}) collective-permute-start(bf16[8,4096]{1,0:T(8,128)(2,1)} %g_ref.1), channel_id=1, source_target_pairs={{0,16},{8,24},{16,0},{24,8},{1,17},{9,25},{17,1},{25,9},{2,18},{10... | collective-permute-start | bytes 196616 | tf_op jit(solution)/shard_map/ppermute | solution.py:253
  28.0 2.5 %collective-permute-start.2 = (bf16[8,4096]{1,0:T(8,128)(2,1)}, bf16[8,4096]{1,0:T(8,128)(2,1)S(1)}, u32[]{:S(2)}, u32[]{:S(2)}) collective-permute-start(bf16[8,4096]{1,0:T(8,128)(2,1)} %g_ref.1), channel_id=1, source_target_pairs={{0,24},{8,16},{16,8},{24,0},{1,25},{9,17},{17,9},{25,1},{2,26},{10... | collective-permute-start | bytes 196616 | tf_op jit(solution)/shard_map/ppermute | solution.py:253
  30.5 2.0 %hidden_copies.1 = bf16[4,464,256]{2,1,0:T(8,128)(2,1)} custom-call(bf16[464,256]{1,0:T(8,128)(2,1)} %bitcast.23, bf16[464,256]{1,0:T(8,128)(2,1)} %bitcast.25), custom_call_target="tpu_custom_call" | custom-call | flops 2000000 | bytes 1425408 | tf_op jit(solution)/shard_map/hidden_copies/pallas_call | solution.py:108
  32.6 0.0 collective-permute-done.b_ref
  32.6 0.1 collective-permute-done.1.c_ref
  32.6 3.6 %collective-permute-done.2.d_ref = bf16[8,4096]{1,0:T(8,128)(2,1)S(1)} collective-permute-done((bf16[8,4096]{1,0:T(8,128)(2,1)}, bf16[8,4096]{1,0:T(8,128)(2,1)S(1)}, u32[]{:S(2)}, u32[]{:S(2)}) %collective-permute-start.2) | collective-permute-done | bytes 65568 | tf_op jit(solution)/shard_map/ppermute | solution.py:253
  36.2 0.0 copy-start.3
  36.2 0.8 copy-done.3
  37.1 0.2 shard_map.67
  37.2 0.0 all-to-all-done.1.rows_ref
  37.2 5.5 %all-to-all-start = ((bf16[4,464,256]{2,1,0:T(8,128)(2,1)}), bf16[4,464,256]{2,1,0:T(8,128)(2,1)S(1)}, u32[]{:S(2)}, u32[]{:S(2)}) async-start(bf16[4,464,256]{2,1,0:T(8,128)(2,1)} %hidden_copies.1), calls=%async_computation | async-start | bytes 1900544 | tf_op jit(solution)/shard_map/all_to_all | solution.py:266
  42.8 0.2 shard_map.68
  43.0 0.1 maximum_convert_fusion
  43.1 42.0 %all-gather.2 = f16[59,64,512]{2,1,0:T(8,128)(2,1)S(1)} all-gather(f16[59,8,512]{2,1,0:T(8,128)(2,1)S(1)} %maximum_convert_fusion), channel_id=1, replica_groups=mesh['zh'=2,'xh'=4,'xl'=2,'c'=2,'zl'=4,'y'=8] {'y'}, dimensions={1}, use_global_device_ids=true | all-gather | bytes 4349952 | tf_op jit(solution)/shard_map/all_gather | solution.py:271
  85.2 0.0 copy-start.4
  85.2 0.4 multiply_select_fusion
  85.6 1.4 %copy-done.4 = f16[59,64,512]{2,1,0:T(8,128)(2,1)} copy-done((f16[59,64,512]{2,1,0:T(8,128)(2,1)}, f16[59,64,512]{2,1,0:T(8,128)(2,1)S(1)}, u32[]{:S(2)}) %copy-start.4) | copy-done | bytes 3866648
  87.0 0.6 multiply_convert_fusion.1
  87.6 0.0 all-to-all-done.hidden_ref
  87.6 1.4 %weight_parts.1 = (bf16[464,512]{1,0:T(8,128)(2,1)S(1)}, f32[464,512]{1,0:T(8,128)S(1)}) custom-call(bf16[4,464,256]{2,1,0:T(8,128)(2,1)S(1)} %all-to-all-done.hidden_ref, bf16[1024,512]{1,0:T(8,128)(2,1)S(1)} %bitcast.19, bf16[1024,512]{1,0:T(8,128)(2,1)S(1)} %bitcast.17), custom_call_target="tpu_custom_call" | custom-call | flops 973078528 | bytes 4000000 | tf_op jit(solution)/shard_map/weight_parts/pallas_call | solution.py:164
  89.0 2.5 %all-gather = bf16[928,512]{1,0:T(8,128)(2,1)S(1)} all-gather(bf16[464,512]{1,0:T(8,128)(2,1)S(1)} %get-tuple-element.16), channel_id=2, replica_groups=mesh['zh'=2,'xh'=4,'xl'=2,'c'=2,'zl'=4,'y'=8] {'c'}, dimensions={0}, use_global_device_ids=true | all-gather | bytes 1425408 | tf_op jit(solution)/shard_map/all_gather | solution.py:280
  91.5 0.9 merged.1
  92.4 0.0 copy-start
  92.5 0.0 copy-start.1
  92.5 6.0 %all-to-all-start.2 = ((bf16[4,464,128]{2,1,0:T(8,128)(2,1)}), bf16[4,464,128]{2,1,0:T(8,128)(2,1)S(1)}, u32[]{:S(2)}, u32[]{:S(2)}) async-start(bf16[4,464,128]{2,1,0:T(8,128)(2,1)} %merged.1), calls=%async_computation.2 | async-start | bytes 950272 | tf_op jit(solution)/shard_map/all_to_all | solution.py:282
  98.4 1.0 multiply_convert_fusion.3
  99.4 2.7 %multiply_convert_fusion = bf16[20,64,512]{2,1,0:T(8,128)(2,1)} fusion(f16[59,64,512]{2,1,0:T(8,128)(2,1)} %copy-done.4, f32[64,512]{1,0:T(8,128)S(1)} %get-tuple-element.21), kind=kLoop, calls=%fused_computation | loop fusion | flops 1966080 | bytes 2752512 | tf_op jit(solution)/shard_map/convert_element_type | solution.py:276
  102.1 0.0 copy-done
  102.1 0.0 copy-done.1
  102.1 6.3 %input_grads.1 = (bf16[464,256]{1,0:T(8,128)(2,1)}, bf16[464,256]{1,0:T(8,128)(2,1)}) custom-call(bf16[5,256,512]{2,1,0:T(8,128)(2,1)} %bitcast.27, bf16[1,256,512]{2,1,0:T(8,128)(2,1)S(1)} %bitcast.22, bf16[1024,512]{1,0:T(8,128)(2,1)S(1)} %bitcast.20, bf16[1024,512]{1,0:T(8,128)(2,1)S(1)} %bitcast.18, bf16[464,4096]{1,0:T(8,128)(2,1)} %bitcast.28, ...), custom_call_target="tpu_custom_call" | custom-call | flops 973078528 | bytes 6000000 | tf_op jit(solution)/shard_map/input_grads/pallas_call | solution.py:233
  108.4 5.6 %all-to-all-done.2 = bf16[4,464,128]{2,1,0:T(8,128)(2,1)S(1)} async-done(((bf16[4,464,128]{2,1,0:T(8,128)(2,1)}), bf16[4,464,128]{2,1,0:T(8,128)(2,1)S(1)}, u32[]{:S(2)}, u32[]{:S(2)}) %all-to-all-start.2) | async-done | bytes 475168 | tf_op jit(solution)/shard_map/all_to_all | solution.py:282
  114.0 0.7 convert_reduce_fusion
  (1 shorter events, 0.0 us)
Async XLA Ops:
  0.6 0.8 copy-start.2
  2.2 35.0 %all-to-all-start.1 = ((bf16[16,8,1024]{2,1,0:T(8,128)(2,1)}), bf16[16,8,1024]{2,1,0:T(8,128)(2,1)S(1)}, u32[]{:S(2)}, u32[]{:S(2)}) async-start(bf16[16,8,1024]{2,1,0:T(8,128)(2,1)} %split_rows.1), calls=%async_computation.1 | async-start | bytes 524288 | tf_op jit(solution)/shard_map/all_to_all | solution.py:261
  20.4 12.2 %collective-permute-start = (bf16[8,4096]{1,0:T(8,128)(2,1)}, bf16[8,4096]{1,0:T(8,128)(2,1)S(1)}, u32[]{:S(2)}, u32[]{:S(2)}) collective-permute-start(bf16[8,4096]{1,0:T(8,128)(2,1)} %g_ref.1), channel_id=1, source_target_pairs={{0,8},{8,0},{16,24},{24,16},{1,9},{9,1},{17,25},{25,17},{2,10},{10... | collective-permute-start | bytes 196616 | tf_op jit(solution)/shard_map/ppermute | solution.py:253
  23.8 8.9 %collective-permute-start.1 = (bf16[8,4096]{1,0:T(8,128)(2,1)}, bf16[8,4096]{1,0:T(8,128)(2,1)S(1)}, u32[]{:S(2)}, u32[]{:S(2)}) collective-permute-start(bf16[8,4096]{1,0:T(8,128)(2,1)} %g_ref.1), channel_id=1, source_target_pairs={{0,16},{8,24},{16,0},{24,8},{1,17},{9,25},{17,1},{25,9},{2,18},{10... | collective-permute-start | bytes 196616 | tf_op jit(solution)/shard_map/ppermute | solution.py:253
  28.0 8.2 %collective-permute-start.2 = (bf16[8,4096]{1,0:T(8,128)(2,1)}, bf16[8,4096]{1,0:T(8,128)(2,1)S(1)}, u32[]{:S(2)}, u32[]{:S(2)}) collective-permute-start(bf16[8,4096]{1,0:T(8,128)(2,1)} %g_ref.1), channel_id=1, source_target_pairs={{0,24},{8,16},{16,8},{24,0},{1,25},{9,17},{17,9},{25,1},{2,26},{10... | collective-permute-start | bytes 196616 | tf_op jit(solution)/shard_map/ppermute | solution.py:253
  36.2 0.8 copy-start.3
  37.2 50.4 %all-to-all-start = ((bf16[4,464,256]{2,1,0:T(8,128)(2,1)}), bf16[4,464,256]{2,1,0:T(8,128)(2,1)S(1)}, u32[]{:S(2)}, u32[]{:S(2)}) async-start(bf16[4,464,256]{2,1,0:T(8,128)(2,1)} %hidden_copies.1), calls=%async_computation | async-start | bytes 1900544 | tf_op jit(solution)/shard_map/all_to_all | solution.py:266
  85.2 1.8 %copy-start.4 = (f16[59,64,512]{2,1,0:T(8,128)(2,1)}, f16[59,64,512]{2,1,0:T(8,128)(2,1)S(1)}, u32[]{:S(2)}) copy-start(f16[59,64,512]{2,1,0:T(8,128)(2,1)S(1)} %all-gather.2) | copy-start | bytes 11599876
  92.4 9.7 %copy-start = (bf16[256,464]{0,1:T(8,128)(2,1)S(1)}, bf16[256,464]{0,1:T(8,128)(2,1)}, u32[]{:S(2)}) copy-start(bf16[256,464]{0,1:T(8,128)(2,1)} %param.5) | copy-start | bytes 712708
  92.5 9.7 %copy-start.1 = (bf16[256,464]{0,1:T(8,128)(2,1)S(1)}, bf16[256,464]{0,1:T(8,128)(2,1)}, u32[]{:S(2)}) copy-start(bf16[256,464]{0,1:T(8,128)(2,1)} %param.6) | copy-start | bytes 712708
  92.5 21.5 %all-to-all-start.2 = ((bf16[4,464,128]{2,1,0:T(8,128)(2,1)}), bf16[4,464,128]{2,1,0:T(8,128)(2,1)S(1)}, u32[]{:S(2)}, u32[]{:S(2)}) async-start(bf16[4,464,128]{2,1,0:T(8,128)(2,1)} %merged.1), calls=%async_computation.2 | async-start | bytes 950272 | tf_op jit(solution)/shard_map/all_to_all | solution.py:282

commit v6 on v5

--- a/solution.py
+++ b/solution.py
@@ -173,56 +173,51 @@
     )(hiddens, first, second)
 
 
-def merge_kernel(ours_ref, swap_ref, out_ref):
-    other = 1 - lax.axis_index("c")
-    for xh in range(4):
-        cols = slice(128 * xh, 128 * (xh + 1))
-        out_ref[xh] = (ours_ref[:, cols] + swap_ref[other, :, cols].astype(jnp.float32)).astype(jnp.bfloat16)
+def merge_kernel(ours_ref, swap_ref, here_ref, *away_refs):
+    other, xh = 1 - lax.axis_index("c"), lax.axis_index("xh")
+    for s in range(4):
+        cols = pl.ds(pl.multiple_of(128 * lax.bitwise_xor(xh, s), 128), 128)
+        value = ours_ref[:, cols] + swap_ref[other, :, cols].astype(jnp.float32)
+        if s == 0:
+            here_ref[...] = value
+        else:
+            away_refs[s - 1][...] = value.astype(jnp.bfloat16)
 
 
 def merged(ours, swap):
     h = ours.shape[0]
     return pl.pallas_call(
         merge_kernel,
-        out_shape=jax.ShapeDtypeStruct((4, h, 128), jnp.bfloat16),
+        out_shape=(jax.ShapeDtypeStruct((h, 128), jnp.float32),) + (jax.ShapeDtypeStruct((h, 128), jnp.bfloat16),) * 3,
         in_specs=[pl.BlockSpec(memory_space=pltpu.VMEM)] * 2,
-        out_specs=pl.BlockSpec(memory_space=pltpu.VMEM),
+        out_specs=(pl.BlockSpec(memory_space=pltpu.VMEM),) * 4,
         cost_estimate=pl.CostEstimate(flops=h * 512, bytes_accessed=h * 512 * 10, transcendentals=0),
         compiler_params=pltpu.CompilerParams(vmem_limit_bytes=4 << 20),
         name="merged",
     )(ours, swap)
 
 
-def inputs_kernel(front_ref, last_ref, first_ref, second_ref, weight_ref, gate_ref, up_ref, grad_gate_ref, grad_up_ref, weight, shared, gate_in, up_in, total, sem):
+def inputs_kernel(front_ref, last_ref, first_ref, second_ref, weight_ref, gate_ref, up_ref, grad_gate_ref, grad_up_ref, weight, total):
     zh, xl, c = lax.axis_index("zh"), lax.axis_index("xl"), lax.axis_index("c")
-    t = gate_in.shape[1]
-    loads = [[] for _ in range(8)]
-    for s in (1, 2, 3):
-        for xh in range(4):
-            at = columns(lax.bitwise_xor(zh, s // 2), xh, lax.bitwise_xor(xl, s % 2), 0, 256)
-            n = 2 * (s - 1) + xh // 2
-            into = weight.at[n, :, 256 * (xh % 2) : 256 * (xh % 2 + 1)]
-            loads[n].append(pltpu.make_async_copy(weight_ref.at[:, pl.ds(at, 256)], into, sem.at[4 * (s - 1) + xh]))
-    for half, (core, rows) in enumerate(((1 - c, first_ref), (c, second_ref))):
-        loads[6 + half].append(pltpu.make_async_copy(rows.at[pl.ds((2 * zh + xl) * t, t), :], shared.at[half], sem.at[12 + half]))
-        for xh in range(4):
-            into = weight.at[6 + half, :, 128 * xh : 128 * (xh + 1)]
-            copy = pltpu.make_async_copy(weight_ref.at[:, pl.ds(columns(zh, xh, xl, core, 128), 128)], into, sem.at[14 + 4 * half + xh])
-            loads[6 + half].append(copy)
-    ends = [pltpu.make_async_copy(gate_ref, gate_in, sem.at[22]), pltpu.make_async_copy(up_ref, up_in, sem.at[23])]
-    for copy in [copy for group in loads for copy in group] + ends:
-        copy.start()
+    t = gate_ref.shape[1]
+    shared = pl.ds(pl.multiple_of((2 * zh + xl) * t, t), t)
     for n in range(8):
-        for copy in loads[n]:
-            copy.wait()
-        rows = front_ref[n] if n < 5 else last_ref[0] if n == 5 else shared[n - 6]
-        part = lax.dot_general(weight[n], rows, (((1,), (1,)), ((), ())), preferred_element_type=jnp.float32)
+        slot = n % 2
+        if n < 6:
+            for i in range(2):
+                at = columns(lax.bitwise_xor(zh, (n // 2 + 1) // 2), 2 * (n % 2) + i, lax.bitwise_xor(xl, (n // 2 + 1) % 2), 0, 256)
+                weight[slot, :, 256 * i : 256 * (i + 1)] = weight_ref[:, pl.ds(at, 256)]
+            rows = front_ref[n] if n < 5 else last_ref[0]
+        else:
+            core = 1 - c if n == 6 else c
+            for xh in range(4):
+                weight[slot, :, 128 * xh : 128 * (xh + 1)] = weight_ref[:, pl.ds(columns(zh, xh, xl, core, 128), 128)]
+            rows = first_ref[shared, :] if n == 6 else second_ref[shared, :]
+        part = lax.dot_general(weight[slot], rows, (((1,), (1,)), ((), ())), preferred_element_type=jnp.float32)
         total[...] = part if n == 0 else total[...] + part
-    for copy in ends:
-        copy.wait()
     grad_hidden = total[...]
-    gate = gate_in[...].astype(jnp.float32)
-    upper = up_in[...].astype(jnp.float32)
+    gate = gate_ref[...].astype(jnp.float32)
+    upper = up_ref[...].astype(jnp.float32)
     sig = jax.nn.sigmoid(gate)
     grad_up_ref[...] = (grad_hidden * (gate * sig)).astype(jnp.bfloat16)
     grad_gate_ref[...] = (grad_hidden * upper * sig * (1.0 + gate * (1.0 - sig))).astype(jnp.bfloat16)
@@ -233,18 +228,11 @@
     return pl.pallas_call(
         inputs_kernel,
         out_shape=(jax.ShapeDtypeStruct((h, t), jnp.bfloat16),) * 2,
-        in_specs=[pl.BlockSpec(memory_space=pltpu.VMEM)] * 2 + [pl.BlockSpec(memory_space=pl.ANY)] * 2 + [pl.BlockSpec(memory_space=pltpu.HBM)] * 3,
+        in_specs=[pl.BlockSpec(memory_space=pltpu.VMEM)] * 7,
         out_specs=(pl.BlockSpec(memory_space=pltpu.VMEM),) * 2,
-        scratch_shapes=[
-            pltpu.VMEM((8, h, 512), jnp.bfloat16),
-            pltpu.VMEM((2, t, 512), jnp.bfloat16),
-            pltpu.VMEM((h, t), jnp.bfloat16),
-            pltpu.VMEM((h, t), jnp.bfloat16),
-            pltpu.VMEM((h, t), jnp.float32),
-            pltpu.SemaphoreType.DMA((24,)),
-        ],
+        scratch_shapes=[pltpu.VMEM((2, h, 512), jnp.bfloat16), pltpu.VMEM((h, t), jnp.float32)],
         cost_estimate=pl.CostEstimate(flops=2 * h * t * 4096, bytes_accessed=6_000_000, transcendentals=h * t),
-        compiler_params=pltpu.CompilerParams(vmem_limit_bytes=50 << 20),
+        compiler_params=pltpu.CompilerParams(vmem_limit_bytes=16 << 20),
         name="input_grads",
     )(front, last, first, second, weight, gate, up)
 
@@ -278,10 +266,11 @@
 
     theirs, ours = weight_parts(hiddens, first, second)
     swap = lax.all_gather(theirs, "c", axis=0)
-    part = merged(ours, swap)
-    terms = lax.all_to_all(part, "xh", 0, 0)
+    here, *away = merged(ours, swap)
+    for s in (2, 1, 3):
+        here = here + turned(away[s - 1], "xh", s).astype(jnp.float32)
     grad_gate, grad_up = input_grads(front, last, first, second, down_weight.T, gate_t, up_t)
-    return terms.astype(jnp.float32).sum(0).T, grad_gate.T, grad_up.T
+    return here.T, grad_gate.T, grad_up.T
 
 
 def solution(mesh):

time: 115 us -> 114 us (level)
  the two profiles are of different devices: /device:TPU:2 before, /device:TPU:6 now
where the time goes in v6:
time: 114 us
  starting transfers between devices  46 us (40%)
  blocking collectives  44.7 us (39%)
  waiting for transfers between devices  8.35 us (7%)
  Pallas kernels  7.81 us (7%)
  other arithmetic  3.21 us (3%)
  local copies, waits for them, and re-layouts  2.8 us (2%)
    all_gather x1, blocking collectives, sections(): got = lax.all_gather(message, 'y', axis=1, tiled=True)  42 us
    ppermute x6, starting transfers between devices, turned(): lax.ppermute(x, axis, [(i, i ^ by) for i in range(lax.axis_size(axis))])  22.3 us
    all_to_all x1, starting transfers between devices, sections(): mine = lax.all_to_all(pieces, NEAR + ('zl',), 0, 0)  18.2 us
    ppermute x6, waiting for transfers between devices, turned(): lax.ppermute(x, axis, [(i, i ^ by) for i in range(lax.axis_size(axis))])  8.34 us
    all_to_all x1, starting transfers between devices, sections(): hiddens = lax.all_to_all(copies, NEAR, 0, 0)  5.52 us
    unnamed x12, local copies, waits for them, and re-layouts  2.77 us
    all_gather x1, blocking collectives, sections(): swap = lax.all_gather(theirs, 'c', axis=0)  2.62 us
    pallas_call x1, Pallas kernels, weight_parts(): pl.pallas_call(weights_kernel, out_shape=(jax.ShapeDtypeStruct((h, 512),...  2.35 us
  transfers between devices with their start and end apart: 8, of which 3 were waited for; matrix products, arithmetic and copies ran while one was open for 2% of the time, Pallas kernels for 4%

profile of v6, /device:TPU:6, one launch (start us, length us, event | category | flops | bytes accessed | tf_op | source)
XLA Modules:
  0.0 113.7 jit_solution(1662991607476731544)
XLA Ops:
  0.6 0.0 copy-start.3
  0.6 0.8 copy-done.3
  1.5 0.7 split_rows.1
  2.2 18.2 %all-to-all-start.1 = ((bf16[16,8,1024]{2,1,0:T(8,128)(2,1)}), bf16[16,8,1024]{2,1,0:T(8,128)(2,1)S(1)}, u32[]{:S(2)}, u32[]{:S(2)}) async-start(bf16[16,8,1024]{2,1,0:T(8,128)(2,1)} %split_rows.1), calls=%async_computation.1 | async-start | bytes 524288 | tf_op jit(solution)/shard_map/all_to_all | solution.py:249
  20.4 3.4 %collective-permute-start = (bf16[8,4096]{1,0:T(8,128)(2,1)}, bf16[8,4096]{1,0:T(8,128)(2,1)S(1)}, u32[]{:S(2)}, u32[]{:S(2)}) collective-permute-start(bf16[8,4096]{1,0:T(8,128)(2,1)} %g_ref.1), channel_id=1, source_target_pairs={{0,8},{8,0},{16,24},{24,16},{1,9},{9,1},{17,25},{25,17},{2,10},{10... | collective-permute-start | bytes 196616 | tf_op jit(solution)/shard_map/ppermute | solution.py:241
  23.8 4.3 %collective-permute-start.1 = (bf16[8,4096]{1,0:T(8,128)(2,1)}, bf16[8,4096]{1,0:T(8,128)(2,1)S(1)}, u32[]{:S(2)}, u32[]{:S(2)}) collective-permute-start(bf16[8,4096]{1,0:T(8,128)(2,1)} %g_ref.1), channel_id=1, source_target_pairs={{0,16},{8,24},{16,0},{24,8},{1,17},{9,25},{17,1},{25,9},{2,18},{10... | collective-permute-start | bytes 196616 | tf_op jit(solution)/shard_map/ppermute | solution.py:241
  28.0 2.5 %collective-permute-start.2 = (bf16[8,4096]{1,0:T(8,128)(2,1)}, bf16[8,4096]{1,0:T(8,128)(2,1)S(1)}, u32[]{:S(2)}, u32[]{:S(2)}) collective-permute-start(bf16[8,4096]{1,0:T(8,128)(2,1)} %g_ref.1), channel_id=1, source_target_pairs={{0,24},{8,16},{16,8},{24,0},{1,25},{9,17},{17,9},{25,1},{2,26},{10... | collective-permute-start | bytes 196616 | tf_op jit(solution)/shard_map/ppermute | solution.py:241
  30.5 2.0 %hidden_copies.1 = bf16[4,464,256]{2,1,0:T(8,128)(2,1)} custom-call(bf16[464,256]{1,0:T(8,128)(2,1)} %bitcast.26, bf16[464,256]{1,0:T(8,128)(2,1)} %bitcast.28), custom_call_target="tpu_custom_call" | custom-call | flops 2000000 | bytes 1425408 | tf_op jit(solution)/shard_map/hidden_copies/pallas_call | solution.py:108
  32.6 0.0 collective-permute-done.b_ref
  32.6 0.0 collective-permute-done.1.c_ref
  32.6 3.6 %collective-permute-done.2.d_ref = bf16[8,4096]{1,0:T(8,128)(2,1)S(1)} collective-permute-done((bf16[8,4096]{1,0:T(8,128)(2,1)}, bf16[8,4096]{1,0:T(8,128)(2,1)S(1)}, u32[]{:S(2)}, u32[]{:S(2)}) %collective-permute-start.2) | collective-permute-done | bytes 65568 | tf_op jit(solution)/shard_map/ppermute | solution.py:241
  36.2 0.0 copy-start.4
  36.2 0.8 copy-done.4
  37.1 0.2 shard_map.67
  37.2 0.0 all-to-all-done.1.rows_ref
  37.2 5.5 %all-to-all-start = ((bf16[4,464,256]{2,1,0:T(8,128)(2,1)}), bf16[4,464,256]{2,1,0:T(8,128)(2,1)}, u32[]{:S(2)}, u32[]{:S(2)}) async-start(bf16[4,464,256]{2,1,0:T(8,128)(2,1)} %hidden_copies.1), calls=%async_computation | async-start | bytes 1900544 | tf_op jit(solution)/shard_map/all_to_all | solution.py:254
  42.8 0.2 shard_map.68
  43.0 0.1 maximum_convert_fusion
  43.1 42.0 %all-gather.2 = f16[59,64,512]{2,1,0:T(8,128)(2,1)S(1)} all-gather(f16[59,8,512]{2,1,0:T(8,128)(2,1)S(1)} %maximum_convert_fusion), channel_id=1, replica_groups=mesh['zh'=2,'xh'=4,'xl'=2,'c'=2,'zl'=4,'y'=8] {'y'}, dimensions={1}, use_global_device_ids=true | all-gather | bytes 4349952 | tf_op jit(solution)/shard_map/all_gather | solution.py:259
  85.2 0.0 copy-start.5
  85.2 0.4 multiply_select_fusion
  85.6 0.4 multiply_convert_fusion
  85.9 1.1 copy-done.5
  87.0 0.6 multiply_convert_fusion.1
  87.6 0.0 all-to-all-done.hidden_ref
  87.6 0.0 copy-start.1
  87.6 0.0 copy-start.2
  87.7 2.3 %weight_parts.1 = (bf16[464,512]{1,0:T(8,128)(2,1)S(1)}, f32[464,512]{1,0:T(8,128)S(1)}) custom-call(bf16[4,464,256]{2,1,0:T(8,128)(2,1)} %all-to-all-done.hidden_ref, bf16[1024,512]{1,0:T(8,128)(2,1)S(1)} %bitcast.21, bf16[1024,512]{1,0:T(8,128)(2,1)S(1)} %bitcast.19), custom_call_target="tpu_custom_call" | custom-call | flops 973078528 | bytes 4000000 | tf_op jit(solution)/shard_map/weight_parts/pallas_call | solution.py:164
  90.0 0.0 copy-start
  90.0 2.6 %all-gather = bf16[928,512]{1,0:T(8,128)(2,1)S(1)} all-gather(bf16[464,512]{1,0:T(8,128)(2,1)S(1)} %get-tuple-element.20), channel_id=2, replica_groups=mesh['zh'=2,'xh'=4,'xl'=2,'c'=2,'zl'=4,'y'=8] {'c'}, dimensions={0}, use_global_device_ids=true | all-gather | bytes 1425408 | tf_op jit(solution)/shard_map/all_gather | solution.py:268
  92.6 0.2 merged.1
  92.8 4.7 %collective-permute-start.3 = (bf16[464,128]{1,0:T(8,128)(2,1)S(1)}, bf16[464,128]{1,0:T(8,128)(2,1)S(1)}, u32[]{:S(2)}, u32[]{:S(2)}) collective-permute-start(bf16[464,128]{1,0:T(8,128)(2,1)S(1)} %get-tuple-element.22), channel_id=1, source_target_pairs={{0,256},{128,384},{256,0},{384,128},{1,257},{129,385},{257,1},{385... | collective-permute-start | bytes 356360 | tf_op jit(solution)/shard_map/ppermute | solution.py:241
  97.5 4.2 %collective-permute-start.4 = (bf16[464,128]{1,0:T(8,128)(2,1)S(1)}, bf16[464,128]{1,0:T(8,128)(2,1)S(1)}, u32[]{:S(2)}, u32[]{:S(2)}) collective-permute-start(bf16[464,128]{1,0:T(8,128)(2,1)S(1)} %get-tuple-element.23), channel_id=1, source_target_pairs={{0,128},{128,0},{256,384},{384,256},{1,129},{129,1},{257,385},{385... | collective-permute-start | bytes 356360 | tf_op jit(solution)/shard_map/ppermute | solution.py:241
  101.8 3.3 %collective-permute-start.5 = (bf16[464,128]{1,0:T(8,128)(2,1)S(1)}, bf16[464,128]{1,0:T(8,128)(2,1)S(1)}, u32[]{:S(2)}, u32[]{:S(2)}) collective-permute-start(bf16[464,128]{1,0:T(8,128)(2,1)S(1)} %get-tuple-element.24), channel_id=1, source_target_pairs={{0,384},{128,256},{256,128},{384,0},{1,385},{129,257},{257,129},{3... | collective-permute-start | bytes 356360 | tf_op jit(solution)/shard_map/ppermute | solution.py:241
  105.1 1.0 multiply_convert_fusion.3
  106.1 0.0 copy-done.1
  106.1 0.0 copy-done.2
  106.1 0.0 copy-done
  106.1 2.1 %input_grads.1 = (bf16[464,256]{1,0:T(8,128)(2,1)}, bf16[464,256]{1,0:T(8,128)(2,1)}) custom-call(bf16[5,256,512]{2,1,0:T(8,128)(2,1)S(1)} %bitcast.18, bf16[1,256,512]{2,1,0:T(8,128)(2,1)S(1)} %bitcast.25, bf16[1024,512]{1,0:T(8,128)(2,1)S(1)} %bitcast.22, bf16[1024,512]{1,0:T(8,128)(2,1)S(1)} %bitcast.20, bf16[464,4096]{1,0:T(8,128)(2,1)S(1)} %bitcast.23, ...), custom_call_target="tpu_custom_call" | custom-call | flops 973078528 | bytes 6000000 | tf_op jit(solution)/shard_map/input_grads/pallas_call | solution.py:228
  108.2 0.0 collective-permute-done.3
  108.2 2.4 %collective-permute-done.4 = bf16[464,128]{1,0:T(8,128)(2,1)S(1)} collective-permute-done((bf16[464,128]{1,0:T(8,128)(2,1)S(1)}, bf16[464,128]{1,0:T(8,128)(2,1)S(1)}, u32[]{:S(2)}, u32[]{:S(2)}) %collective-permute-start.4) | collective-permute-done | bytes 118816 | tf_op jit(solution)/shard_map/ppermute | solution.py:241
  110.6 2.4 %collective-permute-done.5 = bf16[464,128]{1,0:T(8,128)(2,1)S(1)} collective-permute-done((bf16[464,128]{1,0:T(8,128)(2,1)S(1)}, bf16[464,128]{1,0:T(8,128)(2,1)S(1)}, u32[]{:S(2)}, u32[]{:S(2)}) %collective-permute-start.5) | collective-permute-done | bytes 118816 | tf_op jit(solution)/shard_map/ppermute | solution.py:241
  112.9 0.8 add_bitcast_fusion
  (1 shorter events, 0.0 us)
Async XLA Ops:
  0.6 0.8 copy-start.3
  2.2 35.0 %all-to-all-start.1 = ((bf16[16,8,1024]{2,1,0:T(8,128)(2,1)}), bf16[16,8,1024]{2,1,0:T(8,128)(2,1)S(1)}, u32[]{:S(2)}, u32[]{:S(2)}) async-start(bf16[16,8,1024]{2,1,0:T(8,128)(2,1)} %split_rows.1), calls=%async_computation.1 | async-start | bytes 524288 | tf_op jit(solution)/shard_map/all_to_all | solution.py:249
  20.4 12.2 %collective-permute-start = (bf16[8,4096]{1,0:T(8,128)(2,1)}, bf16[8,4096]{1,0:T(8,128)(2,1)S(1)}, u32[]{:S(2)}, u32[]{:S(2)}) collective-permute-start(bf16[8,4096]{1,0:T(8,128)(2,1)} %g_ref.1), channel_id=1, source_target_pairs={{0,8},{8,0},{16,24},{24,16},{1,9},{9,1},{17,25},{25,17},{2,10},{10... | collective-permute-start | bytes 196616 | tf_op jit(solution)/shard_map/ppermute | solution.py:241
  23.8 8.9 %collective-permute-start.1 = (bf16[8,4096]{1,0:T(8,128)(2,1)}, bf16[8,4096]{1,0:T(8,128)(2,1)S(1)}, u32[]{:S(2)}, u32[]{:S(2)}) collective-permute-start(bf16[8,4096]{1,0:T(8,128)(2,1)} %g_ref.1), channel_id=1, source_target_pairs={{0,16},{8,24},{16,0},{24,8},{1,17},{9,25},{17,1},{25,9},{2,18},{10... | collective-permute-start | bytes 196616 | tf_op jit(solution)/shard_map/ppermute | solution.py:241
  28.0 8.2 %collective-permute-start.2 = (bf16[8,4096]{1,0:T(8,128)(2,1)}, bf16[8,4096]{1,0:T(8,128)(2,1)S(1)}, u32[]{:S(2)}, u32[]{:S(2)}) collective-permute-start(bf16[8,4096]{1,0:T(8,128)(2,1)} %g_ref.1), channel_id=1, source_target_pairs={{0,24},{8,16},{16,8},{24,0},{1,25},{9,17},{17,9},{25,1},{2,26},{10... | collective-permute-start | bytes 196616 | tf_op jit(solution)/shard_map/ppermute | solution.py:241
  36.2 0.8 copy-start.4
  37.2 50.4 %all-to-all-start = ((bf16[4,464,256]{2,1,0:T(8,128)(2,1)}), bf16[4,464,256]{2,1,0:T(8,128)(2,1)}, u32[]{:S(2)}, u32[]{:S(2)}) async-start(bf16[4,464,256]{2,1,0:T(8,128)(2,1)} %hidden_copies.1), calls=%async_computation | async-start | bytes 1900544 | tf_op jit(solution)/shard_map/all_to_all | solution.py:254
  85.2 1.8 %copy-start.5 = (f16[59,64,512]{2,1,0:T(8,128)(2,1)}, f16[59,64,512]{2,1,0:T(8,128)(2,1)S(1)}, u32[]{:S(2)}) copy-start(f16[59,64,512]{2,1,0:T(8,128)(2,1)S(1)} %all-gather.2) | copy-start | bytes 11599876
  87.6 18.4 %copy-start.1 = (bf16[256,464]{0,1:T(8,128)(2,1)S(1)}, bf16[256,464]{0,1:T(8,128)(2,1)}, u32[]{:S(2)}) copy-start(bf16[256,464]{0,1:T(8,128)(2,1)} %param.5) | copy-start | bytes 712708
  87.6 18.4 %copy-start.2 = (bf16[256,464]{0,1:T(8,128)(2,1)S(1)}, bf16[256,464]{0,1:T(8,128)(2,1)}, u32[]{:S(2)}) copy-start(bf16[256,464]{0,1:T(8,128)(2,1)} %param.6) | copy-start | bytes 712708
  90.0 16.1 %copy-start = (bf16[4096,464]{0,1:T(8,128)(2,1)S(1)}, bf16[4096,464]{0,1:T(8,128)(2,1)}, u32[]{:S(2)}) copy-start(bf16[4096,464]{0,1:T(8,128)(2,1)} %param.7) | copy-start | bytes 11403268
  92.8 15.4 %collective-permute-start.3 = (bf16[464,128]{1,0:T(8,128)(2,1)S(1)}, bf16[464,128]{1,0:T(8,128)(2,1)S(1)}, u32[]{:S(2)}, u32[]{:S(2)}) collective-permute-start(bf16[464,128]{1,0:T(8,128)(2,1)S(1)} %get-tuple-element.22), channel_id=1, source_target_pairs={{0,256},{128,384},{256,0},{384,128},{1,257},{129,385},{257,1},{385... | collective-permute-start | bytes 356360 | tf_op jit(solution)/shard_map/ppermute | solution.py:241
  97.5 13.0 %collective-permute-start.4 = (bf16[464,128]{1,0:T(8,128)(2,1)S(1)}, bf16[464,128]{1,0:T(8,128)(2,1)S(1)}, u32[]{:S(2)}, u32[]{:S(2)}) collective-permute-start(bf16[464,128]{1,0:T(8,128)(2,1)S(1)} %get-tuple-element.23), channel_id=1, source_target_pairs={{0,128},{128,0},{256,384},{384,256},{1,129},{129,1},{257,385},{385... | collective-permute-start | bytes 356360 | tf_op jit(solution)/shard_map/ppermute | solution.py:241
  101.8 11.2 %collective-permute-start.5 = (bf16[464,128]{1,0:T(8,128)(2,1)S(1)}, bf16[464,128]{1,0:T(8,128)(2,1)S(1)}, u32[]{:S(2)}, u32[]{:S(2)}) collective-permute-start(bf16[464,128]{1,0:T(8,128)(2,1)S(1)} %get-tuple-element.24), channel_id=1, source_target_pairs={{0,384},{128,256},{256,128},{384,0},{1,385},{129,257},{257,129},{3... | collective-permute-start | bytes 356360 | tf_op jit(solution)/shard_map/ppermute | solution.py:241

commit v7 on v4

--- a/solution.py
+++ b/solution.py
@@ -34,21 +34,22 @@
 
 
 def own_kernel(a_ref, b_ref, c_ref, d_ref, out_ref, k_ref):
-    zl = lax.axis_index("zl")
+    x, zl = lax.axis_index("x"), lax.axis_index("zl")
     turns = (a_ref, b_ref, c_ref, d_ref)
-    for b in range(4):
-        most = None
-        for ref in turns:
-            for q in range(8):
-                value = jnp.abs(ref[:, 512 * q + 128 * b : 512 * q + 128 * (b + 1)].astype(jnp.float32))
-                most = value if most is None else jnp.maximum(most, value)
-        scale, k = scales_of(most)
-        k_ref[:, 128 * b : 128 * (b + 1)] = jnp.broadcast_to(k, (8, 128)).astype(jnp.bfloat16)
-        for s, ref in enumerate(turns):
-            place = lax.bitwise_xor(zl, s)
-            for q in range(8):
-                value = ref[:, 512 * q + 128 * b : 512 * q + 128 * (b + 1)].astype(jnp.float32) * scale
-                out_ref[4 * q + place, :, 128 * b : 128 * (b + 1)] = value.astype(jnp.bfloat16)
+    most = None
+    for ref in turns:
+        for n in range(32):
+            value = jnp.abs(ref[:, 128 * n : 128 * (n + 1)].astype(jnp.float32))
+            most = value if most is None else jnp.maximum(most, value)
+    scale, k = scales_of(most)
+    k_ref[...] = jnp.broadcast_to(k[None], (1, 8, 512)).astype(jnp.bfloat16)
+    for turn, ref in enumerate(turns):
+        place = lax.bitwise_xor(zl, turn)
+        for s in range(1, 8):
+            for z in range(2):
+                at = pl.multiple_of(2048 * z + 256 * lax.bitwise_xor(x, s), 256)
+                value = (ref[:, pl.ds(at, 256)].astype(jnp.float32) * scale).astype(jnp.bfloat16)
+                out_ref[4 * (s - 1) + place, :, 256 * z : 256 * (z + 1)] = value
 
 
 def rows_kernel(rows_ref, out_ref, k_ref):
@@ -56,14 +57,14 @@
         cols = slice(128 * b, 128 * (b + 1))
         most = jnp.max(jnp.abs(rows_ref[:, :, cols].astype(jnp.float32)), axis=0)
         scale, k = scales_of(most)
-        k_ref[:, cols] = jnp.broadcast_to(k, (8, 128)).astype(jnp.bfloat16)
+        k_ref[0, :, cols] = jnp.broadcast_to(k, (8, 128)).astype(jnp.bfloat16)
         out_ref[:, :, cols] = (rows_ref[:, :, cols].astype(jnp.float32) * scale[None]).astype(jnp.bfloat16)
 
 
-def scaled(kernel, *rows):
+def scaled(kernel, blocks, ks, *rows):
     return pl.pallas_call(
         kernel,
-        out_shape=(jax.ShapeDtypeStruct((32, 8, 512), jnp.bfloat16), jax.ShapeDtypeStruct((8, 512), jnp.bfloat16)),
+        out_shape=(jax.ShapeDtypeStruct((blocks, 8, 512), jnp.bfloat16), jax.ShapeDtypeStruct((ks, 8, 512), jnp.bfloat16)),
         in_specs=[pl.BlockSpec(memory_space=pltpu.VMEM)] * len(rows),
         out_specs=(pl.BlockSpec(memory_space=pltpu.VMEM),) * 2,
         cost_estimate=pl.CostEstimate(flops=1_000_000, bytes_accessed=600_000, transcendentals=0),
@@ -162,13 +163,53 @@
     )(hiddens, feats)
 
 
+def inputs_kernel(front_ref, last_ref, feats_ref, weight_ref, gate_ref, up_ref, grad_gate_ref, grad_up_ref, weight, total):
+    zh, x, c = lax.axis_index("zh"), lax.axis_index("x"), lax.axis_index("c")
+    t = gate_ref.shape[1]
+    for n in range(8):
+        slot = n % 2
+        if n < 7:
+            for z in range(2):
+                at = pl.multiple_of(2048 * z + 256 * lax.bitwise_xor(x, n + 1), 256)
+                weight[slot, :, 256 * z : 256 * (z + 1)] = weight_ref[:, pl.ds(at, 256)]
+            rows = front_ref[n] if n < 5 else last_ref[n - 5]
+        else:
+            for i, core in enumerate((1 - c, c)):
+                for j, z in enumerate((1 - zh, zh)):
+                    at = pl.multiple_of(2048 * z + 256 * x + 128 * core, 128)
+                    weight[slot, :, 256 * i + 128 * j : 256 * i + 128 * (j + 1)] = weight_ref[:, pl.ds(at, 128)]
+            rows = feats_ref[pl.ds(pl.multiple_of(x * t, t), t), :]
+        part = lax.dot_general(weight[slot], rows, (((1,), (1,)), ((), ())), preferred_element_type=jnp.float32)
+        total[...] = part if n == 0 else total[...] + part
+    grad_hidden = total[...]
+    gate = gate_ref[...].astype(jnp.float32)
+    upper = up_ref[...].astype(jnp.float32)
+    sig = jax.nn.sigmoid(gate)
+    grad_up_ref[...] = (grad_hidden * (gate * sig)).astype(jnp.bfloat16)
+    grad_gate_ref[...] = (grad_hidden * upper * sig * (1.0 + gate * (1.0 - sig))).astype(jnp.bfloat16)
+
+
+def input_grads(front, last, feats, weight, gate, up):
+    h, t = gate.shape
+    return pl.pallas_call(
+        inputs_kernel,
+        out_shape=(jax.ShapeDtypeStruct((h, t), jnp.bfloat16),) * 2,
+        in_specs=[pl.BlockSpec(memory_space=pltpu.VMEM)] * 6,
+        out_specs=(pl.BlockSpec(memory_space=pltpu.VMEM),) * 2,
+        scratch_shapes=[pltpu.VMEM((2, h, 512), jnp.bfloat16), pltpu.VMEM((h, t), jnp.float32)],
+        cost_estimate=pl.CostEstimate(flops=2 * h * t * 4096, bytes_accessed=6_000_000, transcendentals=h * t),
+        compiler_params=pltpu.CompilerParams(vmem_limit_bytes=16 << 20),
+        name="input_grads",
+    )(front, last, feats, weight, gate, up)
+
+
 def turned(x, axis, by):
     return lax.ppermute(x, axis, [(i, i ^ by) for i in range(lax.axis_size(axis))])
 
 
 def sections(grad_out, gate_pre, up_pre, down_weight):
     gate_t, up_t = gate_pre.T, up_pre.T
-    h, t = gate_t.shape
+    _, t = gate_t.shape
 
     pieces = split_rows(grad_out)
     mine = lax.all_to_all(pieces, ("x", "zl"), 0, 0)
@@ -178,29 +219,23 @@
     copies = hidden_copies(gate_t, up_t)
     hiddens = lax.all_to_all(copies, "x", 0, 0)
 
-    own, own_k = scaled(own_kernel, *turns)
-    feats, feats_k = scaled(rows_kernel, mine)
-    message = jnp.concatenate([own, feats, own_k[None], feats_k[None]], 0).astype(jnp.float16)
+    own, own_k = scaled(own_kernel, 28, 1, *turns)
+    rows, rows_k = scaled(rows_kernel, 32, 1, mine)
+    message = jnp.concatenate([own, rows, own_k, rows_k], 0).astype(jnp.float16)
     got = lax.all_gather(message, "y", axis=1, tiled=True)
 
-    scale = power(got[65].astype(jnp.float32), -1)
-    feats = (got[32:64].astype(jnp.float32) * scale).astype(jnp.bfloat16).reshape(8 * t, 512)
+    scale = power(got[60:].astype(jnp.float32), -1)
+    feats = (got[28:60].astype(jnp.float32) * scale[1]).astype(jnp.bfloat16).reshape(8 * t, 512)
+    front = (got[:20].astype(jnp.float32) * scale[0]).astype(jnp.bfloat16).reshape(5, t, 512)
+    last = (got[20:28].astype(jnp.float32) * scale[0]).astype(jnp.bfloat16).reshape(2, t, 512)
+
     theirs, ours = weight_parts(hiddens, feats)
     swap = lax.all_gather(theirs.astype(jnp.bfloat16), "c", axis=0)
     part = ours + lax.dynamic_index_in_dim(swap, 1 - lax.axis_index("c"), 0, keepdims=False).astype(jnp.float32)
     away = turned(part[:, :128].astype(jnp.bfloat16), "zh", 1)
     here = part[:, 128:]
 
-    scale = power(got[64].astype(jnp.float32), -1)
-    whole = (got[:32].astype(jnp.float32) * scale).astype(jnp.bfloat16).reshape(8, t, 512)
-    weight = down_weight.T.reshape(h, 8, 512)
-    grad_hidden = lax.dot_general(weight, whole, (((1, 2), (0, 2)), ((), ())), preferred_element_type=jnp.float32)
-    gate = gate_t.astype(jnp.float32)
-    upper = up_t.astype(jnp.float32)
-    sig = jax.nn.sigmoid(gate)
-    act = gate * sig
-    grad_up = (grad_hidden * act).astype(jnp.bfloat16)
-    grad_gate = (grad_hidden * upper * sig * (1.0 + gate * (1.0 - sig))).astype(jnp.bfloat16)
+    grad_gate, grad_up = input_grads(front, last, feats, down_weight.T, gate_t, up_t)
     return (here + away.astype(jnp.float32)).T, grad_gate.T, grad_up.T
 
 

time: 123 us -> 121 us (0.984)
  matrix products: 2.04 us -> 0 us
  Pallas kernels: 6.21 us -> 8.23 us
  blocking collectives: 52.2 us -> 50.2 us
  local copies, waits for them, and re-layouts: 0.87 us -> 2.22 us
    all_gather x1, blocking collectives: 46.6 us -> 44.4 us  [sections(): got = lax.all_gather(message, 'y', axis=1, tiled=True)]
    pallas_call x2 -> x3, Pallas kernels: 0.4 us -> 2.45 us  [the longest x1 2.07 us: input_grads(): pl.pallas_call(inputs_kernel, out_shape=(jax.ShapeDtypeStruct((h, t), jnp...]
    dot_general x1 -> x0, matrix products: 2.04 us -> none  [sections(): lax.dot_general(weight, whole, (((1, 2), (0, 2)), ((), ())), preferred_el...]
    unnamed x12, local copies, waits for them, and re-layouts: 0.85 us -> 2.18 us
    convert_element_type x2 -> x4, other arithmetic: 2.72 us -> 2.13 us  [the longest x1 1.14 us: sections(): (got[20:28].astype(jnp.float32) * scale[0]).astype(jnp.bfloat16)]
  transfers between devices with their start and end apart: 6 -> 6, of which waited for: 3 -> 3; matrix products, arithmetic and copies ran while one was open for 4% -> 2% of each run, Pallas kernels for 2% -> 4%
where the time goes in v7:
time: 121 us; the launch traced here: 120 us
  blocking collectives  50.2 us (41%)
  starting transfers between devices  41 us (34%)
  waiting for transfers between devices  14.5 us (12%)
  Pallas kernels  8.23 us (7%)
  other arithmetic  3.16 us (3%)
  local copies, waits for them, and re-layouts  2.22 us (2%)
    all_gather x1, blocking collectives, sections(): got = lax.all_gather(message, 'y', axis=1, tiled=True)  44.4 us
    ppermute x4, starting transfers between devices, turned(): lax.ppermute(x, axis, [(i, i ^ by) for i in range(lax.axis_size(axis))])  20.9 us
    all_to_all x1, starting transfers between devices, sections(): mine = lax.all_to_all(pieces, ('x', 'zl'), 0, 0)  15.9 us
    all_to_all x1, waiting for transfers between devices, sections(): mine = lax.all_to_all(pieces, ('x', 'zl'), 0, 0)  8.42 us
    ppermute x4, waiting for transfers between devices, turned(): lax.ppermute(x, axis, [(i, i ^ by) for i in range(lax.axis_size(axis))])  6.08 us
    all_gather x1, blocking collectives, sections(): swap = lax.all_gather(theirs.astype(jnp.bfloat16), 'c', axis=0)  5.75 us
    all_to_all x1, starting transfers between devices, sections(): hiddens = lax.all_to_all(copies, 'x', 0, 0)  4.33 us
    pallas_call x1, Pallas kernels, hidden_copies(): pl.pallas_call(hidden_kernel, out_shape=jax.ShapeDtypeStruct((8, h, t), j...  2.55 us
  transfers between devices with their start and end apart: 6, of which 3 were waited for; matrix products, arithmetic and copies ran while one was open for 2% of the time, Pallas kernels for 4%

profile of v7, /device:TPU:1, one launch (start us, length us, event | category | flops | bytes accessed | tf_op | source)
XLA Modules:
  0.0 120.2 jit_solution(2921127817089006786)
XLA Ops:
  0.6 0.0 copy-start.3
  0.6 0.8 copy-done.3
  1.5 0.8 split_rows.1
  2.2 15.9 %all-to-all-start.1 = ((bf16[32,8,512]{2,1,0:T(8,128)(2,1)}), bf16[32,8,512]{2,1,0:T(8,128)(2,1)S(1)}, u32[]{:S(2)}, u32[]{:S(2)}) async-start(bf16[32,8,512]{2,1,0:T(8,128)(2,1)} %split_rows.1), calls=%async_computation.1 | async-start | bytes 524288 | tf_op jit(solution)/shard_map/all_to_all | solution.py:215
  18.1 0.0 copy-start.4
  18.1 2.6 %hidden_copies.1 = bf16[8,464,256]{2,1,0:T(8,128)(2,1)} custom-call(bf16[464,256]{1,0:T(8,128)(2,1)} %bitcast.23, bf16[464,256]{1,0:T(8,128)(2,1)} %bitcast.25), custom_call_target="tpu_custom_call" | custom-call | flops 2000000 | bytes 2375680 | tf_op jit(solution)/shard_map/hidden_copies/pallas_call | solution.py:100
  20.7 8.4 %all-to-all-done.1.rows_ref = bf16[32,8,512]{2,1,0:T(8,128)(2,1)S(1)} async-done(((bf16[32,8,512]{2,1,0:T(8,128)(2,1)}), bf16[32,8,512]{2,1,0:T(8,128)(2,1)S(1)}, u32[]{:S(2)}, u32[]{:S(2)}) %all-to-all-start.1) | async-done | bytes 262176 | tf_op jit(solution)/shard_map/all_to_all | solution.py:215
  29.1 4.3 %all-to-all-start = ((bf16[8,464,256]{2,1,0:T(8,128)(2,1)}), bf16[8,464,256]{2,1,0:T(8,128)(2,1)}, u32[]{:S(2)}, u32[]{:S(2)}) async-start(bf16[8,464,256]{2,1,0:T(8,128)(2,1)} %hidden_copies.1), calls=%async_computation | async-start | bytes 3801088 | tf_op jit(solution)/shard_map/all_to_all | solution.py:220
  33.4 0.0 copy-done.4
  33.4 1.9 %collective-permute-start = (bf16[8,4096]{1,0:T(8,128)(2,1)S(1)}, bf16[8,4096]{1,0:T(8,128)(2,1)S(1)}, u32[]{:S(2)}, u32[]{:S(2)}) collective-permute-start(bf16[8,4096]{1,0:T(8,128)(2,1)S(1)} %copy-done.4), channel_id=1, source_target_pairs={{0,8},{8,0},{16,24},{24,16},{1,9},{9,1},{17,25},{25,17},{2,10},{10... | collective-permute-start | bytes 196616 | tf_op jit(solution)/shard_map/ppermute | solution.py:207
  35.4 3.7 %collective-permute-start.1 = (bf16[8,4096]{1,0:T(8,128)(2,1)S(1)}, bf16[8,4096]{1,0:T(8,128)(2,1)S(1)}, u32[]{:S(2)}, u32[]{:S(2)}) collective-permute-start(bf16[8,4096]{1,0:T(8,128)(2,1)S(1)} %copy-done.4), channel_id=1, source_target_pairs={{0,16},{8,24},{16,0},{24,8},{1,17},{9,25},{17,1},{25,9},{2,18},{10... | collective-permute-start | bytes 196616 | tf_op jit(solution)/shard_map/ppermute | solution.py:207
  39.1 3.6 %collective-permute-start.2 = (bf16[8,4096]{1,0:T(8,128)(2,1)S(1)}, bf16[8,4096]{1,0:T(8,128)(2,1)S(1)}, u32[]{:S(2)}, u32[]{:S(2)}) collective-permute-start(bf16[8,4096]{1,0:T(8,128)(2,1)S(1)} %copy-done.4), channel_id=1, source_target_pairs={{0,24},{8,16},{16,8},{24,0},{1,25},{9,17},{17,9},{25,1},{2,26},{10... | collective-permute-start | bytes 196616 | tf_op jit(solution)/shard_map/ppermute | solution.py:207
  42.7 0.0 collective-permute-done.b_ref
  42.7 0.0 collective-permute-done.1.c_ref
  42.8 3.6 %collective-permute-done.2.d_ref = bf16[8,4096]{1,0:T(8,128)(2,1)S(1)} collective-permute-done((bf16[8,4096]{1,0:T(8,128)(2,1)S(1)}, bf16[8,4096]{1,0:T(8,128)(2,1)S(1)}, u32[]{:S(2)}, u32[]{:S(2)}) %collective-permute-start.2) | collective-permute-done | bytes 65568 | tf_op jit(solution)/shard_map/ppermute | solution.py:207
  46.3 0.2 shard_map.67
  46.5 0.2 shard_map.68
  46.7 0.1 maximum_convert_fusion
  46.9 44.4 %all-gather.2 = f16[62,64,512]{2,1,0:T(8,128)(2,1)S(1)} all-gather(f16[62,8,512]{2,1,0:T(8,128)(2,1)S(1)} %maximum_convert_fusion), channel_id=1, replica_groups=mesh['zh'=2,'x'=8,'c'=2,'zl'=4,'y'=8] {'y'}, dimensions={1}, use_global_device_ids=true | all-gather | bytes 4571136 | tf_op jit(solution)/shard_map/all_gather | solution.py:225
  91.3 0.0 copy-start.5
  91.3 0.2 multiply_select_fusion
  91.5 0.3 multiply_convert_fusion.1
  91.8 1.3 %copy-done.5 = f16[62,64,512]{2,1,0:T(8,128)(2,1)} copy-done((f16[62,64,512]{2,1,0:T(8,128)(2,1)}, f16[62,64,512]{2,1,0:T(8,128)(2,1)S(1)}, u32[]{:S(2)}) %copy-start.5) | copy-done | bytes 4063256
  93.2 0.5 multiply_convert_fusion
  93.7 0.0 all-to-all-done.hidden_ref
  93.7 0.0 copy-start.2
  93.7 2.5 %weight_parts.1 = (f32[464,256]{1,0:T(8,128)S(1)}, f32[464,256]{1,0:T(8,128)S(1)}) custom-call(bf16[8,464,256]{2,1,0:T(8,128)(2,1)} %all-to-all-done.hidden_ref, bf16[2048,512]{1,0:T(8,128)(2,1)S(1)} %bitcast.18), custom_call_target="tpu_custom_call" | custom-call | flops 973078528 | bytes 4000000 | tf_op jit(solution)/shard_map/weight_parts/pallas_call | solution.py:154
  96.2 0.0 copy-start
  96.2 0.0 copy-start.1
  96.3 5.8 %all-gather = bf16[928,256]{1,0:T(8,128)(2,1)S(1)} all-gather(bf16[464,256]{1,0:T(8,128)(2,1)S(1)} %convert_element_type.41), channel_id=2, replica_groups=mesh['zh'=2,'x'=8,'c'=2,'zl'=4,'y'=8] {'c'}, dimensions={0}, use_global_device_ids=true | all-gather | bytes 712704 | tf_op jit(solution)/shard_map/all_gather | solution.py:233
  102.0 0.1 convert_add_fusion
  102.1 11.6 %collective-permute-start.3 = (bf16[464,128]{1,0:T(8,128)(2,1)S(1)}, bf16[464,128]{1,0:T(8,128)(2,1)S(1)}, u32[]{:S(2)}, u32[]{:S(2)}) collective-permute-start(bf16[464,128]{1,0:T(8,128)(2,1)S(1)} %slice.52), channel_id=1, source_target_pairs={{0,512},{512,0},{1,513},{513,1},{2,514},{514,2},{3,515},{515,3},{4... | collective-permute-start | bytes 356360 | tf_op jit(solution)/shard_map/ppermute | solution.py:207
  113.7 1.1 multiply_convert_fusion.2
  114.8 0.0 copy-done.2
  114.9 0.0 copy-done
  114.9 0.0 copy-done.1
  114.9 2.1 %input_grads.1 = (bf16[464,256]{1,0:T(8,128)(2,1)}, bf16[464,256]{1,0:T(8,128)(2,1)}) custom-call(bf16[5,256,512]{2,1,0:T(8,128)(2,1)S(1)} %bitcast.20, bf16[2,256,512]{2,1,0:T(8,128)(2,1)S(1)} %bitcast.22, bf16[2048,512]{1,0:T(8,128)(2,1)S(1)} %bitcast.19, bf16[464,4096]{1,0:T(8,128)(2,1)S(1)} %bitcast.21, bf16[464,256]{1,0:T(8,128)(2,1)S(1)} %bitcast.24, ...), custom_call_target="tpu_custom_call" | custom-call | flops 973078528 | bytes 6000000 | tf_op jit(solution)/shard_map/input_grads/pallas_call | solution.py:194
  117.0 2.5 %collective-permute-done.3 = bf16[464,128]{1,0:T(8,128)(2,1)S(1)} collective-permute-done((bf16[464,128]{1,0:T(8,128)(2,1)S(1)}, bf16[464,128]{1,0:T(8,128)(2,1)S(1)}, u32[]{:S(2)}, u32[]{:S(2)}) %collective-permute-start.3) | collective-permute-done | bytes 118816 | tf_op jit(solution)/shard_map/ppermute | solution.py:207
  119.5 0.7 fusion.1
  (3 shorter events, 0.1 us)
Async XLA Ops:
  0.6 0.8 copy-start.3
  2.2 26.9 %all-to-all-start.1 = ((bf16[32,8,512]{2,1,0:T(8,128)(2,1)}), bf16[32,8,512]{2,1,0:T(8,128)(2,1)S(1)}, u32[]{:S(2)}, u32[]{:S(2)}) async-start(bf16[32,8,512]{2,1,0:T(8,128)(2,1)} %split_rows.1), calls=%async_computation.1 | async-start | bytes 524288 | tf_op jit(solution)/shard_map/all_to_all | solution.py:215
  18.1 15.3 %copy-start.4 = (bf16[8,4096]{1,0:T(8,128)(2,1)S(1)}, bf16[8,4096]{1,0:T(8,128)(2,1)}, u32[]{:S(2)}) copy-start(bf16[8,4096]{1,0:T(8,128)(2,1)} %g_ref.1) | copy-start | bytes 196612
  29.1 64.6 %all-to-all-start = ((bf16[8,464,256]{2,1,0:T(8,128)(2,1)}), bf16[8,464,256]{2,1,0:T(8,128)(2,1)}, u32[]{:S(2)}, u32[]{:S(2)}) async-start(bf16[8,464,256]{2,1,0:T(8,128)(2,1)} %hidden_copies.1), calls=%async_computation | async-start | bytes 3801088 | tf_op jit(solution)/shard_map/all_to_all | solution.py:220
  33.4 9.3 %collective-permute-start = (bf16[8,4096]{1,0:T(8,128)(2,1)S(1)}, bf16[8,4096]{1,0:T(8,128)(2,1)S(1)}, u32[]{:S(2)}, u32[]{:S(2)}) collective-permute-start(bf16[8,4096]{1,0:T(8,128)(2,1)S(1)} %copy-done.4), channel_id=1, source_target_pairs={{0,8},{8,0},{16,24},{24,16},{1,9},{9,1},{17,25},{25,17},{2,10},{10... | collective-permute-start | bytes 196616 | tf_op jit(solution)/shard_map/ppermute | solution.py:207
  35.4 7.4 %collective-permute-start.1 = (bf16[8,4096]{1,0:T(8,128)(2,1)S(1)}, bf16[8,4096]{1,0:T(8,128)(2,1)S(1)}, u32[]{:S(2)}, u32[]{:S(2)}) collective-permute-start(bf16[8,4096]{1,0:T(8,128)(2,1)S(1)} %copy-done.4), channel_id=1, source_target_pairs={{0,16},{8,24},{16,0},{24,8},{1,17},{9,25},{17,1},{25,9},{2,18},{10... | collective-permute-start | bytes 196616 | tf_op jit(solution)/shard_map/ppermute | solution.py:207
  39.1 7.2 %collective-permute-start.2 = (bf16[8,4096]{1,0:T(8,128)(2,1)S(1)}, bf16[8,4096]{1,0:T(8,128)(2,1)S(1)}, u32[]{:S(2)}, u32[]{:S(2)}) collective-permute-start(bf16[8,4096]{1,0:T(8,128)(2,1)S(1)} %copy-done.4), channel_id=1, source_target_pairs={{0,24},{8,16},{16,8},{24,0},{1,25},{9,17},{17,9},{25,1},{2,26},{10... | collective-permute-start | bytes 196616 | tf_op jit(solution)/shard_map/ppermute | solution.py:207
  91.3 1.9 %copy-start.5 = (f16[62,64,512]{2,1,0:T(8,128)(2,1)}, f16[62,64,512]{2,1,0:T(8,128)(2,1)S(1)}, u32[]{:S(2)}) copy-start(f16[62,64,512]{2,1,0:T(8,128)(2,1)S(1)} %all-gather.2) | copy-start | bytes 12189700
  93.7 21.1 %copy-start.2 = (bf16[256,464]{0,1:T(8,128)(2,1)S(1)}, bf16[256,464]{0,1:T(8,128)(2,1)}, u32[]{:S(2)}) copy-start(bf16[256,464]{0,1:T(8,128)(2,1)} %param.6) | copy-start | bytes 712708
  96.2 18.6 %copy-start = (bf16[4096,464]{0,1:T(8,128)(2,1)S(1)}, bf16[4096,464]{0,1:T(8,128)(2,1)}, u32[]{:S(2)}) copy-start(bf16[4096,464]{0,1:T(8,128)(2,1)} %param.7) | copy-start | bytes 11403268
  96.2 18.6 %copy-start.1 = (bf16[256,464]{0,1:T(8,128)(2,1)S(1)}, bf16[256,464]{0,1:T(8,128)(2,1)}, u32[]{:S(2)}) copy-start(bf16[256,464]{0,1:T(8,128)(2,1)} %param.5) | copy-start | bytes 712708
  102.1 17.4 %collective-permute-start.3 = (bf16[464,128]{1,0:T(8,128)(2,1)S(1)}, bf16[464,128]{1,0:T(8,128)(2,1)S(1)}, u32[]{:S(2)}, u32[]{:S(2)}) collective-permute-start(bf16[464,128]{1,0:T(8,128)(2,1)S(1)} %slice.52), channel_id=1, source_target_pairs={{0,512},{512,0},{1,513},{513,1},{2,514},{514,2},{3,515},{515,3},{4... | collective-permute-start | bytes 356360 | tf_op jit(solution)/shard_map/ppermute | solution.py:207

commit v8 on v7

--- a/solution.py
+++ b/solution.py
@@ -33,9 +33,9 @@
     return power(k, 1), k
 
 
-def own_kernel(a_ref, b_ref, c_ref, d_ref, out_ref, k_ref):
+def own_kernel(pair_ref, far_ref, out_ref, k_ref):
     x, zl = lax.axis_index("x"), lax.axis_index("zl")
-    turns = (a_ref, b_ref, c_ref, d_ref)
+    turns = (pair_ref.at[0], pair_ref.at[1], far_ref.at[0], far_ref.at[1])
     most = None
     for ref in turns:
         for n in range(32):
@@ -213,13 +213,13 @@
 
     pieces = split_rows(grad_out)
     mine = lax.all_to_all(pieces, ("x", "zl"), 0, 0)
-    turns = [grad_out]
-    for s in (1, 2, 3):
-        turns.append(turned(grad_out, "zl", s))
+    near = turned(grad_out, "zl", 1)
+    pair = jnp.stack([grad_out, near])
+    far = turned(pair, "zl", 2)
     copies = hidden_copies(gate_t, up_t)
     hiddens = lax.all_to_all(copies, "x", 0, 0)
 
-    own, own_k = scaled(own_kernel, 28, 1, *turns)
+    own, own_k = scaled(own_kernel, 28, 1, pair, far)
     rows, rows_k = scaled(rows_kernel, 32, 1, mine)
     message = jnp.concatenate([own, rows, own_k, rows_k], 0).astype(jnp.float16)
     got = lax.all_gather(message, "y", axis=1, tiled=True)

time: 121 us -> 114 us (0.942)
  the two profiles are of different devices: /device:TPU:1 before, /device:TPU:16 now
where the time goes in v8:
time: 114 us
  blocking collectives  45.6 us (40%)
  starting transfers between devices  37.6 us (33%)
  waiting for transfers between devices  16 us (14%)
  Pallas kernels  8.16 us (7%)
  other arithmetic  3.17 us (3%)
  local copies, waits for them, and re-layouts  2.22 us (2%)
    all_gather x1, blocking collectives, sections(): got = lax.all_gather(message, 'y', axis=1, tiled=True)  43.3 us
    ppermute x3, starting transfers between devices, turned(): lax.ppermute(x, axis, [(i, i ^ by) for i in range(lax.axis_size(axis))])  18 us
    all_to_all x1, starting transfers between devices, sections(): mine = lax.all_to_all(pieces, ('x', 'zl'), 0, 0)  15.3 us
    ppermute x3, waiting for transfers between devices, turned(): lax.ppermute(x, axis, [(i, i ^ by) for i in range(lax.axis_size(axis))])  8.81 us
    all_to_all x1, waiting for transfers between devices, sections(): mine = lax.all_to_all(pieces, ('x', 'zl'), 0, 0)  7.16 us
    all_to_all x1, starting transfers between devices, sections(): hiddens = lax.all_to_all(copies, 'x', 0, 0)  4.32 us
    pallas_call x1, Pallas kernels, hidden_copies(): pl.pallas_call(hidden_kernel, out_shape=jax.ShapeDtypeStruct((8, h, t), j...  2.51 us
    pallas_call x1, Pallas kernels, weight_parts(): pl.pallas_call(weights_kernel, out_shape=(jax.ShapeDtypeStruct((h, 256),...  2.48 us
  transfers between devices with their start and end apart: 5, of which 3 were waited for; matrix products, arithmetic and copies ran while one was open for 2% of the time, Pallas kernels for 4%

profile of v8, /device:TPU:16, one launch (start us, length us, event | category | flops | bytes accessed | tf_op | source)
XLA Modules:
  0.0 113.6 jit_solution(17702261479488470741)
XLA Ops:
  0.6 0.0 copy-start.3
  0.6 0.8 copy-done.3
  1.5 0.7 split_rows.1
  2.2 15.3 %all-to-all-start.1 = ((bf16[32,8,512]{2,1,0:T(8,128)(2,1)}), bf16[32,8,512]{2,1,0:T(8,128)(2,1)S(1)}, u32[]{:S(2)}, u32[]{:S(2)}) async-start(bf16[32,8,512]{2,1,0:T(8,128)(2,1)} %split_rows.1), calls=%async_computation.1 | async-start | bytes 524288 | tf_op jit(solution)/shard_map/all_to_all | solution.py:215
  17.5 3.7 %collective-permute-start = (bf16[8,4096]{1,0:T(8,128)(2,1)}, bf16[8,4096]{1,0:T(8,128)(2,1)S(1)}, u32[]{:S(2)}, u32[]{:S(2)}) collective-permute-start(bf16[8,4096]{1,0:T(8,128)(2,1)} %g_ref.1), channel_id=1, source_target_pairs={{0,8},{8,0},{16,24},{24,16},{1,9},{9,1},{17,25},{25,17},{2,10},{10... | collective-permute-start | bytes 196616 | tf_op jit(solution)/shard_map/ppermute | solution.py:207
  21.3 0.0 copy-start.4
  21.3 2.5 %hidden_copies.1 = bf16[8,464,256]{2,1,0:T(8,128)(2,1)} custom-call(bf16[464,256]{1,0:T(8,128)(2,1)} %bitcast.25, bf16[464,256]{1,0:T(8,128)(2,1)} %bitcast.27), custom_call_target="tpu_custom_call" | custom-call | flops 2000000 | bytes 2375680 | tf_op jit(solution)/shard_map/hidden_copies/pallas_call | solution.py:100
  23.8 7.2 %all-to-all-done.1.rows_ref = bf16[32,8,512]{2,1,0:T(8,128)(2,1)S(1)} async-done(((bf16[32,8,512]{2,1,0:T(8,128)(2,1)}), bf16[32,8,512]{2,1,0:T(8,128)(2,1)S(1)}, u32[]{:S(2)}, u32[]{:S(2)}) %all-to-all-start.1) | async-done | bytes 262176 | tf_op jit(solution)/shard_map/all_to_all | solution.py:215
  30.9 4.3 %all-to-all-start = ((bf16[8,464,256]{2,1,0:T(8,128)(2,1)}), bf16[8,464,256]{2,1,0:T(8,128)(2,1)}, u32[]{:S(2)}, u32[]{:S(2)}) async-start(bf16[8,464,256]{2,1,0:T(8,128)(2,1)} %hidden_copies.1), calls=%async_computation | async-start | bytes 3801088 | tf_op jit(solution)/shard_map/all_to_all | solution.py:220
  35.3 0.0 collective-permute-done
  35.3 0.0 copy-done.4
  35.3 2.4 %collective-permute-start.1 = (bf16[2,8,4096]{2,1,0:T(8,128)(2,1)S(1)}, bf16[2,8,4096]{2,1,0:T(8,128)(2,1)S(1)}, u32[]{:S(2)}, u32[]{:S(2)}) collective-permute-start(bf16[2,8,4096]{2,1,0:T(8,128)(2,1)S(1)} %pad_maximum_fusion.pair_ref), channel_id=1, source_target_pairs={{0,16},{8,24},{16,0},{24,8},{1,17},{9,25},{17,1},{25,9},{2,18},{10... | collective-permute-start | bytes 393224 | tf_op jit(solution)/shard_map/ppermute | solution.py:207
  37.7 6.0 %collective-permute-done.1.far_ref = bf16[2,8,4096]{2,1,0:T(8,128)(2,1)S(1)} collective-permute-done((bf16[2,8,4096]{2,1,0:T(8,128)(2,1)S(1)}, bf16[2,8,4096]{2,1,0:T(8,128)(2,1)S(1)}, u32[]{:S(2)}, u32[]{:S(2)}) %collective-permute-start.1) | collective-permute-done | bytes 131104 | tf_op jit(solution)/shard_map/ppermute | solution.py:207
  43.7 0.2 shard_map.67
  43.9 0.2 shard_map.68
  44.1 0.1 maximum_convert_fusion
  44.3 43.3 %all-gather.2 = f16[62,64,512]{2,1,0:T(8,128)(2,1)S(1)} all-gather(f16[62,8,512]{2,1,0:T(8,128)(2,1)S(1)} %maximum_convert_fusion), channel_id=1, replica_groups=mesh['zh'=2,'x'=8,'c'=2,'zl'=4,'y'=8] {'y'}, dimensions={1}, use_global_device_ids=true | all-gather | bytes 4571136 | tf_op jit(solution)/shard_map/all_gather | solution.py:225
  87.6 0.0 copy-start.5
  87.6 0.2 multiply_select_fusion
  87.9 0.3 multiply_convert_fusion.1
  88.2 1.3 %copy-done.5 = f16[62,64,512]{2,1,0:T(8,128)(2,1)} copy-done((f16[62,64,512]{2,1,0:T(8,128)(2,1)}, f16[62,64,512]{2,1,0:T(8,128)(2,1)S(1)}, u32[]{:S(2)}) %copy-start.5) | copy-done | bytes 4063256
  89.5 0.5 multiply_convert_fusion
  90.0 0.0 all-to-all-done.hidden_ref
  90.1 0.0 copy-start.2
  90.1 2.5 %weight_parts.1 = (f32[464,256]{1,0:T(8,128)S(1)}, f32[464,256]{1,0:T(8,128)S(1)}) custom-call(bf16[8,464,256]{2,1,0:T(8,128)(2,1)} %all-to-all-done.hidden_ref, bf16[2048,512]{1,0:T(8,128)(2,1)S(1)} %bitcast.20), custom_call_target="tpu_custom_call" | custom-call | flops 973078528 | bytes 4000000 | tf_op jit(solution)/shard_map/weight_parts/pallas_call | solution.py:154
  92.5 0.0 copy-start
  92.6 0.0 copy-start.1
  92.6 2.3 %all-gather = bf16[928,256]{1,0:T(8,128)(2,1)S(1)} all-gather(bf16[464,256]{1,0:T(8,128)(2,1)S(1)} %convert_element_type.41), channel_id=2, replica_groups=mesh['zh'=2,'x'=8,'c'=2,'zl'=4,'y'=8] {'c'}, dimensions={0}, use_global_device_ids=true | all-gather | bytes 712704 | tf_op jit(solution)/shard_map/all_gather | solution.py:233
  95.0 11.9 %collective-permute-start.2 = (bf16[464,128]{1,0:T(8,128)(2,1)S(1)}, bf16[464,128]{1,0:T(8,128)(2,1)S(1)}, u32[]{:S(2)}, u32[]{:S(2)}) collective-permute-start(bf16[464,128]{1,0:T(8,128)(2,1)S(1)} %slice.52), channel_id=1, source_target_pairs={{0,512},{512,0},{1,513},{513,1},{2,514},{514,2},{3,515},{515,3},{4... | collective-permute-start | bytes 356360 | tf_op jit(solution)/shard_map/ppermute | solution.py:207
  106.8 1.1 %multiply_convert_fusion.2 = bf16[8,64,512]{2,1,0:T(8,128)(2,1)S(1)} fusion(f16[62,64,512]{2,1,0:T(8,128)(2,1)} %copy-done.5, f32[64,512]{1,0:T(8,128)S(1)} %get-tuple-element.19), kind=kLoop, calls=%fused_computation.2 | loop fusion | flops 786432 | bytes 1179648 | tf_op jit(solution)/shard_map/convert_element_type | solution.py:230
  108.0 0.0 copy-done.2
  108.0 0.0 copy-done
  108.0 0.0 copy-done.1
  108.0 2.1 %input_grads.1 = (bf16[464,256]{1,0:T(8,128)(2,1)}, bf16[464,256]{1,0:T(8,128)(2,1)}) custom-call(bf16[5,256,512]{2,1,0:T(8,128)(2,1)S(1)} %bitcast.22, bf16[2,256,512]{2,1,0:T(8,128)(2,1)S(1)} %bitcast.24, bf16[2048,512]{1,0:T(8,128)(2,1)S(1)} %bitcast.21, bf16[464,4096]{1,0:T(8,128)(2,1)S(1)} %bitcast.23, bf16[464,256]{1,0:T(8,128)(2,1)S(1)} %bitcast.26, ...), custom_call_target="tpu_custom_call" | custom-call | flops 973078528 | bytes 6000000 | tf_op jit(solution)/shard_map/input_grads/pallas_call | solution.py:194
  110.1 2.8 %collective-permute-done.2 = bf16[464,128]{1,0:T(8,128)(2,1)S(1)} collective-permute-done((bf16[464,128]{1,0:T(8,128)(2,1)S(1)}, bf16[464,128]{1,0:T(8,128)(2,1)S(1)}, u32[]{:S(2)}, u32[]{:S(2)}) %collective-permute-start.2) | collective-permute-done | bytes 118816 | tf_op jit(solution)/shard_map/ppermute | solution.py:207
  112.9 0.7 fusion.1
  (5 shorter events, 0.1 us)
Async XLA Ops:
  0.6 0.8 copy-start.3
  2.2 28.7 %all-to-all-start.1 = ((bf16[32,8,512]{2,1,0:T(8,128)(2,1)}), bf16[32,8,512]{2,1,0:T(8,128)(2,1)S(1)}, u32[]{:S(2)}, u32[]{:S(2)}) async-start(bf16[32,8,512]{2,1,0:T(8,128)(2,1)} %split_rows.1), calls=%async_computation.1 | async-start | bytes 524288 | tf_op jit(solution)/shard_map/all_to_all | solution.py:215
  17.5 17.7 %collective-permute-start = (bf16[8,4096]{1,0:T(8,128)(2,1)}, bf16[8,4096]{1,0:T(8,128)(2,1)S(1)}, u32[]{:S(2)}, u32[]{:S(2)}) collective-permute-start(bf16[8,4096]{1,0:T(8,128)(2,1)} %g_ref.1), channel_id=1, source_target_pairs={{0,8},{8,0},{16,24},{24,16},{1,9},{9,1},{17,25},{25,17},{2,10},{10... | collective-permute-start | bytes 196616 | tf_op jit(solution)/shard_map/ppermute | solution.py:207
  21.3 14.0 %copy-start.4 = (bf16[8,4096]{1,0:T(8,128)(2,1)S(1)}, bf16[8,4096]{1,0:T(8,128)(2,1)}, u32[]{:S(2)}) copy-start(bf16[8,4096]{1,0:T(8,128)(2,1)} %g_ref.1) | copy-start | bytes 196612
  30.9 59.1 %all-to-all-start = ((bf16[8,464,256]{2,1,0:T(8,128)(2,1)}), bf16[8,464,256]{2,1,0:T(8,128)(2,1)}, u32[]{:S(2)}, u32[]{:S(2)}) async-start(bf16[8,464,256]{2,1,0:T(8,128)(2,1)} %hidden_copies.1), calls=%async_computation | async-start | bytes 3801088 | tf_op jit(solution)/shard_map/all_to_all | solution.py:220
  35.3 8.4 %collective-permute-start.1 = (bf16[2,8,4096]{2,1,0:T(8,128)(2,1)S(1)}, bf16[2,8,4096]{2,1,0:T(8,128)(2,1)S(1)}, u32[]{:S(2)}, u32[]{:S(2)}) collective-permute-start(bf16[2,8,4096]{2,1,0:T(8,128)(2,1)S(1)} %pad_maximum_fusion.pair_ref), channel_id=1, source_target_pairs={{0,16},{8,24},{16,0},{24,8},{1,17},{9,25},{17,1},{25,9},{2,18},{10... | collective-permute-start | bytes 393224 | tf_op jit(solution)/shard_map/ppermute | solution.py:207
  87.6 1.9 %copy-start.5 = (f16[62,64,512]{2,1,0:T(8,128)(2,1)}, f16[62,64,512]{2,1,0:T(8,128)(2,1)S(1)}, u32[]{:S(2)}) copy-start(f16[62,64,512]{2,1,0:T(8,128)(2,1)S(1)} %all-gather.2) | copy-start | bytes 12189700
  90.1 17.9 %copy-start.2 = (bf16[256,464]{0,1:T(8,128)(2,1)S(1)}, bf16[256,464]{0,1:T(8,128)(2,1)}, u32[]{:S(2)}) copy-start(bf16[256,464]{0,1:T(8,128)(2,1)} %param.6) | copy-start | bytes 712708
  92.5 15.4 %copy-start = (bf16[4096,464]{0,1:T(8,128)(2,1)S(1)}, bf16[4096,464]{0,1:T(8,128)(2,1)}, u32[]{:S(2)}) copy-start(bf16[4096,464]{0,1:T(8,128)(2,1)} %param.7) | copy-start | bytes 11403268
  92.6 15.4 %copy-start.1 = (bf16[256,464]{0,1:T(8,128)(2,1)S(1)}, bf16[256,464]{0,1:T(8,128)(2,1)}, u32[]{:S(2)}) copy-start(bf16[256,464]{0,1:T(8,128)(2,1)} %param.5) | copy-start | bytes 712708
  95.0 17.9 %collective-permute-start.2 = (bf16[464,128]{1,0:T(8,128)(2,1)S(1)}, bf16[464,128]{1,0:T(8,128)(2,1)S(1)}, u32[]{:S(2)}, u32[]{:S(2)}) collective-permute-start(bf16[464,128]{1,0:T(8,128)(2,1)S(1)} %slice.52), channel_id=1, source_target_pairs={{0,512},{512,0},{1,513},{513,1},{2,514},{514,2},{3,515},{515,3},{4... | collective-permute-start | bytes 356360 | tf_op jit(solution)/shard_map/ppermute | solution.py:207

commit v9 on v8

--- a/solution.py
+++ b/solution.py
@@ -6,7 +6,7 @@
 from jax.sharding import Mesh, PartitionSpec as P
 
 
-AXES = ("zh", "x", "c", "zl", "y")
+AXES = ("zh", "x", "c", "zl2", "zl1", "y")
 STEPS = (64.0, 32.0, 16.0, 8.0, 4.0, 2.0)
 
 
@@ -33,43 +33,51 @@
     return power(k, 1), k
 
 
-def own_kernel(pair_ref, far_ref, out_ref, k_ref):
-    x, zl = lax.axis_index("x"), lax.axis_index("zl")
-    turns = (pair_ref.at[0], pair_ref.at[1], far_ref.at[0], far_ref.at[1])
-    most = None
-    for ref in turns:
-        for n in range(32):
-            value = jnp.abs(ref[:, 128 * n : 128 * (n + 1)].astype(jnp.float32))
-            most = value if most is None else jnp.maximum(most, value)
-    scale, k = scales_of(most)
-    k_ref[...] = jnp.broadcast_to(k[None], (1, 8, 512)).astype(jnp.bfloat16)
-    for turn, ref in enumerate(turns):
-        place = lax.bitwise_xor(zl, turn)
+def pack_kernel(own_ref, near_ref, rows_ref, out_ref):
+    x = lax.axis_index("x")
+    for turn, ref in enumerate((own_ref, near_ref)):
         for s in range(1, 8):
             for z in range(2):
                 at = pl.multiple_of(2048 * z + 256 * lax.bitwise_xor(x, s), 256)
-                value = (ref[:, pl.ds(at, 256)].astype(jnp.float32) * scale).astype(jnp.bfloat16)
-                out_ref[4 * (s - 1) + place, :, 256 * z : 256 * (z + 1)] = value
-
-
-def rows_kernel(rows_ref, out_ref, k_ref):
+                out_ref[7 * turn + s - 1, :, 256 * z : 256 * (z + 1)] = ref[:, pl.ds(at, 256)]
+    out_ref[14:] = rows_ref[...]
+
+
+def code_kernel(here_ref, far_ref, out_ref):
+    zl2, zl1 = lax.axis_index("zl2"), lax.axis_index("zl1")
+    sides = ((here_ref, 2 * zl2), (far_ref, 2 * (1 - zl2)))
+    most = None
+    for ref, _ in sides:
+        for b in range(4):
+            value = jnp.max(jnp.abs(ref[:14, :, 128 * b : 128 * (b + 1)].astype(jnp.float32)), axis=0)
+            most = value if most is None else jnp.maximum(most, value)
+    scale, k = scales_of(most)
+    out_ref[60] = jnp.broadcast_to(k, (8, 512)).astype(jnp.bfloat16)
+    for ref, first in sides:
+        for turn in range(2):
+            place = first + lax.bitwise_xor(zl1, turn)
+            for s in range(7):
+                out_ref[4 * s + place] = (ref[7 * turn + s].astype(jnp.float32) * scale).astype(jnp.bfloat16)
     for b in range(4):
         cols = slice(128 * b, 128 * (b + 1))
-        most = jnp.max(jnp.abs(rows_ref[:, :, cols].astype(jnp.float32)), axis=0)
-        scale, k = scales_of(most)
-        k_ref[0, :, cols] = jnp.broadcast_to(k, (8, 128)).astype(jnp.bfloat16)
-        out_ref[:, :, cols] = (rows_ref[:, :, cols].astype(jnp.float32) * scale[None]).astype(jnp.bfloat16)
-
-
-def scaled(kernel, blocks, ks, *rows):
+        values = [ref[14:, :, cols].astype(jnp.float32) for ref, _ in sides]
+        scale, k = scales_of(jnp.max(jnp.maximum(jnp.abs(values[0]), jnp.abs(values[1])), axis=0))
+        out_ref[61, :, cols] = jnp.broadcast_to(k, (8, 128)).astype(jnp.bfloat16)
+        for value, (_, first) in zip(values, sides):
+            for x in range(8):
+                for i in range(2):
+                    out_ref[28 + 4 * x + first + i, :, cols] = (value[2 * x + i] * scale).astype(jnp.bfloat16)
+
+
+def in_vmem(kernel, blocks, *args):
     return pl.pallas_call(
         kernel,
-        out_shape=(jax.ShapeDtypeStruct((blocks, 8, 512), jnp.bfloat16), jax.ShapeDtypeStruct((ks, 8, 512), jnp.bfloat16)),
-        in_specs=[pl.BlockSpec(memory_space=pltpu.VMEM)] * len(rows),
-        out_specs=(pl.BlockSpec(memory_space=pltpu.VMEM),) * 2,
+        out_shape=jax.ShapeDtypeStruct((blocks, 8, 512), jnp.bfloat16),
+        in_specs=[pl.BlockSpec(memory_space=pltpu.VMEM)] * len(args),
+        out_specs=pl.BlockSpec(memory_space=pltpu.VMEM),
         cost_estimate=pl.CostEstimate(flops=1_000_000, bytes_accessed=600_000, transcendentals=0),
         compiler_params=pltpu.CompilerParams(vmem_limit_bytes=4 << 20),
-    )(*rows)
+    )(*args)
 
 
 def hidden_kernel(gate_ref, up_ref, out_ref, gate_in, up_in, done, in_sem, out_sem):
@@ -116,8 +124,8 @@
             for j, z in enumerate((1 - zh, zh)):
                 at = pl.multiple_of(2048 * z + 256 * x + 128 * core, 128)
                 piece = g_ref[:, pl.ds(at, 128)]
-                for zl in range(4):
-                    held[4 * x + zl, :, 256 * i + 128 * j : 256 * i + 128 * (j + 1)] = piece
+                for zl in range(2):
+                    held[2 * x + zl, :, 256 * i + 128 * j : 256 * i + 128 * (j + 1)] = piece
     copy = pltpu.make_async_copy(held, out_ref, sem)
     copy.start()
     copy.wait()
@@ -126,10 +134,10 @@
 def split_rows(g):
     return pl.pallas_call(
         split_kernel,
-        out_shape=jax.ShapeDtypeStruct((32, 8, 512), jnp.bfloat16),
+        out_shape=jax.ShapeDtypeStruct((16, 8, 512), jnp.bfloat16),
         in_specs=[pl.BlockSpec(memory_space=pltpu.VMEM)],
         out_specs=pl.BlockSpec(memory_space=pl.ANY),
-        scratch_shapes=[pltpu.VMEM((32, 8, 512), jnp.bfloat16), pltpu.SemaphoreType.DMA],
+        scratch_shapes=[pltpu.VMEM((16, 8, 512), jnp.bfloat16), pltpu.SemaphoreType.DMA],
         compiler_params=pltpu.CompilerParams(vmem_limit_bytes=2 << 20),
         name="split_rows",
     )(g)
@@ -212,16 +220,14 @@
     _, t = gate_t.shape
 
     pieces = split_rows(grad_out)
-    mine = lax.all_to_all(pieces, ("x", "zl"), 0, 0)
-    near = turned(grad_out, "zl", 1)
-    pair = jnp.stack([grad_out, near])
-    far = turned(pair, "zl", 2)
+    mine = lax.all_to_all(pieces, ("x", "zl1"), 0, 0)
+    near = turned(grad_out, "zl1", 1)
     copies = hidden_copies(gate_t, up_t)
+    packed = in_vmem(pack_kernel, 30, grad_out, near, mine)
+    far = turned(packed, "zl2", 1)
     hiddens = lax.all_to_all(copies, "x", 0, 0)
 
-    own, own_k = scaled(own_kernel, 28, 1, pair, far)
-    rows, rows_k = scaled(rows_kernel, 32, 1, mine)
-    message = jnp.concatenate([own, rows, own_k, rows_k], 0).astype(jnp.float16)
+    message = in_vmem(code_kernel, 62, packed, far).astype(jnp.float16)
     got = lax.all_gather(message, "y", axis=1, tiled=True)
 
     scale = power(got[60:].astype(jnp.float32), -1)
@@ -240,9 +246,9 @@
 
 
 def solution(mesh):
-    dims = (2, 8, 2, 4, 8)
+    dims = (2, 8, 2, 2, 2, 8)
     fine = Mesh(mesh.devices.reshape(dims), AXES)
-    dp, tensor = ("zh", "x", "c"), ("zl", "y")
+    dp, tensor = ("zh", "x", "c"), ("zl2", "zl1", "y")
     in_specs = (P(dp + tensor, None), P(dp, tensor), P(dp, tensor), P(None, tensor))
     out_specs = (P(dp, tensor), P(dp, tensor), P(dp, tensor))
     return jax.shard_map(sections, mesh=fine, in_specs=in_specs, out_specs=out_specs, check_vma=False)

time: 114 us -> 120 us (1.053)
  the two profiles are of different devices: /device:TPU:16 before, /device:TPU:6 now
where the time goes in v9:
time: 120 us
  blocking collectives  45.2 us (38%)
  starting transfers between devices  40.1 us (33%)
  waiting for transfers between devices  20.4 us (17%)
  Pallas kernels  8.06 us (7%)
  other arithmetic  3.1 us (3%)
  local copies, waits for them, and re-layouts  2.21 us (2%)
    all_gather x1, blocking collectives, sections(): got = lax.all_gather(message, 'y', axis=1, tiled=True)  43 us
    all_to_all x1, starting transfers between devices, sections(): mine = lax.all_to_all(pieces, ('x', 'zl1'), 0, 0)  16.4 us
    ppermute x3, starting transfers between devices, turned(): lax.ppermute(x, axis, [(i, i ^ by) for i in range(lax.axis_size(axis))])  16.2 us
    ppermute x3, waiting for transfers between devices, turned(): lax.ppermute(x, axis, [(i, i ^ by) for i in range(lax.axis_size(axis))])  16.2 us
    all_to_all x1, starting transfers between devices, sections(): hiddens = lax.all_to_all(copies, 'x', 0, 0)  7.38 us
    all_to_all x1, waiting for transfers between devices, sections(): mine = lax.all_to_all(pieces, ('x', 'zl1'), 0, 0)  4.2 us
    pallas_call x1, Pallas kernels, hidden_copies(): pl.pallas_call(hidden_kernel, out_shape=jax.ShapeDtypeStruct((8, h, t), j...  2.53 us
    pallas_call x1, Pallas kernels, weight_parts(): pl.pallas_call(weights_kernel, out_shape=(jax.ShapeDtypeStruct((h, 256),...  2.48 us
  transfers between devices with their start and end apart: 5, of which 4 were waited for; matrix products, arithmetic and copies ran while one was open for 2% of the time, Pallas kernels for 4%

profile of v9, /device:TPU:6, one launch (start us, length us, event | category | flops | bytes accessed | tf_op | source)
XLA Modules:
  0.0 119.9 jit_solution(6371631889259193462)
XLA Ops:
  0.6 0.0 copy-start.3
  0.6 0.8 copy-done.3
  1.5 0.7 split_rows.1
  2.2 16.4 %all-to-all-start.1 = ((bf16[16,8,512]{2,1,0:T(8,128)(2,1)}), bf16[16,8,512]{2,1,0:T(8,128)(2,1)S(1)}, u32[]{:S(2)}, u32[]{:S(2)}) async-start(bf16[16,8,512]{2,1,0:T(8,128)(2,1)} %split_rows.1), calls=%async_computation.1 | async-start | bytes 262144 | tf_op jit(solution)/shard_map/all_to_all | solution.py:223
  18.6 0.0 copy-start.4
  18.6 2.5 %hidden_copies.1 = bf16[8,464,256]{2,1,0:T(8,128)(2,1)} custom-call(bf16[464,256]{1,0:T(8,128)(2,1)} %bitcast.23, bf16[464,256]{1,0:T(8,128)(2,1)} %bitcast.25), custom_call_target="tpu_custom_call" | custom-call | flops 2000000 | bytes 2375680 | tf_op jit(solution)/shard_map/hidden_copies/pallas_call | solution.py:108
  21.2 4.2 %all-to-all-done.1.rows_ref = bf16[16,8,512]{2,1,0:T(8,128)(2,1)S(1)} async-done(((bf16[16,8,512]{2,1,0:T(8,128)(2,1)}), bf16[16,8,512]{2,1,0:T(8,128)(2,1)S(1)}, u32[]{:S(2)}, u32[]{:S(2)}) %all-to-all-start.1) | async-done | bytes 131104 | tf_op jit(solution)/shard_map/all_to_all | solution.py:223
  25.4 7.4 %all-to-all-start = ((bf16[8,464,256]{2,1,0:T(8,128)(2,1)}), bf16[8,464,256]{2,1,0:T(8,128)(2,1)}, u32[]{:S(2)}, u32[]{:S(2)}) async-start(bf16[8,464,256]{2,1,0:T(8,128)(2,1)} %hidden_copies.1), calls=%async_computation | async-start | bytes 3801088 | tf_op jit(solution)/shard_map/all_to_all | solution.py:228
  32.7 0.0 copy-done.4
  32.7 2.4 %collective-permute-start = (bf16[8,4096]{1,0:T(8,128)(2,1)S(1)}, bf16[8,4096]{1,0:T(8,128)(2,1)S(1)}, u32[]{:S(2)}, u32[]{:S(2)}) collective-permute-start(bf16[8,4096]{1,0:T(8,128)(2,1)S(1)} %copy-done.4), channel_id=1, source_target_pairs={{0,8},{8,0},{1,9},{9,1},{2,10},{10,2},{3,11},{11,3},{4,12},{12,4},... | collective-permute-start | bytes 196616 | tf_op jit(solution)/shard_map/ppermute | solution.py:215
  35.2 3.8 %collective-permute-done.near_ref = bf16[8,4096]{1,0:T(8,128)(2,1)S(1)} collective-permute-done((bf16[8,4096]{1,0:T(8,128)(2,1)S(1)}, bf16[8,4096]{1,0:T(8,128)(2,1)S(1)}, u32[]{:S(2)}, u32[]{:S(2)}) %collective-permute-start) | collective-permute-done | bytes 65568 | tf_op jit(solution)/shard_map/ppermute | solution.py:215
  39.0 1.9 %collective-permute-start.1 = (bf16[30,8,512]{2,1,0:T(8,128)(2,1)S(1)}, bf16[30,8,512]{2,1,0:T(8,128)(2,1)S(1)}, u32[]{:S(2)}, u32[]{:S(2)}) collective-permute-start(bf16[30,8,512]{2,1,0:T(8,128)(2,1)S(1)} %shard_map.67.here_ref), channel_id=1, source_target_pairs={{0,16},{16,0},{1,17},{17,1},{2,18},{18,2},{3,19},{19,3},{4,20},{20... | collective-permute-start | bytes 737288 | tf_op jit(solution)/shard_map/ppermute | solution.py:215
  41.0 9.6 %collective-permute-done.1.far_ref = bf16[30,8,512]{2,1,0:T(8,128)(2,1)S(1)} collective-permute-done((bf16[30,8,512]{2,1,0:T(8,128)(2,1)S(1)}, bf16[30,8,512]{2,1,0:T(8,128)(2,1)S(1)}, u32[]{:S(2)}, u32[]{:S(2)}) %collective-permute-start.1) | collective-permute-done | bytes 245792 | tf_op jit(solution)/shard_map/ppermute | solution.py:215
  50.5 0.3 shard_map.68
  50.8 0.1 convert_element_type.37
  50.9 43.0 %all-gather.2 = f16[62,64,512]{2,1,0:T(8,128)(2,1)S(1)} all-gather(f16[62,8,512]{2,1,0:T(8,128)(2,1)S(1)} %convert_element_type.37), channel_id=1, replica_groups=mesh['zh'=2,'x'=8,'c'=2,'zl2'=2,'zl1'=2,'y'=8] {'y'}, dimensions={1}, use_global_device_ids=true | all-gather | bytes 4571136 | tf_op jit(solution)/shard_map/all_gather | solution.py:231
  93.8 0.0 copy-start.5
  93.8 0.2 multiply_select_fusion
  94.1 0.3 multiply_convert_fusion.1
  94.4 1.3 %copy-done.5 = f16[62,64,512]{2,1,0:T(8,128)(2,1)} copy-done((f16[62,64,512]{2,1,0:T(8,128)(2,1)}, f16[62,64,512]{2,1,0:T(8,128)(2,1)S(1)}, u32[]{:S(2)}) %copy-start.5) | copy-done | bytes 4063256
  95.7 0.5 multiply_convert_fusion
  96.3 0.0 all-to-all-done.hidden_ref
  96.3 0.0 copy-start.2
  96.3 2.5 %weight_parts.1 = (f32[464,256]{1,0:T(8,128)S(1)}, f32[464,256]{1,0:T(8,128)S(1)}) custom-call(bf16[8,464,256]{2,1,0:T(8,128)(2,1)} %all-to-all-done.hidden_ref, bf16[2048,512]{1,0:T(8,128)(2,1)S(1)} %bitcast.18), custom_call_target="tpu_custom_call" | custom-call | flops 973078528 | bytes 4000000 | tf_op jit(solution)/shard_map/weight_parts/pallas_call | solution.py:162
  98.8 0.0 copy-start
  98.8 0.0 copy-start.1
  98.9 2.3 %all-gather = bf16[928,256]{1,0:T(8,128)(2,1)S(1)} all-gather(bf16[464,256]{1,0:T(8,128)(2,1)S(1)} %convert_element_type.41), channel_id=2, replica_groups=mesh['zh'=2,'x'=8,'c'=2,'zl2'=2,'zl1'=2,'y'=8] {'c'}, dimensions={0}, use_global_device_ids=true | all-gather | bytes 712704 | tf_op jit(solution)/shard_map/all_gather | solution.py:239
  101.2 11.9 %collective-permute-start.2 = (bf16[464,128]{1,0:T(8,128)(2,1)S(1)}, bf16[464,128]{1,0:T(8,128)(2,1)S(1)}, u32[]{:S(2)}, u32[]{:S(2)}) collective-permute-start(bf16[464,128]{1,0:T(8,128)(2,1)S(1)} %slice.52), channel_id=1, source_target_pairs={{0,512},{512,0},{1,513},{513,1},{2,514},{514,2},{3,515},{515,3},{4... | collective-permute-start | bytes 356360 | tf_op jit(solution)/shard_map/ppermute | solution.py:215
  113.1 1.1 multiply_convert_fusion.2
  114.2 0.0 copy-done.2
  114.2 0.0 copy-done
  114.2 0.0 copy-done.1
  114.3 2.1 %input_grads.1 = (bf16[464,256]{1,0:T(8,128)(2,1)}, bf16[464,256]{1,0:T(8,128)(2,1)}) custom-call(bf16[5,256,512]{2,1,0:T(8,128)(2,1)S(1)} %bitcast.20, bf16[2,256,512]{2,1,0:T(8,128)(2,1)S(1)} %bitcast.22, bf16[2048,512]{1,0:T(8,128)(2,1)S(1)} %bitcast.19, bf16[464,4096]{1,0:T(8,128)(2,1)S(1)} %bitcast.21, bf16[464,256]{1,0:T(8,128)(2,1)S(1)} %bitcast.24, ...), custom_call_target="tpu_custom_call" | custom-call | flops 973078528 | bytes 6000000 | tf_op jit(solution)/shard_map/input_grads/pallas_call | solution.py:202
  116.3 2.8 %collective-permute-done.2 = bf16[464,128]{1,0:T(8,128)(2,1)S(1)} collective-permute-done((bf16[464,128]{1,0:T(8,128)(2,1)S(1)}, bf16[464,128]{1,0:T(8,128)(2,1)S(1)}, u32[]{:S(2)}, u32[]{:S(2)}) %collective-permute-start.2) | collective-permute-done | bytes 118816 | tf_op jit(solution)/shard_map/ppermute | solution.py:215
  119.2 0.7 fusion.1
  (5 shorter events, 0.1 us)
Async XLA Ops:
  0.6 0.8 copy-start.3
  2.2 23.2 %all-to-all-start.1 = ((bf16[16,8,512]{2,1,0:T(8,128)(2,1)}), bf16[16,8,512]{2,1,0:T(8,128)(2,1)S(1)}, u32[]{:S(2)}, u32[]{:S(2)}) async-start(bf16[16,8,512]{2,1,0:T(8,128)(2,1)} %split_rows.1), calls=%async_computation.1 | async-start | bytes 262144 | tf_op jit(solution)/shard_map/all_to_all | solution.py:223
  18.6 14.1 %copy-start.4 = (bf16[8,4096]{1,0:T(8,128)(2,1)S(1)}, bf16[8,4096]{1,0:T(8,128)(2,1)}, u32[]{:S(2)}) copy-start(bf16[8,4096]{1,0:T(8,128)(2,1)} %own_ref.1) | copy-start | bytes 196612
  25.4 70.9 %all-to-all-start = ((bf16[8,464,256]{2,1,0:T(8,128)(2,1)}), bf16[8,464,256]{2,1,0:T(8,128)(2,1)}, u32[]{:S(2)}, u32[]{:S(2)}) async-start(bf16[8,464,256]{2,1,0:T(8,128)(2,1)} %hidden_copies.1), calls=%async_computation | async-start | bytes 3801088 | tf_op jit(solution)/shard_map/all_to_all | solution.py:228
  32.7 6.3 %collective-permute-start = (bf16[8,4096]{1,0:T(8,128)(2,1)S(1)}, bf16[8,4096]{1,0:T(8,128)(2,1)S(1)}, u32[]{:S(2)}, u32[]{:S(2)}) collective-permute-start(bf16[8,4096]{1,0:T(8,128)(2,1)S(1)} %copy-done.4), channel_id=1, source_target_pairs={{0,8},{8,0},{1,9},{9,1},{2,10},{10,2},{3,11},{11,3},{4,12},{12,4},... | collective-permute-start | bytes 196616 | tf_op jit(solution)/shard_map/ppermute | solution.py:215
  39.0 11.5 %collective-permute-start.1 = (bf16[30,8,512]{2,1,0:T(8,128)(2,1)S(1)}, bf16[30,8,512]{2,1,0:T(8,128)(2,1)S(1)}, u32[]{:S(2)}, u32[]{:S(2)}) collective-permute-start(bf16[30,8,512]{2,1,0:T(8,128)(2,1)S(1)} %shard_map.67.here_ref), channel_id=1, source_target_pairs={{0,16},{16,0},{1,17},{17,1},{2,18},{18,2},{3,19},{19,3},{4,20},{20... | collective-permute-start | bytes 737288 | tf_op jit(solution)/shard_map/ppermute | solution.py:215
  93.8 1.9 %copy-start.5 = (f16[62,64,512]{2,1,0:T(8,128)(2,1)}, f16[62,64,512]{2,1,0:T(8,128)(2,1)S(1)}, u32[]{:S(2)}) copy-start(f16[62,64,512]{2,1,0:T(8,128)(2,1)S(1)} %all-gather.2) | copy-start | bytes 12189700
  96.3 17.9 %copy-start.2 = (bf16[256,464]{0,1:T(8,128)(2,1)S(1)}, bf16[256,464]{0,1:T(8,128)(2,1)}, u32[]{:S(2)}) copy-start(bf16[256,464]{0,1:T(8,128)(2,1)} %param.6) | copy-start | bytes 712708
  98.8 15.4 %copy-start = (bf16[4096,464]{0,1:T(8,128)(2,1)S(1)}, bf16[4096,464]{0,1:T(8,128)(2,1)}, u32[]{:S(2)}) copy-start(bf16[4096,464]{0,1:T(8,128)(2,1)} %param.7) | copy-start | bytes 11403268
  98.8 15.4 %copy-start.1 = (bf16[256,464]{0,1:T(8,128)(2,1)S(1)}, bf16[256,464]{0,1:T(8,128)(2,1)}, u32[]{:S(2)}) copy-start(bf16[256,464]{0,1:T(8,128)(2,1)} %param.5) | copy-start | bytes 712708
  101.2 17.9 %collective-permute-start.2 = (bf16[464,128]{1,0:T(8,128)(2,1)S(1)}, bf16[464,128]{1,0:T(8,128)(2,1)S(1)}, u32[]{:S(2)}, u32[]{:S(2)}) collective-permute-start(bf16[464,128]{1,0:T(8,128)(2,1)S(1)} %slice.52), channel_id=1, source_target_pairs={{0,512},{512,0},{1,513},{513,1},{2,514},{514,2},{3,515},{515,3},{4... | collective-permute-start | bytes 356360 | tf_op jit(solution)/shard_map/ppermute | solution.py:215

commit v10 on v9

--- a/solution.py
+++ b/solution.py
@@ -45,7 +45,7 @@
 
 def code_kernel(here_ref, far_ref, out_ref):
     zl2, zl1 = lax.axis_index("zl2"), lax.axis_index("zl1")
-    sides = ((here_ref, 2 * zl2), (far_ref, 2 * (1 - zl2)))
+    sides = ((here_ref, zl1), (far_ref, 1 - zl1))
     most = None
     for ref, _ in sides:
         for b in range(4):
@@ -55,7 +55,7 @@
     out_ref[60] = jnp.broadcast_to(k, (8, 512)).astype(jnp.bfloat16)
     for ref, first in sides:
         for turn in range(2):
-            place = first + lax.bitwise_xor(zl1, turn)
+            place = first + 2 * lax.bitwise_xor(zl2, turn)
             for s in range(7):
                 out_ref[4 * s + place] = (ref[7 * turn + s].astype(jnp.float32) * scale).astype(jnp.bfloat16)
     for b in range(4):
@@ -66,7 +66,7 @@
         for value, (_, first) in zip(values, sides):
             for x in range(8):
                 for i in range(2):
-                    out_ref[28 + 4 * x + first + i, :, cols] = (value[2 * x + i] * scale).astype(jnp.bfloat16)
+                    out_ref[28 + 4 * x + first + 2 * i, :, cols] = (value[2 * x + i] * scale).astype(jnp.bfloat16)
 
 
 def in_vmem(kernel, blocks, *args):
@@ -220,11 +220,11 @@
     _, t = gate_t.shape
 
     pieces = split_rows(grad_out)
-    mine = lax.all_to_all(pieces, ("x", "zl1"), 0, 0)
-    near = turned(grad_out, "zl1", 1)
+    mine = lax.all_to_all(pieces, ("x", "zl2"), 0, 0)
+    near = turned(grad_out, "zl2", 1)
     copies = hidden_copies(gate_t, up_t)
     packed = in_vmem(pack_kernel, 30, grad_out, near, mine)
-    far = turned(packed, "zl2", 1)
+    far = turned(packed, "zl1", 1)
     hiddens = lax.all_to_all(copies, "x", 0, 0)
 
     message = in_vmem(code_kernel, 62, packed, far).astype(jnp.float16)

time: 120 us -> 115 us (0.958)
  the two profiles are of different devices: /device:TPU:6 before, /device:TPU:135 now
where the time goes in v10:
time: 115 us
  blocking collectives  48.9 us (43%)
  starting transfers between devices  34.5 us (30%)
  waiting for transfers between devices  17 us (15%)
  Pallas kernels  8.07 us (7%)
  other arithmetic  3.11 us (3%)
  local copies, waits for them, and re-layouts  2.21 us (2%)
    all_gather x1, blocking collectives, sections(): got = lax.all_gather(message, 'y', axis=1, tiled=True)  42.6 us
    ppermute x3, starting transfers between devices, turned(): lax.ppermute(x, axis, [(i, i ^ by) for i in range(lax.axis_size(axis))])  15.6 us
    ppermute x3, waiting for transfers between devices, turned(): lax.ppermute(x, axis, [(i, i ^ by) for i in range(lax.axis_size(axis))])  12.5 us
    all_to_all x1, starting transfers between devices, sections(): mine = lax.all_to_all(pieces, ('x', 'zl2'), 0, 0)  12.1 us
    all_to_all x1, starting transfers between devices, sections(): hiddens = lax.all_to_all(copies, 'x', 0, 0)  6.71 us
    all_gather x1, blocking collectives, sections(): swap = lax.all_gather(theirs.astype(jnp.bfloat16), 'c', axis=0)  6.35 us
    all_to_all x1, waiting for transfers between devices, sections(): mine = lax.all_to_all(pieces, ('x', 'zl2'), 0, 0)  4.5 us
    pallas_call x1, Pallas kernels, hidden_copies(): pl.pallas_call(hidden_kernel, out_shape=jax.ShapeDtypeStruct((8, h, t), j...  2.53 us
  transfers between devices with their start and end apart: 5, of which 4 were waited for; matrix products, arithmetic and copies ran while one was open for 2% of the time, Pallas kernels for 4%

profile of v10, /device:TPU:135, one launch (start us, length us, event | category | flops | bytes accessed | tf_op | source)
XLA Modules:
  0.0 114.6 jit_solution(3381124238109519270)
XLA Ops:
  0.6 0.0 copy-start.3
  0.6 0.8 copy-done.3
  1.5 0.7 split_rows.1
  2.2 12.1 %all-to-all-start.1 = ((bf16[16,8,512]{2,1,0:T(8,128)(2,1)}), bf16[16,8,512]{2,1,0:T(8,128)(2,1)S(1)}, u32[]{:S(2)}, u32[]{:S(2)}) async-start(bf16[16,8,512]{2,1,0:T(8,128)(2,1)} %split_rows.1), calls=%async_computation.1 | async-start | bytes 262144 | tf_op jit(solution)/shard_map/all_to_all | solution.py:223
  14.3 0.0 copy-start.4
  14.3 2.5 %hidden_copies.1 = bf16[8,464,256]{2,1,0:T(8,128)(2,1)} custom-call(bf16[464,256]{1,0:T(8,128)(2,1)} %bitcast.23, bf16[464,256]{1,0:T(8,128)(2,1)} %bitcast.25), custom_call_target="tpu_custom_call" | custom-call | flops 2000000 | bytes 2375680 | tf_op jit(solution)/shard_map/hidden_copies/pallas_call | solution.py:108
  16.9 4.5 %all-to-all-done.1.rows_ref = bf16[16,8,512]{2,1,0:T(8,128)(2,1)S(1)} async-done(((bf16[16,8,512]{2,1,0:T(8,128)(2,1)}), bf16[16,8,512]{2,1,0:T(8,128)(2,1)S(1)}, u32[]{:S(2)}, u32[]{:S(2)}) %all-to-all-start.1) | async-done | bytes 131104 | tf_op jit(solution)/shard_map/all_to_all | solution.py:223
  21.4 6.7 %all-to-all-start = ((bf16[8,464,256]{2,1,0:T(8,128)(2,1)}), bf16[8,464,256]{2,1,0:T(8,128)(2,1)}, u32[]{:S(2)}, u32[]{:S(2)}) async-start(bf16[8,464,256]{2,1,0:T(8,128)(2,1)} %hidden_copies.1), calls=%async_computation | async-start | bytes 3801088 | tf_op jit(solution)/shard_map/all_to_all | solution.py:228
  28.1 0.0 copy-done.4
  28.1 2.1 %collective-permute-start = (bf16[8,4096]{1,0:T(8,128)(2,1)S(1)}, bf16[8,4096]{1,0:T(8,128)(2,1)S(1)}, u32[]{:S(2)}, u32[]{:S(2)}) collective-permute-start(bf16[8,4096]{1,0:T(8,128)(2,1)S(1)} %copy-done.4), channel_id=1, source_target_pairs={{0,16},{16,0},{1,17},{17,1},{2,18},{18,2},{3,19},{19,3},{4,20},{20... | collective-permute-start | bytes 196616 | tf_op jit(solution)/shard_map/ppermute | solution.py:215
  30.2 4.2 %collective-permute-done.near_ref = bf16[8,4096]{1,0:T(8,128)(2,1)S(1)} collective-permute-done((bf16[8,4096]{1,0:T(8,128)(2,1)S(1)}, bf16[8,4096]{1,0:T(8,128)(2,1)S(1)}, u32[]{:S(2)}, u32[]{:S(2)}) %collective-permute-start) | collective-permute-done | bytes 65568 | tf_op jit(solution)/shard_map/ppermute | solution.py:215
  34.4 1.9 %collective-permute-start.1 = (bf16[30,8,512]{2,1,0:T(8,128)(2,1)S(1)}, bf16[30,8,512]{2,1,0:T(8,128)(2,1)S(1)}, u32[]{:S(2)}, u32[]{:S(2)}) collective-permute-start(bf16[30,8,512]{2,1,0:T(8,128)(2,1)S(1)} %shard_map.67.here_ref), channel_id=1, source_target_pairs={{0,8},{8,0},{1,9},{9,1},{2,10},{10,2},{3,11},{11,3},{4,12},{12,4},... | collective-permute-start | bytes 737288 | tf_op jit(solution)/shard_map/ppermute | solution.py:215
  36.3 5.4 %collective-permute-done.1.far_ref = bf16[30,8,512]{2,1,0:T(8,128)(2,1)S(1)} collective-permute-done((bf16[30,8,512]{2,1,0:T(8,128)(2,1)S(1)}, bf16[30,8,512]{2,1,0:T(8,128)(2,1)S(1)}, u32[]{:S(2)}, u32[]{:S(2)}) %collective-permute-start.1) | collective-permute-done | bytes 245792 | tf_op jit(solution)/shard_map/ppermute | solution.py:215
  41.7 0.3 shard_map.68
  42.0 0.1 convert_element_type.37
  42.1 42.6 %all-gather.2 = f16[62,64,512]{2,1,0:T(8,128)(2,1)S(1)} all-gather(f16[62,8,512]{2,1,0:T(8,128)(2,1)S(1)} %convert_element_type.37), channel_id=1, replica_groups=mesh['zh'=2,'x'=8,'c'=2,'zl2'=2,'zl1'=2,'y'=8] {'y'}, dimensions={1}, use_global_device_ids=true | all-gather | bytes 4571136 | tf_op jit(solution)/shard_map/all_gather | solution.py:231
  84.7 0.0 copy-start.5
  84.7 0.2 multiply_select_fusion
  84.9 0.3 multiply_convert_fusion.1
  85.3 1.3 %copy-done.5 = f16[62,64,512]{2,1,0:T(8,128)(2,1)} copy-done((f16[62,64,512]{2,1,0:T(8,128)(2,1)}, f16[62,64,512]{2,1,0:T(8,128)(2,1)S(1)}, u32[]{:S(2)}) %copy-start.5) | copy-done | bytes 4063256
  86.6 0.5 multiply_convert_fusion
  87.1 0.0 all-to-all-done.hidden_ref
  87.1 0.0 copy-start.2
  87.1 2.5 %weight_parts.1 = (f32[464,256]{1,0:T(8,128)S(1)}, f32[464,256]{1,0:T(8,128)S(1)}) custom-call(bf16[8,464,256]{2,1,0:T(8,128)(2,1)} %all-to-all-done.hidden_ref, bf16[2048,512]{1,0:T(8,128)(2,1)S(1)} %bitcast.18), custom_call_target="tpu_custom_call" | custom-call | flops 973078528 | bytes 4000000 | tf_op jit(solution)/shard_map/weight_parts/pallas_call | solution.py:162
  89.6 0.0 copy-start
  89.6 0.0 copy-start.1
  89.7 6.4 %all-gather = bf16[928,256]{1,0:T(8,128)(2,1)S(1)} all-gather(bf16[464,256]{1,0:T(8,128)(2,1)S(1)} %convert_element_type.41), channel_id=2, replica_groups=mesh['zh'=2,'x'=8,'c'=2,'zl2'=2,'zl1'=2,'y'=8] {'c'}, dimensions={0}, use_global_device_ids=true | all-gather | bytes 712704 | tf_op jit(solution)/shard_map/all_gather | solution.py:239
  96.0 0.1 convert_add_fusion
  96.1 11.6 %collective-permute-start.2 = (bf16[464,128]{1,0:T(8,128)(2,1)S(1)}, bf16[464,128]{1,0:T(8,128)(2,1)S(1)}, u32[]{:S(2)}, u32[]{:S(2)}) collective-permute-start(bf16[464,128]{1,0:T(8,128)(2,1)S(1)} %slice.52), channel_id=1, source_target_pairs={{0,512},{512,0},{1,513},{513,1},{2,514},{514,2},{3,515},{515,3},{4... | collective-permute-start | bytes 356360 | tf_op jit(solution)/shard_map/ppermute | solution.py:215
  107.7 1.1 multiply_convert_fusion.2
  108.9 0.0 copy-done.2
  108.9 0.0 copy-done
  108.9 0.0 copy-done.1
  108.9 2.1 %input_grads.1 = (bf16[464,256]{1,0:T(8,128)(2,1)}, bf16[464,256]{1,0:T(8,128)(2,1)}) custom-call(bf16[5,256,512]{2,1,0:T(8,128)(2,1)S(1)} %bitcast.20, bf16[2,256,512]{2,1,0:T(8,128)(2,1)S(1)} %bitcast.22, bf16[2048,512]{1,0:T(8,128)(2,1)S(1)} %bitcast.19, bf16[464,4096]{1,0:T(8,128)(2,1)S(1)} %bitcast.21, bf16[464,256]{1,0:T(8,128)(2,1)S(1)} %bitcast.24, ...), custom_call_target="tpu_custom_call" | custom-call | flops 973078528 | bytes 6000000 | tf_op jit(solution)/shard_map/input_grads/pallas_call | solution.py:202
  111.0 3.0 %collective-permute-done.2 = bf16[464,128]{1,0:T(8,128)(2,1)S(1)} collective-permute-done((bf16[464,128]{1,0:T(8,128)(2,1)S(1)}, bf16[464,128]{1,0:T(8,128)(2,1)S(1)}, u32[]{:S(2)}, u32[]{:S(2)}) %collective-permute-start.2) | collective-permute-done | bytes 118816 | tf_op jit(solution)/shard_map/ppermute | solution.py:215
  113.9 0.7 fusion.1
  (4 shorter events, 0.1 us)
Async XLA Ops:
  0.6 0.8 copy-start.3
  2.2 19.2 %all-to-all-start.1 = ((bf16[16,8,512]{2,1,0:T(8,128)(2,1)}), bf16[16,8,512]{2,1,0:T(8,128)(2,1)S(1)}, u32[]{:S(2)}, u32[]{:S(2)}) async-start(bf16[16,8,512]{2,1,0:T(8,128)(2,1)} %split_rows.1), calls=%async_computation.1 | async-start | bytes 262144 | tf_op jit(solution)/shard_map/all_to_all | solution.py:223
  14.3 13.8 %copy-start.4 = (bf16[8,4096]{1,0:T(8,128)(2,1)S(1)}, bf16[8,4096]{1,0:T(8,128)(2,1)}, u32[]{:S(2)}) copy-start(bf16[8,4096]{1,0:T(8,128)(2,1)} %own_ref.1) | copy-start | bytes 196612
  21.4 65.8 %all-to-all-start = ((bf16[8,464,256]{2,1,0:T(8,128)(2,1)}), bf16[8,464,256]{2,1,0:T(8,128)(2,1)}, u32[]{:S(2)}, u32[]{:S(2)}) async-start(bf16[8,464,256]{2,1,0:T(8,128)(2,1)} %hidden_copies.1), calls=%async_computation | async-start | bytes 3801088 | tf_op jit(solution)/shard_map/all_to_all | solution.py:228
  28.1 6.3 %collective-permute-start = (bf16[8,4096]{1,0:T(8,128)(2,1)S(1)}, bf16[8,4096]{1,0:T(8,128)(2,1)S(1)}, u32[]{:S(2)}, u32[]{:S(2)}) collective-permute-start(bf16[8,4096]{1,0:T(8,128)(2,1)S(1)} %copy-done.4), channel_id=1, source_target_pairs={{0,16},{16,0},{1,17},{17,1},{2,18},{18,2},{3,19},{19,3},{4,20},{20... | collective-permute-start | bytes 196616 | tf_op jit(solution)/shard_map/ppermute | solution.py:215
  34.4 7.3 %collective-permute-start.1 = (bf16[30,8,512]{2,1,0:T(8,128)(2,1)S(1)}, bf16[30,8,512]{2,1,0:T(8,128)(2,1)S(1)}, u32[]{:S(2)}, u32[]{:S(2)}) collective-permute-start(bf16[30,8,512]{2,1,0:T(8,128)(2,1)S(1)} %shard_map.67.here_ref), channel_id=1, source_target_pairs={{0,8},{8,0},{1,9},{9,1},{2,10},{10,2},{3,11},{11,3},{4,12},{12,4},... | collective-permute-start | bytes 737288 | tf_op jit(solution)/shard_map/ppermute | solution.py:215
  84.7 1.9 %copy-start.5 = (f16[62,64,512]{2,1,0:T(8,128)(2,1)}, f16[62,64,512]{2,1,0:T(8,128)(2,1)S(1)}, u32[]{:S(2)}) copy-start(f16[62,64,512]{2,1,0:T(8,128)(2,1)S(1)} %all-gather.2) | copy-start | bytes 12189700
  87.1 21.7 %copy-start.2 = (bf16[256,464]{0,1:T(8,128)(2,1)S(1)}, bf16[256,464]{0,1:T(8,128)(2,1)}, u32[]{:S(2)}) copy-start(bf16[256,464]{0,1:T(8,128)(2,1)} %param.6) | copy-start | bytes 712708
  89.6 19.2 %copy-start = (bf16[4096,464]{0,1:T(8,128)(2,1)S(1)}, bf16[4096,464]{0,1:T(8,128)(2,1)}, u32[]{:S(2)}) copy-start(bf16[4096,464]{0,1:T(8,128)(2,1)} %param.7) | copy-start | bytes 11403268
  89.6 19.2 %copy-start.1 = (bf16[256,464]{0,1:T(8,128)(2,1)S(1)}, bf16[256,464]{0,1:T(8,128)(2,1)}, u32[]{:S(2)}) copy-start(bf16[256,464]{0,1:T(8,128)(2,1)} %param.5) | copy-start | bytes 712708
  96.1 17.8 %collective-permute-start.2 = (bf16[464,128]{1,0:T(8,128)(2,1)S(1)}, bf16[464,128]{1,0:T(8,128)(2,1)S(1)}, u32[]{:S(2)}, u32[]{:S(2)}) collective-permute-start(bf16[464,128]{1,0:T(8,128)(2,1)S(1)} %slice.52), channel_id=1, source_target_pairs={{0,512},{512,0},{1,513},{513,1},{2,514},{514,2},{3,515},{515,3},{4... | collective-permute-start | bytes 356360 | tf_op jit(solution)/shard_map/ppermute | solution.py:215

commit v11 on v10

--- a/solution.py
+++ b/solution.py
@@ -171,7 +171,7 @@
     )(hiddens, feats)
 
 
-def inputs_kernel(front_ref, last_ref, feats_ref, weight_ref, gate_ref, up_ref, grad_gate_ref, grad_up_ref, weight, total):
+def input_grads(front_ref, last_ref, feats_ref, weight_ref, gate_ref, up_ref, grads, weight, total, done, sem):
     zh, x, c = lax.axis_index("zh"), lax.axis_index("x"), lax.axis_index("c")
     t = gate_ref.shape[1]
     for n in range(8):
@@ -193,22 +193,49 @@
     gate = gate_ref[...].astype(jnp.float32)
     upper = up_ref[...].astype(jnp.float32)
     sig = jax.nn.sigmoid(gate)
-    grad_up_ref[...] = (grad_hidden * (gate * sig)).astype(jnp.bfloat16)
-    grad_gate_ref[...] = (grad_hidden * upper * sig * (1.0 + gate * (1.0 - sig))).astype(jnp.bfloat16)
-
-
-def input_grads(front, last, feats, weight, gate, up):
-    h, t = gate.shape
-    return pl.pallas_call(
-        inputs_kernel,
-        out_shape=(jax.ShapeDtypeStruct((h, t), jnp.bfloat16),) * 2,
-        in_specs=[pl.BlockSpec(memory_space=pltpu.VMEM)] * 6,
-        out_specs=(pl.BlockSpec(memory_space=pltpu.VMEM),) * 2,
-        scratch_shapes=[pltpu.VMEM((2, h, 512), jnp.bfloat16), pltpu.VMEM((h, t), jnp.float32)],
+    done[0] = (grad_hidden * upper * sig * (1.0 + gate * (1.0 - sig))).astype(jnp.bfloat16)
+    done[1] = (grad_hidden * (gate * sig)).astype(jnp.bfloat16)
+    copies = [pltpu.make_async_copy(done.at[i], grads[i], sem.at[i]) for i in range(2)]
+    for copy in copies:
+        copy.start()
+    for copy in copies:
+        copy.wait()
+
+
+def before_kernel(ours_ref, swap_ref, *refs):
+    inputs, (send_ref, here_ref), grads, scratch = refs[:6], refs[6:8], refs[8:10], refs[10:]
+    other = 1 - lax.axis_index("c")
+    send_ref[...] = (ours_ref[:, :128] + swap_ref[other, :, :128].astype(jnp.float32)).astype(jnp.bfloat16)
+    here_ref[...] = ours_ref[:, 128:] + swap_ref[other, :, 128:].astype(jnp.float32)
+    pl.when(lax.axis_index("zh") == 0)(lambda: input_grads(*inputs, grads, *scratch))
+
+
+def after_kernel(here_ref, both_ref, *refs):
+    inputs, sum_ref, grads, scratch = refs[:6], refs[8], refs[9:11], refs[11:]
+    zh = lax.axis_index("zh")
+    sum_ref[...] = here_ref[...] + both_ref[1 - zh].astype(jnp.float32)
+    pl.when(zh == 1)(lambda: input_grads(*inputs, grads, *scratch))
+
+
+def with_grads(kernel, terms, inputs, grads, outs):
+    h, t = inputs[-1].shape
+    vmem, anywhere = pl.BlockSpec(memory_space=pltpu.VMEM), pl.BlockSpec(memory_space=pl.ANY)
+    args = terms + inputs + grads
+    return pl.pallas_call(
+        kernel,
+        out_shape=tuple(jax.ShapeDtypeStruct((h, 128), dtype) for dtype in outs) + (jax.ShapeDtypeStruct((h, t), jnp.bfloat16),) * 2,
+        in_specs=[vmem] * len(terms + inputs) + [anywhere] * len(grads),
+        out_specs=(vmem,) * len(outs) + (anywhere,) * 2,
+        input_output_aliases={len(terms + inputs) + i: len(outs) + i for i in range(len(grads))},
+        scratch_shapes=[
+            pltpu.VMEM((2, h, 512), jnp.bfloat16),
+            pltpu.VMEM((h, t), jnp.float32),
+            pltpu.VMEM((2, h, t), jnp.bfloat16),
+            pltpu.SemaphoreType.DMA((2,)),
+        ],
         cost_estimate=pl.CostEstimate(flops=2 * h * t * 4096, bytes_accessed=6_000_000, transcendentals=h * t),
         compiler_params=pltpu.CompilerParams(vmem_limit_bytes=16 << 20),
-        name="input_grads",
-    )(front, last, feats, weight, gate, up)
+    )(*args)
 
 
 def turned(x, axis, by):
@@ -237,12 +264,11 @@
 
     theirs, ours = weight_parts(hiddens, feats)
     swap = lax.all_gather(theirs.astype(jnp.bfloat16), "c", axis=0)
-    part = ours + lax.dynamic_index_in_dim(swap, 1 - lax.axis_index("c"), 0, keepdims=False).astype(jnp.float32)
-    away = turned(part[:, :128].astype(jnp.bfloat16), "zh", 1)
-    here = part[:, 128:]
-
-    grad_gate, grad_up = input_grads(front, last, feats, down_weight.T, gate_t, up_t)
-    return (here + away.astype(jnp.float32)).T, grad_gate.T, grad_up.T
+    inputs = (front, last, feats, down_weight.T, gate_t, up_t)
+    send, here, *grads = with_grads(before_kernel, (ours, swap), inputs, (), (jnp.bfloat16, jnp.float32))
+    both = lax.all_gather(send, "zh", axis=0)
+    total, grad_gate, grad_up = with_grads(after_kernel, (here, both), inputs, tuple(grads), (jnp.float32,))
+    return total.T, grad_gate.T, grad_up.T
 
 
 def solution(mesh):

time: 115 us -> 106 us (0.922)
  the two profiles are of different devices: /device:TPU:135 before, /device:TPU:131 now
where the time goes in v11:
time: 106 us
  blocking collectives  64.4 us (61%)
  starting transfers between devices  23.6 us (22%)
  Pallas kernels  8.93 us (8%)
  waiting for transfers between devices  4.25 us (4%)
  other arithmetic  2.1 us (2%)
  local copies, waits for them, and re-layouts  1.72 us (2%)
    all_gather x1, blocking collectives, sections(): got = lax.all_gather(message, 'y', axis=1, tiled=True)  42.9 us
    all_gather x1, blocking collectives, sections(): both = lax.all_gather(send, 'zh', axis=0)  15.9 us
    all_to_all x1, starting transfers between devices, sections(): mine = lax.all_to_all(pieces, ('x', 'zl2'), 0, 0)  12.2 us
    ppermute x2, starting transfers between devices, turned(): lax.ppermute(x, axis, [(i, i ^ by) for i in range(lax.axis_size(axis))])  5.9 us
    all_gather x1, blocking collectives, sections(): swap = lax.all_gather(theirs.astype(jnp.bfloat16), 'c', axis=0)  5.65 us
    all_to_all x1, starting transfers between devices, sections(): hiddens = lax.all_to_all(copies, 'x', 0, 0)  5.53 us
    pallas_call x2, Pallas kernels, with_grads(): pl.pallas_call(kernel, out_shape=tuple((jax.ShapeDtypeStruct((h, 128), dt...  2.87 us
    ppermute x2, waiting for transfers between devices, turned(): lax.ppermute(x, axis, [(i, i ^ by) for i in range(lax.axis_size(axis))])  2.68 us
  transfers between devices with their start and end apart: 4, of which 2 were waited for; matrix products, arithmetic and copies ran while one was open for 2% of the time, Pallas kernels for 3%

profile of v11, /device:TPU:131, one launch (start us, length us, event | category | flops | bytes accessed | tf_op | source)
XLA Modules:
  0.0 105.8 jit_solution(8883708834147464456)
XLA Ops:
  0.6 0.0 copy-start.4
  0.6 0.8 copy-done.4
  1.5 0.7 split_rows.1
  2.2 12.2 %all-to-all-start.1 = ((bf16[16,8,512]{2,1,0:T(8,128)(2,1)}), bf16[16,8,512]{2,1,0:T(8,128)(2,1)S(1)}, u32[]{:S(2)}, u32[]{:S(2)}) async-start(bf16[16,8,512]{2,1,0:T(8,128)(2,1)} %split_rows.1), calls=%async_computation.1 | async-start | bytes 262144 | tf_op jit(solution)/shard_map/all_to_all | solution.py:250
  14.4 4.0 %collective-permute-start = (bf16[8,4096]{1,0:T(8,128)(2,1)}, bf16[8,4096]{1,0:T(8,128)(2,1)S(1)}, u32[]{:S(2)}, u32[]{:S(2)}) collective-permute-start(bf16[8,4096]{1,0:T(8,128)(2,1)} %own_ref.1), channel_id=1, source_target_pairs={{0,16},{16,0},{1,17},{17,1},{2,18},{18,2},{3,19},{19,3},{4,20},{20... | collective-permute-start | bytes 196616 | tf_op jit(solution)/shard_map/ppermute | solution.py:242
  18.4 2.7 %collective-permute-done.near_ref = bf16[8,4096]{1,0:T(8,128)(2,1)S(1)} collective-permute-done((bf16[8,4096]{1,0:T(8,128)(2,1)}, bf16[8,4096]{1,0:T(8,128)(2,1)S(1)}, u32[]{:S(2)}, u32[]{:S(2)}) %collective-permute-start) | collective-permute-done | bytes 65568 | tf_op jit(solution)/shard_map/ppermute | solution.py:242
  21.0 1.6 %all-to-all-done.1.rows_ref = bf16[16,8,512]{2,1,0:T(8,128)(2,1)S(1)} async-done(((bf16[16,8,512]{2,1,0:T(8,128)(2,1)}), bf16[16,8,512]{2,1,0:T(8,128)(2,1)S(1)}, u32[]{:S(2)}, u32[]{:S(2)}) %all-to-all-start.1) | async-done | bytes 131104 | tf_op jit(solution)/shard_map/all_to_all | solution.py:250
  22.6 0.0 copy-start.5
  22.6 0.8 copy-done.5
  23.5 1.9 %collective-permute-start.1 = (bf16[30,8,512]{2,1,0:T(8,128)(2,1)S(1)}, bf16[30,8,512]{2,1,0:T(8,128)(2,1)S(1)}, u32[]{:S(2)}, u32[]{:S(2)}) collective-permute-start(bf16[30,8,512]{2,1,0:T(8,128)(2,1)S(1)} %shard_map.67.here_ref), channel_id=1, source_target_pairs={{0,8},{8,0},{1,9},{9,1},{2,10},{10,2},{3,11},{11,3},{4,12},{12,4},... | collective-permute-start | bytes 737288 | tf_op jit(solution)/shard_map/ppermute | solution.py:242
  25.4 2.5 %hidden_copies.1 = bf16[8,464,256]{2,1,0:T(8,128)(2,1)} custom-call(bf16[464,256]{1,0:T(8,128)(2,1)} %bitcast.24, bf16[464,256]{1,0:T(8,128)(2,1)} %bitcast.27), custom_call_target="tpu_custom_call" | custom-call | flops 2000000 | bytes 2375680 | tf_op jit(solution)/shard_map/hidden_copies/pallas_call | solution.py:108
  27.9 5.5 %all-to-all-start = ((bf16[8,464,256]{2,1,0:T(8,128)(2,1)}), bf16[8,464,256]{2,1,0:T(8,128)(2,1)}, u32[]{:S(2)}, u32[]{:S(2)}) async-start(bf16[8,464,256]{2,1,0:T(8,128)(2,1)} %hidden_copies.1), calls=%async_computation | async-start | bytes 3801088 | tf_op jit(solution)/shard_map/all_to_all | solution.py:255
  33.4 0.0 collective-permute-done.1.far_ref
  33.4 0.3 shard_map.68
  33.7 0.1 convert_element_type.27
  33.8 42.9 %all-gather.3 = f16[62,64,512]{2,1,0:T(8,128)(2,1)S(1)} all-gather(f16[62,8,512]{2,1,0:T(8,128)(2,1)S(1)} %convert_element_type.27), channel_id=1, replica_groups=mesh['zh'=2,'x'=8,'c'=2,'zl2'=2,'zl1'=2,'y'=8] {'y'}, dimensions={1}, use_global_device_ids=true | all-gather | bytes 4571136 | tf_op jit(solution)/shard_map/all_gather | solution.py:258
  76.7 0.2 multiply_select_fusion
  76.9 0.9 multiply_convert_fusion.2
  77.8 0.3 multiply_convert_fusion.1
  78.2 0.5 multiply_convert_fusion
  78.7 0.0 all-to-all-done.hidden_ref
  78.7 0.0 copy-start
  78.7 0.0 copy-start.1
  78.7 0.0 copy-start.2
  78.7 0.0 copy-start.3
  78.8 2.6 %weight_parts.1 = (f32[464,256]{1,0:T(8,128)S(1)}, f32[464,256]{1,0:T(8,128)S(1)}) custom-call(bf16[8,464,256]{2,1,0:T(8,128)(2,1)} %all-to-all-done.hidden_ref, bf16[2048,512]{1,0:T(8,128)(2,1)S(1)} %bitcast.15), custom_call_target="tpu_custom_call" | custom-call | flops 973078528 | bytes 4000000 | tf_op jit(solution)/shard_map/weight_parts/pallas_call | solution.py:162
  81.4 5.7 %all-gather = bf16[928,256]{1,0:T(8,128)(2,1)S(1)} all-gather(bf16[464,256]{1,0:T(8,128)(2,1)S(1)} %convert_element_type.31), channel_id=2, replica_groups=mesh['zh'=2,'x'=8,'c'=2,'zl2'=2,'zl1'=2,'y'=8] {'c'}, dimensions={0}, use_global_device_ids=true | all-gather | bytes 712704 | tf_op jit(solution)/shard_map/all_gather | solution.py:266
  87.0 0.0 copy-done
  87.0 0.0 copy-done.1
  87.0 0.0 copy-done.2
  87.0 0.0 copy-done.3
  87.1 2.1 %shard_map.69 = (bf16[464,128]{1,0:T(8,128)(2,1)S(1)}, f32[464,128]{1,0:T(8,128)S(1)}, bf16[464,256]{1,0:T(8,128)(2,1)}, bf16[464,256]{1,0:T(8,128)(2,1)}) custom-call(f32[464,256]{1,0:T(8,128)S(1)} %get-tuple-element.12.ours_ref, bf16[2,464,256]{2,1,0:T(8,128)(2,1)S(1)} %bitcast.30, bf16[5,256,512]{2,1,0:T(8,128)(2,1)S(1)} %bitcast.20, ...), custom_call_target="tpu_custom_call" | custom-call | flops 973078528 | bytes 6000000 | tf_op jit(solution)/shard_map/pallas_call | solution.py:224
  89.2 15.9 %all-gather.1 = bf16[928,128]{1,0:T(8,128)(2,1)S(1)} all-gather(bf16[464,128]{1,0:T(8,128)(2,1)S(1)} %get-tuple-element.15), channel_id=3, replica_groups=mesh['zh'=2,'x'=8,'c'=2,'zl2'=2,'zl1'=2,'y'=8] {'zh'}, dimensions={0}, use_global_device_ids=true | all-gather | bytes 356352 | tf_op jit(solution)/shard_map/all_gather | solution.py:269
  105.1 0.7 shard_map.70
  (3 shorter events, 0.1 us)
Async XLA Ops:
  0.6 0.8 copy-start.4
  2.2 20.4 %all-to-all-start.1 = ((bf16[16,8,512]{2,1,0:T(8,128)(2,1)}), bf16[16,8,512]{2,1,0:T(8,128)(2,1)S(1)}, u32[]{:S(2)}, u32[]{:S(2)}) async-start(bf16[16,8,512]{2,1,0:T(8,128)(2,1)} %split_rows.1), calls=%async_computation.1 | async-start | bytes 262144 | tf_op jit(solution)/shard_map/all_to_all | solution.py:250
  14.4 6.7 %collective-permute-start = (bf16[8,4096]{1,0:T(8,128)(2,1)}, bf16[8,4096]{1,0:T(8,128)(2,1)S(1)}, u32[]{:S(2)}, u32[]{:S(2)}) collective-permute-start(bf16[8,4096]{1,0:T(8,128)(2,1)} %own_ref.1), channel_id=1, source_target_pairs={{0,16},{16,0},{1,17},{17,1},{2,18},{18,2},{3,19},{19,3},{4,20},{20... | collective-permute-start | bytes 196616 | tf_op jit(solution)/shard_map/ppermute | solution.py:242
  22.6 0.8 copy-start.5
  23.5 10.0 %collective-permute-start.1 = (bf16[30,8,512]{2,1,0:T(8,128)(2,1)S(1)}, bf16[30,8,512]{2,1,0:T(8,128)(2,1)S(1)}, u32[]{:S(2)}, u32[]{:S(2)}) collective-permute-start(bf16[30,8,512]{2,1,0:T(8,128)(2,1)S(1)} %shard_map.67.here_ref), channel_id=1, source_target_pairs={{0,8},{8,0},{1,9},{9,1},{2,10},{10,2},{3,11},{11,3},{4,12},{12,4},... | collective-permute-start | bytes 737288 | tf_op jit(solution)/shard_map/ppermute | solution.py:242
  27.9 50.8 %all-to-all-start = ((bf16[8,464,256]{2,1,0:T(8,128)(2,1)}), bf16[8,464,256]{2,1,0:T(8,128)(2,1)}, u32[]{:S(2)}, u32[]{:S(2)}) async-start(bf16[8,464,256]{2,1,0:T(8,128)(2,1)} %hidden_copies.1), calls=%async_computation | async-start | bytes 3801088 | tf_op jit(solution)/shard_map/all_to_all | solution.py:255
  78.7 8.3 %copy-start = (bf16[4096,464]{0,1:T(8,128)(2,1)S(1)}, bf16[4096,464]{0,1:T(8,128)(2,1)}, u32[]{:S(2)}) copy-start(bf16[4096,464]{0,1:T(8,128)(2,1)} %param.7) | copy-start | bytes 11403268
  78.7 8.3 %copy-start.1 = (bf16[8,64,512]{2,1,0:T(8,128)(2,1)S(1)}, bf16[8,64,512]{2,1,0:T(8,128)(2,1)}, u32[]{:S(2)}) copy-start(bf16[8,64,512]{2,1,0:T(8,128)(2,1)} %multiply_convert_fusion.2) | copy-start | bytes 1572868
  78.7 8.3 %copy-start.2 = (bf16[256,464]{0,1:T(8,128)(2,1)S(1)}, bf16[256,464]{0,1:T(8,128)(2,1)}, u32[]{:S(2)}) copy-start(bf16[256,464]{0,1:T(8,128)(2,1)} %param.5) | copy-start | bytes 712708
  78.7 8.3 %copy-start.3 = (bf16[256,464]{0,1:T(8,128)(2,1)S(1)}, bf16[256,464]{0,1:T(8,128)(2,1)}, u32[]{:S(2)}) copy-start(bf16[256,464]{0,1:T(8,128)(2,1)} %param.6) | copy-start | bytes 712708

commit v12 on v11

--- a/solution.py
+++ b/solution.py
@@ -34,12 +34,8 @@
 
 
 def pack_kernel(own_ref, near_ref, rows_ref, out_ref):
-    x = lax.axis_index("x")
-    for turn, ref in enumerate((own_ref, near_ref)):
-        for s in range(1, 8):
-            for z in range(2):
-                at = pl.multiple_of(2048 * z + 256 * lax.bitwise_xor(x, s), 256)
-                out_ref[7 * turn + s - 1, :, 256 * z : 256 * (z + 1)] = ref[:, pl.ds(at, 256)]
+    out_ref[:7] = own_ref[...]
+    out_ref[7:14] = near_ref[...]
     out_ref[14:] = rows_ref[...]
 
 
@@ -117,26 +113,30 @@
     )(gate, up)
 
 
-def split_kernel(g_ref, out_ref, held, sem):
-    zh, c = lax.axis_index("zh"), lax.axis_index("c")
-    for x in range(8):
+def split_kernel(g_ref, out_ref, own_ref, held, sem):
+    zh, x, c = lax.axis_index("zh"), lax.axis_index("x"), lax.axis_index("c")
+    for n in range(8):
         for i, core in enumerate((1 - c, c)):
             for j, z in enumerate((1 - zh, zh)):
-                at = pl.multiple_of(2048 * z + 256 * x + 128 * core, 128)
+                at = pl.multiple_of(2048 * z + 256 * n + 128 * core, 128)
                 piece = g_ref[:, pl.ds(at, 128)]
                 for zl in range(2):
-                    held[2 * x + zl, :, 256 * i + 128 * j : 256 * i + 128 * (j + 1)] = piece
+                    held[2 * n + zl, :, 256 * i + 128 * j : 256 * i + 128 * (j + 1)] = piece
     copy = pltpu.make_async_copy(held, out_ref, sem)
     copy.start()
+    for s in range(1, 8):
+        for z in range(2):
+            at = pl.multiple_of(2048 * z + 256 * lax.bitwise_xor(x, s), 256)
+            own_ref[s - 1, :, 256 * z : 256 * (z + 1)] = g_ref[:, pl.ds(at, 256)]
     copy.wait()
 
 
 def split_rows(g):
     return pl.pallas_call(
         split_kernel,
-        out_shape=jax.ShapeDtypeStruct((16, 8, 512), jnp.bfloat16),
+        out_shape=(jax.ShapeDtypeStruct((16, 8, 512), jnp.bfloat16), jax.ShapeDtypeStruct((7, 8, 512), jnp.bfloat16)),
         in_specs=[pl.BlockSpec(memory_space=pltpu.VMEM)],
-        out_specs=pl.BlockSpec(memory_space=pl.ANY),
+        out_specs=(pl.BlockSpec(memory_space=pl.ANY), pl.BlockSpec(memory_space=pltpu.VMEM)),
         scratch_shapes=[pltpu.VMEM((16, 8, 512), jnp.bfloat16), pltpu.SemaphoreType.DMA],
         compiler_params=pltpu.CompilerParams(vmem_limit_bytes=2 << 20),
         name="split_rows",
@@ -180,7 +180,12 @@
             for z in range(2):
                 at = pl.multiple_of(2048 * z + 256 * lax.bitwise_xor(x, n + 1), 256)
                 weight[slot, :, 256 * z : 256 * (z + 1)] = weight_ref[:, pl.ds(at, 256)]
-            rows = front_ref[n] if n < 5 else last_ref[n - 5]
+            if n < 5:
+                rows = front_ref[t * n : t * (n + 1), :]
+            elif n == 5:
+                rows = jnp.concatenate([front_ref[t * n :, :], last_ref[: last_ref.shape[0] - t, :]], 0)
+            else:
+                rows = last_ref[last_ref.shape[0] - t :, :]
         else:
             for i, core in enumerate((1 - c, c)):
                 for j, z in enumerate((1 - zh, zh)):
@@ -246,11 +251,11 @@
     gate_t, up_t = gate_pre.T, up_pre.T
     _, t = gate_t.shape
 
-    pieces = split_rows(grad_out)
+    pieces, own = split_rows(grad_out)
     mine = lax.all_to_all(pieces, ("x", "zl2"), 0, 0)
-    near = turned(grad_out, "zl2", 1)
+    near = turned(own, "zl2", 1)
     copies = hidden_copies(gate_t, up_t)
-    packed = in_vmem(pack_kernel, 30, grad_out, near, mine)
+    packed = in_vmem(pack_kernel, 30, own, near, mine)
     far = turned(packed, "zl1", 1)
     hiddens = lax.all_to_all(copies, "x", 0, 0)
 
@@ -259,8 +264,8 @@
 
     scale = power(got[60:].astype(jnp.float32), -1)
     feats = (got[28:60].astype(jnp.float32) * scale[1]).astype(jnp.bfloat16).reshape(8 * t, 512)
-    front = (got[:20].astype(jnp.float32) * scale[0]).astype(jnp.bfloat16).reshape(5, t, 512)
-    last = (got[20:28].astype(jnp.float32) * scale[0]).astype(jnp.bfloat16).reshape(2, t, 512)
+    front = (got[:22].astype(jnp.float32) * scale[0]).astype(jnp.bfloat16).reshape(22 * 64, 512)
+    last = (got[22:28].astype(jnp.float32) * scale[0]).astype(jnp.bfloat16).reshape(6 * 64, 512)
 
     theirs, ours = weight_parts(hiddens, feats)
     swap = lax.all_gather(theirs.astype(jnp.bfloat16), "c", axis=0)

time: 106 us -> 105 us (level)
  the two profiles are of different devices: /device:TPU:131 before, /device:TPU:130 now
where the time goes in v12:
time: 105 us; the launch traced here: 104 us
  blocking collectives  59.6 us (57%)
  starting transfers between devices  27.5 us (26%)
  Pallas kernels  8.9 us (8%)
  waiting for transfers between devices  4.73 us (5%)
  other arithmetic  2.05 us (2%)
    all_gather x1, blocking collectives, sections(): got = lax.all_gather(message, 'y', axis=1, tiled=True)  41.8 us
    all_gather x1, blocking collectives, sections(): both = lax.all_gather(send, 'zh', axis=0)  15.7 us
    all_to_all x1, starting transfers between devices, sections(): mine = lax.all_to_all(pieces, ('x', 'zl2'), 0, 0)  12.8 us
    ppermute x2, starting transfers between devices, turned(): lax.ppermute(x, axis, [(i, i ^ by) for i in range(lax.axis_size(axis))])  8.73 us
    all_to_all x1, starting transfers between devices, sections(): hiddens = lax.all_to_all(copies, 'x', 0, 0)  5.97 us
    ppermute x2, waiting for transfers between devices, turned(): lax.ppermute(x, axis, [(i, i ^ by) for i in range(lax.axis_size(axis))])  2.96 us
    pallas_call x2, Pallas kernels, with_grads(): pl.pallas_call(kernel, out_shape=tuple((jax.ShapeDtypeStruct((h, 128), dt...  2.85 us
    pallas_call x1, Pallas kernels, weight_parts(): pl.pallas_call(weights_kernel, out_shape=(jax.ShapeDtypeStruct((h, 256),...  2.59 us
  transfers between devices with their start and end apart: 4, of which 2 were waited for; matrix products, arithmetic and copies ran while one was open for 2% of the time, Pallas kernels for 3%

profile of v12, /device:TPU:130, one launch (start us, length us, event | category | flops | bytes accessed | tf_op | source)
XLA Modules:
  0.0 104.4 jit_solution(7472277585296452449)
XLA Ops:
  0.6 0.0 copy-start.4
  0.6 0.8 copy-done.4
  1.5 0.7 split_rows.1
  2.2 12.8 %all-to-all-start.1 = ((bf16[16,8,512]{2,1,0:T(8,128)(2,1)}), bf16[16,8,512]{2,1,0:T(8,128)(2,1)S(1)}, u32[]{:S(2)}, u32[]{:S(2)}) async-start(bf16[16,8,512]{2,1,0:T(8,128)(2,1)} %get-tuple-element.15), calls=%async_computation.1 | async-start | bytes 262144 | tf_op jit(solution)/shard_map/all_to_all | solution.py:255
  14.9 4.3 %collective-permute-start = (bf16[7,8,512]{2,1,0:T(8,128)(2,1)S(1)}, bf16[7,8,512]{2,1,0:T(8,128)(2,1)S(1)}, u32[]{:S(2)}, u32[]{:S(2)}) collective-permute-start(bf16[7,8,512]{2,1,0:T(8,128)(2,1)S(1)} %get-tuple-element.14.own_ref), channel_id=1, source_target_pairs={{0,16},{16,0},{1,17},{17,1},{2,18},{18,2},{3,19},{19,3},{4,20},{20... | collective-permute-start | bytes 172040 | tf_op jit(solution)/shard_map/ppermute | solution.py:247
  19.2 3.0 %collective-permute-done.near_ref = bf16[7,8,512]{2,1,0:T(8,128)(2,1)S(1)} collective-permute-done((bf16[7,8,512]{2,1,0:T(8,128)(2,1)S(1)}, bf16[7,8,512]{2,1,0:T(8,128)(2,1)S(1)}, u32[]{:S(2)}, u32[]{:S(2)}) %collective-permute-start) | collective-permute-done | bytes 57376 | tf_op jit(solution)/shard_map/ppermute | solution.py:247
  22.1 1.8 %all-to-all-done.1.rows_ref = bf16[16,8,512]{2,1,0:T(8,128)(2,1)S(1)} async-done(((bf16[16,8,512]{2,1,0:T(8,128)(2,1)}), bf16[16,8,512]{2,1,0:T(8,128)(2,1)S(1)}, u32[]{:S(2)}, u32[]{:S(2)}) %all-to-all-start.1) | async-done | bytes 131104 | tf_op jit(solution)/shard_map/all_to_all | solution.py:255
  23.9 4.5 %collective-permute-start.1 = (bf16[30,8,512]{2,1,0:T(8,128)(2,1)S(1)}, bf16[30,8,512]{2,1,0:T(8,128)(2,1)S(1)}, u32[]{:S(2)}, u32[]{:S(2)}) collective-permute-start(bf16[30,8,512]{2,1,0:T(8,128)(2,1)S(1)} %shard_map.67.here_ref), channel_id=1, source_target_pairs={{0,8},{8,0},{1,9},{9,1},{2,10},{10,2},{3,11},{11,3},{4,12},{12,4},... | collective-permute-start | bytes 737288 | tf_op jit(solution)/shard_map/ppermute | solution.py:247
  28.4 2.5 %hidden_copies.1 = bf16[8,464,256]{2,1,0:T(8,128)(2,1)} custom-call(bf16[464,256]{1,0:T(8,128)(2,1)} %bitcast.24, bf16[464,256]{1,0:T(8,128)(2,1)} %bitcast.27), custom_call_target="tpu_custom_call" | custom-call | flops 2000000 | bytes 2375680 | tf_op jit(solution)/shard_map/hidden_copies/pallas_call | solution.py:104
  30.9 6.0 %all-to-all-start = ((bf16[8,464,256]{2,1,0:T(8,128)(2,1)}), bf16[8,464,256]{2,1,0:T(8,128)(2,1)}, u32[]{:S(2)}, u32[]{:S(2)}) async-start(bf16[8,464,256]{2,1,0:T(8,128)(2,1)} %hidden_copies.1), calls=%async_computation | async-start | bytes 3801088 | tf_op jit(solution)/shard_map/all_to_all | solution.py:260
  36.9 0.0 collective-permute-done.1.far_ref
  36.9 0.3 shard_map.68
  37.2 0.1 convert_element_type.27
  37.3 41.8 %all-gather.3 = f16[62,64,512]{2,1,0:T(8,128)(2,1)S(1)} all-gather(f16[62,8,512]{2,1,0:T(8,128)(2,1)S(1)} %convert_element_type.27), channel_id=1, replica_groups=mesh['zh'=2,'x'=8,'c'=2,'zl2'=2,'zl1'=2,'y'=8] {'y'}, dimensions={1}, use_global_device_ids=true | all-gather | bytes 4571136 | tf_op jit(solution)/shard_map/all_gather | solution.py:263
  79.0 0.2 multiply_select_fusion
  79.3 0.8 multiply_convert_fusion.2
  80.1 0.3 multiply_convert_fusion.1
  80.5 0.5 multiply_convert_fusion
  81.0 0.0 all-to-all-done.hidden_ref
  81.0 0.0 copy-start
  81.0 0.0 copy-start.1
  81.0 0.0 copy-start.2
  81.0 0.0 copy-start.3
  81.1 2.6 %weight_parts.1 = (f32[464,256]{1,0:T(8,128)S(1)}, f32[464,256]{1,0:T(8,128)S(1)}) custom-call(bf16[8,464,256]{2,1,0:T(8,128)(2,1)} %all-to-all-done.hidden_ref, bf16[2048,512]{1,0:T(8,128)(2,1)S(1)} %bitcast.15), custom_call_target="tpu_custom_call" | custom-call | flops 973078528 | bytes 4000000 | tf_op jit(solution)/shard_map/weight_parts/pallas_call | solution.py:162
  83.7 2.1 %all-gather = bf16[928,256]{1,0:T(8,128)(2,1)S(1)} all-gather(bf16[464,256]{1,0:T(8,128)(2,1)S(1)} %convert_element_type.31), channel_id=2, replica_groups=mesh['zh'=2,'x'=8,'c'=2,'zl2'=2,'zl1'=2,'y'=8] {'c'}, dimensions={0}, use_global_device_ids=true | all-gather | bytes 712704 | tf_op jit(solution)/shard_map/all_gather | solution.py:271
  85.8 0.0 copy-done
  85.8 0.0 copy-done.1
  85.8 0.0 copy-done.2
  85.8 0.0 copy-done.3
  85.8 2.1 %shard_map.69 = (bf16[464,128]{1,0:T(8,128)(2,1)S(1)}, f32[464,128]{1,0:T(8,128)S(1)}, bf16[464,256]{1,0:T(8,128)(2,1)}, bf16[464,256]{1,0:T(8,128)(2,1)}) custom-call(f32[464,256]{1,0:T(8,128)S(1)} %get-tuple-element.16.ours_ref, bf16[2,464,256]{2,1,0:T(8,128)(2,1)S(1)} %bitcast.30, bf16[1408,512]{1,0:T(8,128)(2,1)S(1)} %bitcast.20, ...), custom_call_target="tpu_custom_call" | custom-call | flops 973078528 | bytes 6000000 | tf_op jit(solution)/shard_map/pallas_call | solution.py:229
  88.0 15.7 %all-gather.1 = bf16[928,128]{1,0:T(8,128)(2,1)S(1)} all-gather(bf16[464,128]{1,0:T(8,128)(2,1)S(1)} %get-tuple-element.19), channel_id=3, replica_groups=mesh['zh'=2,'x'=8,'c'=2,'zl2'=2,'zl1'=2,'y'=8] {'zh'}, dimensions={0}, use_global_device_ids=true | all-gather | bytes 356352 | tf_op jit(solution)/shard_map/all_gather | solution.py:274
  103.7 0.7 shard_map.70
  (3 shorter events, 0.1 us)
Async XLA Ops:
  0.6 0.8 copy-start.4
  2.2 21.7 %all-to-all-start.1 = ((bf16[16,8,512]{2,1,0:T(8,128)(2,1)}), bf16[16,8,512]{2,1,0:T(8,128)(2,1)S(1)}, u32[]{:S(2)}, u32[]{:S(2)}) async-start(bf16[16,8,512]{2,1,0:T(8,128)(2,1)} %get-tuple-element.15), calls=%async_computation.1 | async-start | bytes 262144 | tf_op jit(solution)/shard_map/all_to_all | solution.py:255
  14.9 7.2 %collective-permute-start = (bf16[7,8,512]{2,1,0:T(8,128)(2,1)S(1)}, bf16[7,8,512]{2,1,0:T(8,128)(2,1)S(1)}, u32[]{:S(2)}, u32[]{:S(2)}) collective-permute-start(bf16[7,8,512]{2,1,0:T(8,128)(2,1)S(1)} %get-tuple-element.14.own_ref), channel_id=1, source_target_pairs={{0,16},{16,0},{1,17},{17,1},{2,18},{18,2},{3,19},{19,3},{4,20},{20... | collective-permute-start | bytes 172040 | tf_op jit(solution)/shard_map/ppermute | solution.py:247
  23.9 12.9 %collective-permute-start.1 = (bf16[30,8,512]{2,1,0:T(8,128)(2,1)S(1)}, bf16[30,8,512]{2,1,0:T(8,128)(2,1)S(1)}, u32[]{:S(2)}, u32[]{:S(2)}) collective-permute-start(bf16[30,8,512]{2,1,0:T(8,128)(2,1)S(1)} %shard_map.67.here_ref), channel_id=1, source_target_pairs={{0,8},{8,0},{1,9},{9,1},{2,10},{10,2},{3,11},{11,3},{4,12},{12,4},... | collective-permute-start | bytes 737288 | tf_op jit(solution)/shard_map/ppermute | solution.py:247
  30.9 50.1 %all-to-all-start = ((bf16[8,464,256]{2,1,0:T(8,128)(2,1)}), bf16[8,464,256]{2,1,0:T(8,128)(2,1)}, u32[]{:S(2)}, u32[]{:S(2)}) async-start(bf16[8,464,256]{2,1,0:T(8,128)(2,1)} %hidden_copies.1), calls=%async_computation | async-start | bytes 3801088 | tf_op jit(solution)/shard_map/all_to_all | solution.py:260
  81.0 4.8 %copy-start = (bf16[4096,464]{0,1:T(8,128)(2,1)S(1)}, bf16[4096,464]{0,1:T(8,128)(2,1)}, u32[]{:S(2)}) copy-start(bf16[4096,464]{0,1:T(8,128)(2,1)} %param.7) | copy-start | bytes 11403268
  81.0 4.8 %copy-start.1 = (bf16[6,64,512]{2,1,0:T(8,128)(2,1)S(1)}, bf16[6,64,512]{2,1,0:T(8,128)(2,1)}, u32[]{:S(2)}) copy-start(bf16[6,64,512]{2,1,0:T(8,128)(2,1)} %multiply_convert_fusion.2) | copy-start | bytes 1179652
  81.0 4.8 %copy-start.2 = (bf16[256,464]{0,1:T(8,128)(2,1)S(1)}, bf16[256,464]{0,1:T(8,128)(2,1)}, u32[]{:S(2)}) copy-start(bf16[256,464]{0,1:T(8,128)(2,1)} %param.5) | copy-start | bytes 712708
  81.0 4.8 %copy-start.3 = (bf16[256,464]{0,1:T(8,128)(2,1)S(1)}, bf16[256,464]{0,1:T(8,128)(2,1)}, u32[]{:S(2)}) copy-start(bf16[256,464]{0,1:T(8,128)(2,1)} %param.6) | copy-start | bytes 712708

commit v13 on v12

--- a/solution.py
+++ b/solution.py
@@ -48,7 +48,8 @@
             value = jnp.max(jnp.abs(ref[:14, :, 128 * b : 128 * (b + 1)].astype(jnp.float32)), axis=0)
             most = value if most is None else jnp.maximum(most, value)
     scale, k = scales_of(most)
-    out_ref[60] = jnp.broadcast_to(k, (8, 512)).astype(jnp.bfloat16)
+    line = lax.broadcasted_iota(jnp.int32, (8, 128), 0)
+    own_k = k
     for ref, first in sides:
         for turn in range(2):
             place = first + 2 * lax.bitwise_xor(zl2, turn)
@@ -58,7 +59,7 @@
         cols = slice(128 * b, 128 * (b + 1))
         values = [ref[14:, :, cols].astype(jnp.float32) for ref, _ in sides]
         scale, k = scales_of(jnp.max(jnp.maximum(jnp.abs(values[0]), jnp.abs(values[1])), axis=0))
-        out_ref[61, :, cols] = jnp.broadcast_to(k, (8, 128)).astype(jnp.bfloat16)
+        out_ref[60, :, cols] = jnp.where(line < 4, own_k, k).astype(jnp.bfloat16)
         for value, (_, first) in zip(values, sides):
             for x in range(8):
                 for i in range(2):
@@ -74,6 +75,26 @@
         cost_estimate=pl.CostEstimate(flops=1_000_000, bytes_accessed=600_000, transcendentals=0),
         compiler_params=pltpu.CompilerParams(vmem_limit_bytes=4 << 20),
     )(*args)
+
+
+def scales_kernel(k_ref, own_ref, rows_ref):
+    for y in range(8):
+        k = k_ref[8 * y : 8 * y + 8, :].astype(jnp.float32)
+        scale = power(k, -1)
+        own_ref[8 * y : 8 * y + 8, :] = jnp.broadcast_to(scale[:1], (8, 512))
+        rows_ref[8 * y : 8 * y + 8, :] = jnp.broadcast_to(scale[4:5], (8, 512))
+
+
+def scales(k):
+    return pl.pallas_call(
+        scales_kernel,
+        out_shape=(jax.ShapeDtypeStruct((64, 512), jnp.float32),) * 2,
+        in_specs=[pl.BlockSpec(memory_space=pltpu.VMEM)],
+        out_specs=(pl.BlockSpec(memory_space=pltpu.VMEM),) * 2,
+        cost_estimate=pl.CostEstimate(flops=1_000_000, bytes_accessed=400_000, transcendentals=0),
+        compiler_params=pltpu.CompilerParams(vmem_limit_bytes=2 << 20),
+        name="scales",
+    )(k)
 
 
 def hidden_kernel(gate_ref, up_ref, out_ref, gate_in, up_in, done, in_sem, out_sem):
@@ -259,10 +280,10 @@
     far = turned(packed, "zl1", 1)
     hiddens = lax.all_to_all(copies, "x", 0, 0)
 
-    message = in_vmem(code_kernel, 62, packed, far).astype(jnp.float16)
+    message = in_vmem(code_kernel, 61, packed, far).astype(jnp.float16)
     got = lax.all_gather(message, "y", axis=1, tiled=True)
 
-    scale = power(got[60:].astype(jnp.float32), -1)
+    scale = scales(got[60].astype(jnp.bfloat16))
     feats = (got[28:60].astype(jnp.float32) * scale[1]).astype(jnp.bfloat16).reshape(8 * t, 512)
     front = (got[:22].astype(jnp.float32) * scale[0]).astype(jnp.bfloat16).reshape(22 * 64, 512)
     last = (got[22:28].astype(jnp.float32) * scale[0]).astype(jnp.bfloat16).reshape(6 * 64, 512)

time: 105 us -> 113 us (1.076)
  the two profiles are of different devices: /device:TPU:130 before, /device:TPU:135 now
where the time goes in v13:
time: 113 us; the launch traced here: 112 us
  blocking collectives  62.7 us (55%)
  starting transfers between devices  22.9 us (20%)
  waiting for transfers between devices  14.1 us (12%)
  Pallas kernels  9.04 us (8%)
  other arithmetic  1.82 us (2%)
    all_gather x1, blocking collectives, sections(): got = lax.all_gather(message, 'y', axis=1, tiled=True)  42 us
    all_gather x1, blocking collectives, sections(): both = lax.all_gather(send, 'zh', axis=0)  14.5 us
    all_to_all x1, starting transfers between devices, sections(): mine = lax.all_to_all(pieces, ('x', 'zl2'), 0, 0)  12.1 us
    ppermute x2, waiting for transfers between devices, turned(): lax.ppermute(x, axis, [(i, i ^ by) for i in range(lax.axis_size(axis))])  9.5 us
    all_to_all x1, starting transfers between devices, sections(): hiddens = lax.all_to_all(copies, 'x', 0, 0)  6.72 us
    all_gather x1, blocking collectives, sections(): swap = lax.all_gather(theirs.astype(jnp.bfloat16), 'c', axis=0)  6.22 us
    all_to_all x1, waiting for transfers between devices, sections(): mine = lax.all_to_all(pieces, ('x', 'zl2'), 0, 0)  4.55 us
    ppermute x2, starting transfers between devices, turned(): lax.ppermute(x, axis, [(i, i ^ by) for i in range(lax.axis_size(axis))])  4.04 us
  transfers between devices with their start and end apart: 4, of which 3 were waited for; matrix products, arithmetic and copies ran while one was open for 2% of the time, Pallas kernels for 3%

profile of v13, /device:TPU:135, one launch (start us, length us, event | category | flops | bytes accessed | tf_op | source)
XLA Modules:
  0.0 112.2 jit_solution(818074815087690359)
XLA Ops:
  0.6 0.0 copy-start.4
  0.6 0.8 copy-done.4
  1.5 0.7 split_rows.1
  2.2 12.1 %all-to-all-start.1 = ((bf16[16,8,512]{2,1,0:T(8,128)(2,1)}), bf16[16,8,512]{2,1,0:T(8,128)(2,1)S(1)}, u32[]{:S(2)}, u32[]{:S(2)}) async-start(bf16[16,8,512]{2,1,0:T(8,128)(2,1)} %get-tuple-element.17), calls=%async_computation.1 | async-start | bytes 262144 | tf_op jit(solution)/shard_map/all_to_all | solution.py:276
  14.3 2.5 %hidden_copies.1 = bf16[8,464,256]{2,1,0:T(8,128)(2,1)} custom-call(bf16[464,256]{1,0:T(8,128)(2,1)} %bitcast.22, bf16[464,256]{1,0:T(8,128)(2,1)} %bitcast.25), custom_call_target="tpu_custom_call" | custom-call | flops 2000000 | bytes 2375680 | tf_op jit(solution)/shard_map/hidden_copies/pallas_call | solution.py:125
  16.8 4.6 %all-to-all-done.1.rows_ref = bf16[16,8,512]{2,1,0:T(8,128)(2,1)S(1)} async-done(((bf16[16,8,512]{2,1,0:T(8,128)(2,1)}), bf16[16,8,512]{2,1,0:T(8,128)(2,1)S(1)}, u32[]{:S(2)}, u32[]{:S(2)}) %all-to-all-start.1) | async-done | bytes 131104 | tf_op jit(solution)/shard_map/all_to_all | solution.py:276
  21.4 6.7 %all-to-all-start = ((bf16[8,464,256]{2,1,0:T(8,128)(2,1)}), bf16[8,464,256]{2,1,0:T(8,128)(2,1)}, u32[]{:S(2)}, u32[]{:S(2)}) async-start(bf16[8,464,256]{2,1,0:T(8,128)(2,1)} %hidden_copies.1), calls=%async_computation | async-start | bytes 3801088 | tf_op jit(solution)/shard_map/all_to_all | solution.py:281
  28.1 2.1 %collective-permute-start = (bf16[7,8,512]{2,1,0:T(8,128)(2,1)S(1)}, bf16[7,8,512]{2,1,0:T(8,128)(2,1)S(1)}, u32[]{:S(2)}, u32[]{:S(2)}) collective-permute-start(bf16[7,8,512]{2,1,0:T(8,128)(2,1)S(1)} %get-tuple-element.16.own_ref), channel_id=1, source_target_pairs={{0,16},{16,0},{1,17},{17,1},{2,18},{18,2},{3,19},{19,3},{4,20},{20... | collective-permute-start | bytes 172040 | tf_op jit(solution)/shard_map/ppermute | solution.py:268
  30.2 4.1 %collective-permute-done.near_ref = bf16[7,8,512]{2,1,0:T(8,128)(2,1)S(1)} collective-permute-done((bf16[7,8,512]{2,1,0:T(8,128)(2,1)S(1)}, bf16[7,8,512]{2,1,0:T(8,128)(2,1)S(1)}, u32[]{:S(2)}, u32[]{:S(2)}) %collective-permute-start) | collective-permute-done | bytes 57376 | tf_op jit(solution)/shard_map/ppermute | solution.py:268
  34.3 1.9 %collective-permute-start.1 = (bf16[30,8,512]{2,1,0:T(8,128)(2,1)S(1)}, bf16[30,8,512]{2,1,0:T(8,128)(2,1)S(1)}, u32[]{:S(2)}, u32[]{:S(2)}) collective-permute-start(bf16[30,8,512]{2,1,0:T(8,128)(2,1)S(1)} %shard_map.67.here_ref), channel_id=1, source_target_pairs={{0,8},{8,0},{1,9},{9,1},{2,10},{10,2},{3,11},{11,3},{4,12},{12,4},... | collective-permute-start | bytes 737288 | tf_op jit(solution)/shard_map/ppermute | solution.py:268
  36.2 5.4 %collective-permute-done.1.far_ref = bf16[30,8,512]{2,1,0:T(8,128)(2,1)S(1)} collective-permute-done((bf16[30,8,512]{2,1,0:T(8,128)(2,1)S(1)}, bf16[30,8,512]{2,1,0:T(8,128)(2,1)S(1)}, u32[]{:S(2)}, u32[]{:S(2)}) %collective-permute-start.1) | collective-permute-done | bytes 245792 | tf_op jit(solution)/shard_map/ppermute | solution.py:268
  41.6 0.3 shard_map.68
  41.9 0.1 convert_element_type.29
  42.0 42.0 %all-gather.3 = f16[61,64,512]{2,1,0:T(8,128)(2,1)S(1)} all-gather(f16[61,8,512]{2,1,0:T(8,128)(2,1)S(1)} %convert_element_type.29), channel_id=1, replica_groups=mesh['zh'=2,'x'=8,'c'=2,'zl2'=2,'zl1'=2,'y'=8] {'y'}, dimensions={1}, use_global_device_ids=true | all-gather | bytes 4497408 | tf_op jit(solution)/shard_map/all_gather | solution.py:284
  84.0 0.1 scales.1
  84.2 0.8 multiply_convert_fusion.2
  85.0 0.3 multiply_convert_fusion.1
  85.3 0.5 multiply_convert_fusion
  85.9 0.0 all-to-all-done.hidden_ref
  85.9 0.0 copy-start
  85.9 0.0 copy-start.1
  85.9 0.0 copy-start.2
  85.9 0.0 copy-start.3
  86.0 2.6 %weight_parts.1 = (f32[464,256]{1,0:T(8,128)S(1)}, f32[464,256]{1,0:T(8,128)S(1)}) custom-call(bf16[8,464,256]{2,1,0:T(8,128)(2,1)} %all-to-all-done.hidden_ref, bf16[2048,512]{1,0:T(8,128)(2,1)S(1)} %bitcast.13), custom_call_target="tpu_custom_call" | custom-call | flops 973078528 | bytes 4000000 | tf_op jit(solution)/shard_map/weight_parts/pallas_call | solution.py:183
  88.6 6.2 %all-gather = bf16[928,256]{1,0:T(8,128)(2,1)S(1)} all-gather(bf16[464,256]{1,0:T(8,128)(2,1)S(1)} %convert_element_type.34), channel_id=2, replica_groups=mesh['zh'=2,'x'=8,'c'=2,'zl2'=2,'zl1'=2,'y'=8] {'c'}, dimensions={0}, use_global_device_ids=true | all-gather | bytes 712704 | tf_op jit(solution)/shard_map/all_gather | solution.py:292
  94.8 0.0 copy-done
  94.8 0.0 copy-done.1
  94.8 0.0 copy-done.2
  94.8 0.0 copy-done.3
  94.8 2.1 %shard_map.69 = (bf16[464,128]{1,0:T(8,128)(2,1)S(1)}, f32[464,128]{1,0:T(8,128)S(1)}, bf16[464,256]{1,0:T(8,128)(2,1)}, bf16[464,256]{1,0:T(8,128)(2,1)}) custom-call(f32[464,256]{1,0:T(8,128)S(1)} %get-tuple-element.19.ours_ref, bf16[2,464,256]{2,1,0:T(8,128)(2,1)S(1)} %bitcast.28, bf16[1408,512]{1,0:T(8,128)(2,1)S(1)} %bitcast.18, ...), custom_call_target="tpu_custom_call" | custom-call | flops 973078528 | bytes 6000000 | tf_op jit(solution)/shard_map/pallas_call | solution.py:250
  97.0 14.5 %all-gather.1 = bf16[928,128]{1,0:T(8,128)(2,1)S(1)} all-gather(bf16[464,128]{1,0:T(8,128)(2,1)S(1)} %get-tuple-element.23), channel_id=3, replica_groups=mesh['zh'=2,'x'=8,'c'=2,'zl2'=2,'zl1'=2,'y'=8] {'zh'}, dimensions={0}, use_global_device_ids=true | all-gather | bytes 356352 | tf_op jit(solution)/shard_map/all_gather | solution.py:295
  111.5 0.7 shard_map.70
  (3 shorter events, 0.1 us)
Async XLA Ops:
  0.6 0.8 copy-start.4
  2.2 19.2 %all-to-all-start.1 = ((bf16[16,8,512]{2,1,0:T(8,128)(2,1)}), bf16[16,8,512]{2,1,0:T(8,128)(2,1)S(1)}, u32[]{:S(2)}, u32[]{:S(2)}) async-start(bf16[16,8,512]{2,1,0:T(8,128)(2,1)} %get-tuple-element.17), calls=%async_computation.1 | async-start | bytes 262144 | tf_op jit(solution)/shard_map/all_to_all | solution.py:276
  21.4 64.5 %all-to-all-start = ((bf16[8,464,256]{2,1,0:T(8,128)(2,1)}), bf16[8,464,256]{2,1,0:T(8,128)(2,1)}, u32[]{:S(2)}, u32[]{:S(2)}) async-start(bf16[8,464,256]{2,1,0:T(8,128)(2,1)} %hidden_copies.1), calls=%async_computation | async-start | bytes 3801088 | tf_op jit(solution)/shard_map/all_to_all | solution.py:281
  28.1 6.2 %collective-permute-start = (bf16[7,8,512]{2,1,0:T(8,128)(2,1)S(1)}, bf16[7,8,512]{2,1,0:T(8,128)(2,1)S(1)}, u32[]{:S(2)}, u32[]{:S(2)}) collective-permute-start(bf16[7,8,512]{2,1,0:T(8,128)(2,1)S(1)} %get-tuple-element.16.own_ref), channel_id=1, source_target_pairs={{0,16},{16,0},{1,17},{17,1},{2,18},{18,2},{3,19},{19,3},{4,20},{20... | collective-permute-start | bytes 172040 | tf_op jit(solution)/shard_map/ppermute | solution.py:268
  34.3 7.3 %collective-permute-start.1 = (bf16[30,8,512]{2,1,0:T(8,128)(2,1)S(1)}, bf16[30,8,512]{2,1,0:T(8,128)(2,1)S(1)}, u32[]{:S(2)}, u32[]{:S(2)}) collective-permute-start(bf16[30,8,512]{2,1,0:T(8,128)(2,1)S(1)} %shard_map.67.here_ref), channel_id=1, source_target_pairs={{0,8},{8,0},{1,9},{9,1},{2,10},{10,2},{3,11},{11,3},{4,12},{12,4},... | collective-permute-start | bytes 737288 | tf_op jit(solution)/shard_map/ppermute | solution.py:268
  85.9 8.9 %copy-start = (bf16[4096,464]{0,1:T(8,128)(2,1)S(1)}, bf16[4096,464]{0,1:T(8,128)(2,1)}, u32[]{:S(2)}) copy-start(bf16[4096,464]{0,1:T(8,128)(2,1)} %param.7) | copy-start | bytes 11403268
  85.9 8.9 %copy-start.1 = (bf16[6,64,512]{2,1,0:T(8,128)(2,1)S(1)}, bf16[6,64,512]{2,1,0:T(8,128)(2,1)}, u32[]{:S(2)}) copy-start(bf16[6,64,512]{2,1,0:T(8,128)(2,1)} %multiply_convert_fusion.2) | copy-start | bytes 1179652
  85.9 8.9 %copy-start.2 = (bf16[256,464]{0,1:T(8,128)(2,1)S(1)}, bf16[256,464]{0,1:T(8,128)(2,1)}, u32[]{:S(2)}) copy-start(bf16[256,464]{0,1:T(8,128)(2,1)} %param.5) | copy-start | bytes 712708
  85.9 8.9 %copy-start.3 = (bf16[256,464]{0,1:T(8,128)(2,1)S(1)}, bf16[256,464]{0,1:T(8,128)(2,1)}, u32[]{:S(2)}) copy-start(bf16[256,464]{0,1:T(8,128)(2,1)} %param.6) | copy-start | bytes 712708

commit v14 on v13

--- a/solution.py
+++ b/solution.py
@@ -63,7 +63,7 @@
         for value, (_, first) in zip(values, sides):
             for x in range(8):
                 for i in range(2):
-                    out_ref[28 + 4 * x + first + 2 * i, :, cols] = (value[2 * x + i] * scale).astype(jnp.bfloat16)
+                    out_ref[28 + 4 * x + first + 2 * i, :, cols] = (value[8 * i + x] * scale).astype(jnp.bfloat16)
 
 
 def in_vmem(kernel, blocks, *args):
@@ -142,7 +142,7 @@
                 at = pl.multiple_of(2048 * z + 256 * n + 128 * core, 128)
                 piece = g_ref[:, pl.ds(at, 128)]
                 for zl in range(2):
-                    held[2 * n + zl, :, 256 * i + 128 * j : 256 * i + 128 * (j + 1)] = piece
+                    held[8 * zl + n, :, 256 * i + 128 * j : 256 * i + 128 * (j + 1)] = piece
     copy = pltpu.make_async_copy(held, out_ref, sem)
     copy.start()
     for s in range(1, 8):
@@ -273,7 +273,7 @@
     _, t = gate_t.shape
 
     pieces, own = split_rows(grad_out)
-    mine = lax.all_to_all(pieces, ("x", "zl2"), 0, 0)
+    mine = lax.all_to_all(pieces, ("zl2", "x"), 0, 0)
     near = turned(own, "zl2", 1)
     copies = hidden_copies(gate_t, up_t)
     packed = in_vmem(pack_kernel, 30, own, near, mine)

time: 113 us -> 112 us (level)
  the two profiles are of different devices: /device:TPU:135 before, /device:TPU:134 now
where the time goes in v14:
time: 112 us; the launch traced here: 111 us
  blocking collectives  59 us (53%)
  starting transfers between devices  26.5 us (24%)
  waiting for transfers between devices  13.1 us (12%)
  Pallas kernels  9.04 us (8%)
  other arithmetic  1.82 us (2%)
    all_gather x1, blocking collectives, sections(): got = lax.all_gather(message, 'y', axis=1, tiled=True)  42.1 us
    all_gather x1, blocking collectives, sections(): both = lax.all_gather(send, 'zh', axis=0)  14.8 us
    all_to_all x1, starting transfers between devices, sections(): mine = lax.all_to_all(pieces, ('zl2', 'x'), 0, 0)  12.7 us
    ppermute x2, waiting for transfers between devices, turned(): lax.ppermute(x, axis, [(i, i ^ by) for i in range(lax.axis_size(axis))])  8.31 us
    ppermute x2, starting transfers between devices, turned(): lax.ppermute(x, axis, [(i, i ^ by) for i in range(lax.axis_size(axis))])  7.28 us
    all_to_all x1, starting transfers between devices, sections(): hiddens = lax.all_to_all(copies, 'x', 0, 0)  6.52 us
    all_to_all x1, waiting for transfers between devices, sections(): mine = lax.all_to_all(pieces, ('zl2', 'x'), 0, 0)  4.79 us
    pallas_call x2, Pallas kernels, with_grads(): pl.pallas_call(kernel, out_shape=tuple((jax.ShapeDtypeStruct((h, 128), dt...  2.86 us
  transfers between devices with their start and end apart: 4, of which 3 were waited for; matrix products, arithmetic and copies ran while one was open for 2% of the time, Pallas kernels for 3%

profile of v14, /device:TPU:134, one launch (start us, length us, event | category | flops | bytes accessed | tf_op | source)
XLA Modules:
  0.0 111.1 jit_solution(13329077560667783665)
XLA Ops:
  0.6 0.0 copy-start.4
  0.6 0.8 copy-done.4
  1.5 0.7 split_rows.1
  2.2 12.7 %all-to-all-start.1 = ((bf16[16,8,512]{2,1,0:T(8,128)(2,1)}), bf16[16,8,512]{2,1,0:T(8,128)(2,1)S(1)}, u32[]{:S(2)}, u32[]{:S(2)}) async-start(bf16[16,8,512]{2,1,0:T(8,128)(2,1)} %get-tuple-element.17), calls=%async_computation.1 | async-start | bytes 262144 | tf_op jit(solution)/shard_map/all_to_all | solution.py:276
  14.9 2.5 %hidden_copies.1 = bf16[8,464,256]{2,1,0:T(8,128)(2,1)} custom-call(bf16[464,256]{1,0:T(8,128)(2,1)} %bitcast.22, bf16[464,256]{1,0:T(8,128)(2,1)} %bitcast.25), custom_call_target="tpu_custom_call" | custom-call | flops 2000000 | bytes 2375680 | tf_op jit(solution)/shard_map/hidden_copies/pallas_call | solution.py:125
  17.4 4.8 %all-to-all-done.1.rows_ref = bf16[16,8,512]{2,1,0:T(8,128)(2,1)S(1)} async-done(((bf16[16,8,512]{2,1,0:T(8,128)(2,1)}), bf16[16,8,512]{2,1,0:T(8,128)(2,1)S(1)}, u32[]{:S(2)}, u32[]{:S(2)}) %all-to-all-start.1) | async-done | bytes 131104 | tf_op jit(solution)/shard_map/all_to_all | solution.py:276
  22.2 6.5 %all-to-all-start = ((bf16[8,464,256]{2,1,0:T(8,128)(2,1)}), bf16[8,464,256]{2,1,0:T(8,128)(2,1)}, u32[]{:S(2)}, u32[]{:S(2)}) async-start(bf16[8,464,256]{2,1,0:T(8,128)(2,1)} %hidden_copies.1), calls=%async_computation | async-start | bytes 3801088 | tf_op jit(solution)/shard_map/all_to_all | solution.py:281
  28.7 2.8 %collective-permute-start = (bf16[7,8,512]{2,1,0:T(8,128)(2,1)S(1)}, bf16[7,8,512]{2,1,0:T(8,128)(2,1)S(1)}, u32[]{:S(2)}, u32[]{:S(2)}) collective-permute-start(bf16[7,8,512]{2,1,0:T(8,128)(2,1)S(1)} %get-tuple-element.16.own_ref), channel_id=1, source_target_pairs={{0,16},{16,0},{1,17},{17,1},{2,18},{18,2},{3,19},{19,3},{4,20},{20... | collective-permute-start | bytes 172040 | tf_op jit(solution)/shard_map/ppermute | solution.py:268
  31.5 4.1 %collective-permute-done.near_ref = bf16[7,8,512]{2,1,0:T(8,128)(2,1)S(1)} collective-permute-done((bf16[7,8,512]{2,1,0:T(8,128)(2,1)S(1)}, bf16[7,8,512]{2,1,0:T(8,128)(2,1)S(1)}, u32[]{:S(2)}, u32[]{:S(2)}) %collective-permute-start) | collective-permute-done | bytes 57376 | tf_op jit(solution)/shard_map/ppermute | solution.py:268
  35.6 4.5 %collective-permute-start.1 = (bf16[30,8,512]{2,1,0:T(8,128)(2,1)S(1)}, bf16[30,8,512]{2,1,0:T(8,128)(2,1)S(1)}, u32[]{:S(2)}, u32[]{:S(2)}) collective-permute-start(bf16[30,8,512]{2,1,0:T(8,128)(2,1)S(1)} %shard_map.67.here_ref), channel_id=1, source_target_pairs={{0,8},{8,0},{1,9},{9,1},{2,10},{10,2},{3,11},{11,3},{4,12},{12,4},... | collective-permute-start | bytes 737288 | tf_op jit(solution)/shard_map/ppermute | solution.py:268
  40.1 4.2 %collective-permute-done.1.far_ref = bf16[30,8,512]{2,1,0:T(8,128)(2,1)S(1)} collective-permute-done((bf16[30,8,512]{2,1,0:T(8,128)(2,1)S(1)}, bf16[30,8,512]{2,1,0:T(8,128)(2,1)S(1)}, u32[]{:S(2)}, u32[]{:S(2)}) %collective-permute-start.1) | collective-permute-done | bytes 245792 | tf_op jit(solution)/shard_map/ppermute | solution.py:268
  44.3 0.3 shard_map.68
  44.6 0.1 convert_element_type.29
  44.7 42.1 %all-gather.3 = f16[61,64,512]{2,1,0:T(8,128)(2,1)S(1)} all-gather(f16[61,8,512]{2,1,0:T(8,128)(2,1)S(1)} %convert_element_type.29), channel_id=1, replica_groups=mesh['zh'=2,'x'=8,'c'=2,'zl2'=2,'zl1'=2,'y'=8] {'y'}, dimensions={1}, use_global_device_ids=true | all-gather | bytes 4497408 | tf_op jit(solution)/shard_map/all_gather | solution.py:284
  86.8 0.1 scales.1
  86.9 0.8 multiply_convert_fusion.2
  87.7 0.3 multiply_convert_fusion.1
  88.1 0.5 multiply_convert_fusion
  88.6 0.0 all-to-all-done.hidden_ref
  88.6 0.0 copy-start
  88.7 0.0 copy-start.1
  88.7 0.0 copy-start.2
  88.7 0.0 copy-start.3
  88.7 2.6 %weight_parts.1 = (f32[464,256]{1,0:T(8,128)S(1)}, f32[464,256]{1,0:T(8,128)S(1)}) custom-call(bf16[8,464,256]{2,1,0:T(8,128)(2,1)} %all-to-all-done.hidden_ref, bf16[2048,512]{1,0:T(8,128)(2,1)S(1)} %bitcast.13), custom_call_target="tpu_custom_call" | custom-call | flops 973078528 | bytes 4000000 | tf_op jit(solution)/shard_map/weight_parts/pallas_call | solution.py:183
  91.3 2.1 %all-gather = bf16[928,256]{1,0:T(8,128)(2,1)S(1)} all-gather(bf16[464,256]{1,0:T(8,128)(2,1)S(1)} %convert_element_type.34), channel_id=2, replica_groups=mesh['zh'=2,'x'=8,'c'=2,'zl2'=2,'zl1'=2,'y'=8] {'c'}, dimensions={0}, use_global_device_ids=true | all-gather | bytes 712704 | tf_op jit(solution)/shard_map/all_gather | solution.py:292
  93.5 0.0 copy-done
  93.5 0.0 copy-done.1
  93.5 0.0 copy-done.2
  93.5 0.0 copy-done.3
  93.5 2.1 %shard_map.69 = (bf16[464,128]{1,0:T(8,128)(2,1)S(1)}, f32[464,128]{1,0:T(8,128)S(1)}, bf16[464,256]{1,0:T(8,128)(2,1)}, bf16[464,256]{1,0:T(8,128)(2,1)}) custom-call(f32[464,256]{1,0:T(8,128)S(1)} %get-tuple-element.19.ours_ref, bf16[2,464,256]{2,1,0:T(8,128)(2,1)S(1)} %bitcast.28, bf16[1408,512]{1,0:T(8,128)(2,1)S(1)} %bitcast.18, ...), custom_call_target="tpu_custom_call" | custom-call | flops 973078528 | bytes 6000000 | tf_op jit(solution)/shard_map/pallas_call | solution.py:250
  95.6 14.8 %all-gather.1 = bf16[928,128]{1,0:T(8,128)(2,1)S(1)} all-gather(bf16[464,128]{1,0:T(8,128)(2,1)S(1)} %get-tuple-element.23), channel_id=3, replica_groups=mesh['zh'=2,'x'=8,'c'=2,'zl2'=2,'zl1'=2,'y'=8] {'zh'}, dimensions={0}, use_global_device_ids=true | all-gather | bytes 356352 | tf_op jit(solution)/shard_map/all_gather | solution.py:295
  110.4 0.7 shard_map.70
  (3 shorter events, 0.1 us)
Async XLA Ops:
  0.6 0.8 copy-start.4
  2.2 20.0 %all-to-all-start.1 = ((bf16[16,8,512]{2,1,0:T(8,128)(2,1)}), bf16[16,8,512]{2,1,0:T(8,128)(2,1)S(1)}, u32[]{:S(2)}, u32[]{:S(2)}) async-start(bf16[16,8,512]{2,1,0:T(8,128)(2,1)} %get-tuple-element.17), calls=%async_computation.1 | async-start | bytes 262144 | tf_op jit(solution)/shard_map/all_to_all | solution.py:276
  22.2 66.5 %all-to-all-start = ((bf16[8,464,256]{2,1,0:T(8,128)(2,1)}), bf16[8,464,256]{2,1,0:T(8,128)(2,1)}, u32[]{:S(2)}, u32[]{:S(2)}) async-start(bf16[8,464,256]{2,1,0:T(8,128)(2,1)} %hidden_copies.1), calls=%async_computation | async-start | bytes 3801088 | tf_op jit(solution)/shard_map/all_to_all | solution.py:281
  28.7 7.0 %collective-permute-start = (bf16[7,8,512]{2,1,0:T(8,128)(2,1)S(1)}, bf16[7,8,512]{2,1,0:T(8,128)(2,1)S(1)}, u32[]{:S(2)}, u32[]{:S(2)}) collective-permute-start(bf16[7,8,512]{2,1,0:T(8,128)(2,1)S(1)} %get-tuple-element.16.own_ref), channel_id=1, source_target_pairs={{0,16},{16,0},{1,17},{17,1},{2,18},{18,2},{3,19},{19,3},{4,20},{20... | collective-permute-start | bytes 172040 | tf_op jit(solution)/shard_map/ppermute | solution.py:268
  35.6 8.6 %collective-permute-start.1 = (bf16[30,8,512]{2,1,0:T(8,128)(2,1)S(1)}, bf16[30,8,512]{2,1,0:T(8,128)(2,1)S(1)}, u32[]{:S(2)}, u32[]{:S(2)}) collective-permute-start(bf16[30,8,512]{2,1,0:T(8,128)(2,1)S(1)} %shard_map.67.here_ref), channel_id=1, source_target_pairs={{0,8},{8,0},{1,9},{9,1},{2,10},{10,2},{3,11},{11,3},{4,12},{12,4},... | collective-permute-start | bytes 737288 | tf_op jit(solution)/shard_map/ppermute | solution.py:268
  88.6 4.8 %copy-start = (bf16[4096,464]{0,1:T(8,128)(2,1)S(1)}, bf16[4096,464]{0,1:T(8,128)(2,1)}, u32[]{:S(2)}) copy-start(bf16[4096,464]{0,1:T(8,128)(2,1)} %param.7) | copy-start | bytes 11403268
  88.7 4.8 %copy-start.1 = (bf16[6,64,512]{2,1,0:T(8,128)(2,1)S(1)}, bf16[6,64,512]{2,1,0:T(8,128)(2,1)}, u32[]{:S(2)}) copy-start(bf16[6,64,512]{2,1,0:T(8,128)(2,1)} %multiply_convert_fusion.2) | copy-start | bytes 1179652
  88.7 4.8 %copy-start.2 = (bf16[256,464]{0,1:T(8,128)(2,1)S(1)}, bf16[256,464]{0,1:T(8,128)(2,1)}, u32[]{:S(2)}) copy-start(bf16[256,464]{0,1:T(8,128)(2,1)} %param.5) | copy-start | bytes 712708
  88.7 4.8 %copy-start.3 = (bf16[256,464]{0,1:T(8,128)(2,1)S(1)}, bf16[256,464]{0,1:T(8,128)(2,1)}, u32[]{:S(2)}) copy-start(bf16[256,464]{0,1:T(8,128)(2,1)} %param.6) | copy-start | bytes 712708
